TPU v7x, 128 devices: a whole 4x4x4 slice. The times are simulated.
128 devices in a mesh: tiles: 32 (over x, y, core), reps: 4 (over z).
Axes of the slice: x: 4, y: 4, z: 4, core: 2. Of those that a mesh axis runs over, the one named last changes fastest.
Arguments:
- tiles_w: bfloat16 [4096, 128, 128], P('tiles'), may hold values from 0.0001 to 4
- tile_worker: int32 [4096], P('tiles'), may hold values from 0 to 15
- tile_owner: int32 [4096], P('tiles'), may hold values from 0 to 31
- owner_block: int32 [32, 32], P('tiles'), may hold values from 0 to 1
- worker_base: float32 [65536], P('tiles'), may hold values from -6 to 6
- worker_noise: float32 [65536], P('tiles'), may hold values from 0.2 to 1.5
- worker_cluster: int32 [65536], P('tiles'), may hold values from 0 to 255
- firm_base: float32 [8192], P('tiles'), may hold values from -6 to 6
- firm_noise: float32 [8192], P('tiles'), may hold values from 0.2 to 1.5
- firm_cluster: int32 [8192], P('tiles'), may hold values from 0 to 255
- signs: int32 [256, 256], P('reps'), may hold values from 0 to 1
- covariates: float32 [8192, 512], P('tiles'), may hold values from -0.0625 to 0.0625
- whitening: float32 [512, 512], replicated, may hold values from -0.25 to 0.25
Outputs:
- worker_effect: float32 [256, 65536], P('reps', 'tiles')
- firm_effect: float32 [256, 8192], P('reps', 'tiles')
- coefficients: float32 [256, 512], P('reps')
- covariance: float32 [512, 512], P('tiles')
Inputs may be any that keep to these rules, and one draw needn't show every extreme that they name: `tile_worker`: local worker block of each tile. `tile_owner`: owner of each tile's firm block. `owner_block`: firm block among the owner's 2 blocks. `signs`: a bit that gives the sign 2 b - 1.
All inputs are finite; a program needn't handle non-finite values.
Results may differ from a plain program's by a relative error of at most 0.0023.
Values may be sent and summed in bfloat16 or wider, within the bound.
No kernel may reach another device: no remote copies, remote signals or barrier semaphores. Data moves between devices by JAX's collectives and lax.ppermute only.
A program may use at most 64 MiB of HBM per device.

v0:
```python
import jax
import jax.numpy as jnp
from jax import lax
from jax.sharding import PartitionSpec as P

WORK_BLOCKS = 16
FIRM_BLOCKS = 2
SWEEPS = 6


spectral_bound = 0.8


def chebyshev_weights(sweep_count):
    weights = [1.0]
    weights.append(1.0 / (1.0 - 0.5 * spectral_bound * spectral_bound))
    while len(weights) < sweep_count:
        weights.append(1.0 / (1.0 - 0.25 * spectral_bound * spectral_bound * weights[-1]))
    return weights


def one_hot_rows(indices, row_count):
    return (indices[None, :] == jnp.arange(row_count, dtype=jnp.int32)[:, None]).astype(jnp.float32)


def wild_outcome(base_value, noise_scale, cluster, flip_table):
    clusters_hot = (
        cluster[None, :] == jnp.arange(flip_table.shape[1], dtype=jnp.int32)[:, None]
    ).astype(jnp.bfloat16)
    flip_values = jnp.dot(flip_table, clusters_hot, preferred_element_type=jnp.float32)
    return base_value[None, :] + noise_scale[None, :] * flip_values


def body(
    tiles_w,
    tile_worker,
    tile_owner,
    owner_block,
    worker_base,
    worker_noise,
    worker_cluster,
    firm_base,
    firm_noise,
    firm_cluster,
    signs,
    covariates,
    whitening,
):
    highest = lax.Precision.HIGHEST
    owners_count = lax.axis_size("tiles")
    tile_cells = tiles_w.shape[1]
    replicas_here = signs.shape[0]
    flip_table = (2 * signs - 1).astype(jnp.bfloat16)
    worker_outcome = wild_outcome(worker_base, worker_noise, worker_cluster, flip_table).reshape(
        replicas_here, WORK_BLOCKS, tile_cells
    )
    firm_outcome = wild_outcome(firm_base, firm_noise, firm_cluster, flip_table).reshape(
        replicas_here, FIRM_BLOCKS, tile_cells
    )
    row_mass = jnp.sum(tiles_w, axis=2, dtype=jnp.float32)
    col_mass = jnp.sum(tiles_w, axis=1, dtype=jnp.float32)
    worker_hot = one_hot_rows(tile_worker, WORK_BLOCKS)
    worker_scale = 1.0 + jnp.einsum("bt,tw->bw", worker_hot, row_mass, precision=highest)
    owner_hot = one_hot_rows(tile_owner, owners_count)
    my_blocks = owner_block[0]
    tile_block = tile_owner * FIRM_BLOCKS + jnp.sum(
        jnp.where(owner_hot > 0, my_blocks[:, None], 0), axis=0
    )
    dense_hot = one_hot_rows(tile_block, owners_count * FIRM_BLOCKS)
    firm_mass = lax.psum_scatter(
        jnp.einsum("nt,tf->nf", dense_hot, col_mass, precision=highest),
        "tiles",
        scatter_dimension=0,
        tiled=True,
    )
    firm_scale = 1.0 + firm_mass
    omegas = chebyshev_weights(SWEEPS)
    firm_older = jnp.zeros((replicas_here, FIRM_BLOCKS, tile_cells), jnp.float32)
    firm_newer = firm_older
    firm_now = firm_older
    worker_now = worker_outcome
    tile_firm = None
    for sweep_index in range(SWEEPS):
        if sweep_index == 0:
            worker_now = worker_outcome
        else:
            pulled = jnp.einsum(
                "twf,rtf->rtw", tiles_w, tile_firm, preferred_element_type=jnp.float32
            )
            worker_sum = jnp.einsum("bt,rtw->rbw", worker_hot, pulled, precision=highest)
            worker_now = worker_outcome - worker_sum / worker_scale[None]
        worker_round = worker_now.astype(jnp.bfloat16)
        tile_values = jnp.take(worker_round, tile_worker, axis=1)
        pushed = jnp.einsum(
            "twf,rtw->rtf", tiles_w, tile_values, preferred_element_type=jnp.float32
        )
        firm_sum = lax.psum_scatter(
            jnp.einsum("nt,rtf->rnf", dense_hot, pushed, precision=highest),
            "tiles",
            scatter_dimension=1,
            tiled=True,
        )
        firm_target = firm_outcome - firm_sum / firm_scale[None]
        firm_now = firm_older + omegas[sweep_index] * (firm_target - firm_older)
        firm_older, firm_newer = (firm_newer, firm_now)
        if sweep_index + 1 < SWEEPS:
            firm_round = firm_now.astype(jnp.bfloat16)
            every_firm = lax.all_gather(firm_round, "tiles", axis=1, tiled=True)
            tile_firm = jnp.take(every_firm, tile_block, axis=1)
    worker_effect = worker_now.reshape(replicas_here, WORK_BLOCKS * tile_cells)
    firm_flat = firm_now.reshape(replicas_here, FIRM_BLOCKS * tile_cells)
    mixing = jnp.dot(covariates, whitening.T, precision=highest)
    local_term = jnp.dot(firm_flat, mixing, precision=highest)
    summed = lax.psum(local_term, "tiles")
    share_rows = summed.shape[1] // owners_count
    own_columns = lax.dynamic_slice_in_dim(
        summed, lax.axis_index("tiles") * share_rows, share_rows, 1
    )
    moment = jnp.dot(own_columns.T, summed, precision=highest)
    covariance = lax.psum(moment, "reps") / (replicas_here * lax.axis_size("reps"))
    return (worker_effect, firm_flat, summed, covariance)


def solution(mesh):
    placed = (
        P("tiles", None, None),
        P("tiles"),
        P("tiles"),
        P("tiles", None),
        P("tiles"),
        P("tiles"),
        P("tiles"),
        P("tiles"),
        P("tiles"),
        P("tiles"),
        P("reps", None),
        P("tiles", None),
        P(),
    )
    return jax.shard_map(
        body,
        mesh=mesh,
        in_specs=placed,
        out_specs=(P("reps", "tiles"), P("reps", "tiles"), P("reps", None), P("tiles", None)),
        check_vma=False,
    )
```

profile of v0, /device:TPU:0, one launch (start us, length us, event | category | flops | bytes accessed | tf_op | source)
XLA Modules:
  0.0 1032.7 jit_solution(7390925900868006559)
XLA Ops:
  8.6 1.4 fusion.74
  10.4 2.2 gather_fusion
  12.5 4.1 convolution_bitcast_fusion.10
  16.6 4.2 fusion.56
  20.8 2.6 copy.89
  25.3 3.5 convert_reduce_fusion
  28.9 128.5 %all-reduce = f32[64,128]{1,0:T(8,128)S(1)} all-reduce(f32[64,128]{1,0:T(8,128)S(1)} %fusion.164), channel_id=3, replica_groups=mesh['tiles'=32,'reps'=4] {'tiles'}, use_global_device_ids=true, to_apply=%region_3.0.clone | all-reduce | flops 8192 | bytes 65536
  157.7 1.5 fusion.172
  159.6 39.5 %all-gather.6.cloned.1.call-done = bf16[64,64,128]{2,0,1:T(8,128)(2,1)} async-done(((bf16[64,2,128]{2,0,1:T(8,128)(2,1)}), bf16[64,64,128]{2,0,1:T(8,128)(2,1)}) %all-gather.6.cloned.1.call-update) | async-done | bytes 1048592 | tf_op jit(solution)/shard_map/all_gather | solution.py:108
  199.1 3.4 gather_fusion.1
  202.5 5.8 convolution_bitcast_fusion.9
  208.2 3.8 fusion.129
  212.1 2.2 gather_fusion.2
  214.3 4.1 convolution_bitcast_fusion.8
  218.4 4.2 fusion.59
  222.5 3.0 copy.94
  225.6 78.4 %reduce-scatter.9.cloned.1.call-done = f32[64,2,128]{2,0,1:T(8,128)} async-done(((f32[64,64,128]{2,0,1:T(8,128)}), f32[64,2,128]{2,0,1:T(8,128)}) %reduce-scatter.9.cloned.1.call-update) | async-done | bytes 65552 | tf_op jit(solution)/shard_map/reduce_scatter | solution.py:97
  303.9 1.5 fusion.180
  305.5 43.0 %all-gather.8.cloned.1.call-done = bf16[64,64,128]{2,0,1:T(8,128)(2,1)} async-done(((bf16[64,2,128]{2,0,1:T(8,128)(2,1)}), bf16[64,64,128]{2,0,1:T(8,128)(2,1)}) %all-gather.8.cloned.1.call-update) | async-done | bytes 1048592 | tf_op jit(solution)/shard_map/all_gather | solution.py:108
  348.4 3.4 gather_fusion.3
  351.8 5.8 convolution_bitcast_fusion.7
  357.6 3.8 fusion.126
  361.5 2.2 gather_fusion.4
  363.6 4.1 convolution_bitcast_fusion.6
  367.7 4.2 fusion.62
  371.9 2.7 copy.99
  374.7 78.4 %reduce-scatter.11.cloned.1.call-done = f32[64,2,128]{2,0,1:T(8,128)} async-done(((f32[64,64,128]{2,0,1:T(8,128)}), f32[64,2,128]{2,0,1:T(8,128)}) %reduce-scatter.11.cloned.1.call-update) | async-done | bytes 65552 | tf_op jit(solution)/shard_map/reduce_scatter | solution.py:97
  453.1 1.5 fusion.211
  454.6 43.0 %all-gather.10.cloned.1.call-done = bf16[64,64,128]{2,0,1:T(8,128)(2,1)} async-done(((bf16[64,2,128]{2,0,1:T(8,128)(2,1)}), bf16[64,64,128]{2,0,1:T(8,128)(2,1)}) %all-gather.10.cloned.1.call-update) | async-done | bytes 1048592 | tf_op jit(solution)/shard_map/all_gather | solution.py:108
  497.6 3.4 gather_fusion.5
  501.0 5.8 convolution_bitcast_fusion.5
  506.7 3.8 fusion.123
  510.6 2.2 gather_fusion.6
  512.8 4.1 convolution_bitcast_fusion.4
  516.9 4.2 fusion.65
  521.0 3.0 copy.104
  524.1 78.4 %reduce-scatter.13.cloned.1.call-done = f32[64,2,128]{2,0,1:T(8,128)} async-done(((f32[64,64,128]{2,0,1:T(8,128)}), f32[64,2,128]{2,0,1:T(8,128)}) %reduce-scatter.13.cloned.1.call-update) | async-done | bytes 65552 | tf_op jit(solution)/shard_map/reduce_scatter | solution.py:97
  602.4 1.5 fusion.209
  604.0 43.1 %all-gather.12.cloned.1.call-done = bf16[64,64,128]{2,0,1:T(8,128)(2,1)} async-done(((bf16[64,2,128]{2,0,1:T(8,128)(2,1)}), bf16[64,64,128]{2,0,1:T(8,128)(2,1)}) %all-gather.12.cloned.1.call-update) | async-done | bytes 1048592 | tf_op jit(solution)/shard_map/all_gather | solution.py:108
  647.1 3.4 gather_fusion.7
  650.5 5.8 convolution_bitcast_fusion.3
  656.3 3.8 fusion.120
  660.2 2.2 gather_fusion.8
  662.3 4.1 convolution_bitcast_fusion.2
  666.4 4.2 fusion.68
  670.6 2.7 copy.109
  673.4 78.4 %reduce-scatter.15.cloned.1.call-done = f32[64,2,128]{2,0,1:T(8,128)} async-done(((f32[64,64,128]{2,0,1:T(8,128)}), f32[64,2,128]{2,0,1:T(8,128)}) %reduce-scatter.15.cloned.1.call-update) | async-done | bytes 65552 | tf_op jit(solution)/shard_map/reduce_scatter | solution.py:97
  751.7 1.5 fusion.154
  753.3 43.0 %all-gather.14.cloned.1.call-done = bf16[64,64,128]{2,0,1:T(8,128)(2,1)} async-done(((bf16[64,2,128]{2,0,1:T(8,128)(2,1)}), bf16[64,64,128]{2,0,1:T(8,128)(2,1)}) %all-gather.14.cloned.1.call-update) | async-done | bytes 1048592 | tf_op jit(solution)/shard_map/all_gather | solution.py:108
  796.2 3.4 gather_fusion.9
  799.6 5.8 convolution_bitcast_fusion.1
  805.4 3.8 fusion.213
  809.3 2.2 gather_fusion.10
  811.5 4.1 convolution_bitcast_fusion
  815.6 4.2 fusion.71
  819.7 2.8 copy.114
  822.6 1.0 copy-done.1
  823.5 1.0 fusion.214
  824.6 76.3 %reduce-scatter.17.cloned.1.call-done = f32[64,2,128]{2,0,1:T(8,128)} async-done(((f32[64,64,128]{2,0,1:T(8,128)}), f32[64,2,128]{2,0,1:T(8,128)}) %reduce-scatter.17.cloned.1.call-update) | async-done | bytes 65552 | tf_op jit(solution)/shard_map/reduce_scatter | solution.py:97
  901.8 1.1 fusion.215
  903.9 101.0 %all-reduce.3.cloned.1.call-done = f32[64,512]{1,0:T(8,128)} async-done(((f32[64,512]{1,0:T(8,128)}), f32[64,512]{1,0:T(8,128)}) %all-reduce.3.cloned.1.call-update) | async-done | bytes 131088 | tf_op jit(solution)/shard_map/psum | solution.py:114
  1004.9 1.3 fusion.162
  1006.2 17.3 %psum.15 = f32[16,512]{1,0:T(8,128)S(1)} all-reduce(f32[16,512]{1,0:T(8,128)S(1)} %fusion.162), channel_id=1, replica_groups=mesh['tiles'=32,'reps'=4] {'reps'}, use_global_device_ids=true, to_apply=%region_11.14 | all-reduce | flops 8192 | bytes 65536 | tf_op jit(solution)/shard_map/psum | solution.py:120
  1024.1 1.6 copy.216
  (73 shorter events, 7.1 us)
Async XLA Ops:
  7.2 815.4 %copy-start = (f32[512,512]{1,0:T(8,128)S(1)}, f32[512,512]{1,0:T(8,128)}, u32[]{:S(2)}) copy-start(f32[512,512]{1,0:T(8,128)} %param.29) | copy-start | bytes 3145732
  7.2 3.1 copy-start.11
  7.2 3.1 copy-start.6
  7.2 150.5 %reduce-scatter.7.cloned.1.call-start = ((), (), s32[]{:S(2)}) async-start(), calls=%async_computation.6 | async-start | bytes 2162688 | tf_op jit(solution)/shard_map/reduce_scatter | solution.py:97
  23.3 0.7 copy-start.12
  23.4 175.7 %all-gather.6.cloned.1.call-start = ((), (), s32[]{:S(2)}) async-start(), calls=%async_computation.7 | async-start | bytes 1081344 | tf_op jit(solution)/shard_map/all_gather | solution.py:108
  25.2 132.2 %copy-start.7 = (s32[64,256]{1,0:T(8,128)S(1)}, s32[64,256]{1,0:T(8,128)}, u32[]{:S(2)}) copy-start(s32[64,256]{1,0:T(8,128)} %param.27) | copy-start | bytes 196612
  25.2 132.2 %copy-start.8 = (s32[256]{0:T(256)S(1)}, s32[256]{0:T(256)}, u32[]{:S(2)}) copy-start(s32[256]{0:T(256)} %param.26) | copy-start | bytes 3076
  25.2 132.2 %copy-start.9 = (f32[256]{0:T(256)S(1)}, f32[256]{0:T(256)}, u32[]{:S(2)}) copy-start(f32[256]{0:T(256)} %param.25) | copy-start | bytes 3076
  25.3 132.2 %copy-start.10 = (f32[256]{0:T(256)S(1)}, f32[256]{0:T(256)}, u32[]{:S(2)}) copy-start(f32[256]{0:T(256)} %param.24) | copy-start | bytes 3076
  25.3 134.1 %copy-start.5 = (s32[128]{0:T(128)S(1)}, s32[128]{0:T(128)}, u32[]{:S(2)}) copy-start(s32[128]{0:T(128)} %param.18) | copy-start | bytes 1540
  159.2 144.8 %reduce-scatter.9.cloned.1.call-start = ((), (), s32[]{:S(2)}) async-start(), calls=%async_computation.8 | async-start | bytes 2162688 | tf_op jit(solution)/shard_map/reduce_scatter | solution.py:97
  225.5 122.9 %all-gather.8.cloned.1.call-start = ((), (), s32[]{:S(2)}) async-start(), calls=%async_computation.9 | async-start | bytes 1081344 | tf_op jit(solution)/shard_map/all_gather | solution.py:108
  305.4 147.6 %reduce-scatter.11.cloned.1.call-start = ((), (), s32[]{:S(2)}) async-start(), calls=%async_computation.10 | async-start | bytes 2162688 | tf_op jit(solution)/shard_map/reduce_scatter | solution.py:97
  374.6 78.4 %copy-start.2 = (f32[64,2,128]{2,0,1:T(8,128)S(1)}, f32[64,2,128]{2,0,1:T(8,128)}, u32[]{:S(2)}) copy-start(f32[64,2,128]{2,0,1:T(8,128)} %reduce-scatter.7.cloned.1.call-done) | copy-start | bytes 196612
  374.7 122.9 %all-gather.10.cloned.1.call-start = ((), (), s32[]{:S(2)}) async-start(), calls=%async_computation.11 | async-start | bytes 1081344 | tf_op jit(solution)/shard_map/all_gather | solution.py:108
  454.6 147.9 %reduce-scatter.13.cloned.1.call-start = ((), (), s32[]{:S(2)}) async-start(), calls=%async_computation.12 | async-start | bytes 2162688 | tf_op jit(solution)/shard_map/reduce_scatter | solution.py:97
  524.0 78.4 %copy-start.3 = (f32[64,2,128]{2,0,1:T(8,128)S(1)}, f32[64,2,128]{2,0,1:T(8,128)}, u32[]{:S(2)}) copy-start(f32[64,2,128]{2,0,1:T(8,128)} %reduce-scatter.9.cloned.1.call-done) | copy-start | bytes 196612
  524.0 123.1 %all-gather.12.cloned.1.call-start = ((), (), s32[]{:S(2)}) async-start(), calls=%async_computation.13 | async-start | bytes 1081344 | tf_op jit(solution)/shard_map/all_gather | solution.py:108
  604.0 147.8 %reduce-scatter.15.cloned.1.call-start = ((), (), s32[]{:S(2)}) async-start(), calls=%async_computation.14 | async-start | bytes 2162688 | tf_op jit(solution)/shard_map/reduce_scatter | solution.py:97
  673.3 122.9 %all-gather.14.cloned.1.call-start = ((), (), s32[]{:S(2)}) async-start(), calls=%async_computation.15 | async-start | bytes 1081344 | tf_op jit(solution)/shard_map/all_gather | solution.py:108
  753.2 147.7 %reduce-scatter.17.cloned.1.call-start = ((), (), s32[]{:S(2)}) async-start(), calls=%async_computation.16 | async-start | bytes 2162688 | tf_op jit(solution)/shard_map/reduce_scatter | solution.py:97
  822.5 1.0 copy-start.1
  822.5 182.4 %all-reduce.3.cloned.1.call-start = ((), (), s32[]{:S(2)}) async-start(), calls=%async_computation.17 | async-start | bytes 262144 | tf_op jit(solution)/shard_map/psum | solution.py:114
  901.8 123.9 %copy-start.4 = (f32[64,256]{1,0:T(8,128)}, f32[64,256]{1,0:T(8,128)S(1)}, u32[]{:S(2)}) copy-start(f32[64,256]{1,0:T(8,128)S(1)} %copy_bitcast_fusion.1) | copy-start | bytes 196612
Sparse Core Ops, SparseCore 0:
  23.5 81.2 reduce-scatter.6
  159.3 39.7 all-gather.5
  225.6 78.2 reduce-scatter.8
  306.6 41.7 all-gather.7
  374.8 78.2 reduce-scatter.10
  455.8 41.7 all-gather.9
  524.2 78.2 reduce-scatter.12
  605.3 41.8 all-gather.11
  673.5 78.2 reduce-scatter.14
  754.4 41.7 all-gather.13
  822.6 78.2 reduce-scatter.16
  904.6 100.3 all-reduce.2
where the time goes:
time: 1040 us; the launch traced here: 1030 us
  waiting for transfers between devices  703 us (68%)
  blocking collectives  146 us (14%)
  matrix products  103 us (10%)
  local copies, waits for them, and re-layouts  51.7 us (5%)
  between operations  15.5 us (1%)
  other arithmetic  13.9 us (1%)
    reduce_scatter x6, waiting for transfers between devices, body(): lax.psum_scatter(jnp.einsum('nt,rtf->rnf', dense_hot, pushed, precision=h...  390 us
    all_gather x5, waiting for transfers between devices, body(): every_firm = lax.all_gather(firm_round, 'tiles', axis=1, tiled=True)  212 us
    unnamed x1, blocking collectives  129 us
    psum x1, waiting for transfers between devices, body(): summed = lax.psum(local_term, 'tiles')  101 us
    dot_general x5, matrix products, body(): jnp.einsum('twf,rtf->rtw', tiles_w, tile_firm, preferred_element_type=jnp...  28.8 us
    dot_general x6, matrix products, body(): jnp.einsum('nt,rtf->rnf', dense_hot, pushed, precision=highest)  24.9 us
    dot_general x6, matrix products, body(): jnp.einsum('twf,rtw->rtf', tiles_w, tile_values, preferred_element_type=j...  24.6 us
  transfers between devices with their start and end apart: 12, of which 11 were waited for; matrix products, arithmetic and copies ran while one was open for 1% of the time, Pallas kernels for 0%

commit v1 on v0

v1 whole, which is shorter than its diff:
```python
import jax
import jax.numpy as jnp
from jax import lax
from jax.experimental import pallas as pl
from jax.experimental.pallas import tpu as pltpu
from jax.sharding import PartitionSpec as P

WORK_BLOCKS = 16
FIRM_BLOCKS = 2
SWEEPS = 6
CELLS = 128
EXTRA = 16
SPECTRAL = 0.8
UNROLL = 8

F32 = jnp.float32
BF16 = jnp.bfloat16
HIGHEST = lax.Precision.HIGHEST

VMEM = pl.BlockSpec(memory_space=pltpu.VMEM)
SMEM = pl.BlockSpec(memory_space=pltpu.SMEM)
PARAMS = pltpu.CompilerParams(vmem_limit_bytes=40 << 20)


def chebyshev_weights(count):
    weights = [1.0, 1.0 / (1.0 - 0.5 * SPECTRAL * SPECTRAL)]
    while len(weights) < count:
        weights.append(1.0 / (1.0 - 0.25 * SPECTRAL * SPECTRAL * weights[-1]))
    return weights


def flip_table(signs_ref):
    return (2 * signs_ref[...] - 1).astype(F32).astype(BF16)


def outcome(flips, base, noise, cluster):
    hot = lax.broadcasted_iota(jnp.int32, (flips.shape[1], CELLS), 0) == cluster
    values = jnp.dot(flips, jnp.where(hot, 1.0, 0.0).astype(BF16), preferred_element_type=F32)
    return base + noise * values


def each_tile(count, step):
    def body(index, carry):
        step(index)
        return carry

    lax.fori_loop(0, count, body, 0, unroll=UNROLL)


def push_tiles(tw, to, w_ref, x_ref, acc_ref):
    acc_ref[...] = jnp.zeros_like(acc_ref)

    def step(t):
        acc_ref[to[t]] += jnp.dot(x_ref[tw[t]], w_ref[t], preferred_element_type=F32)

    each_tile(w_ref.shape[0], step)


def pull_tiles(tw, to, w_ref, f_ref, acc_ref):
    acc_ref[...] = jnp.zeros_like(acc_ref)
    rows = acc_ref.shape[1]

    def step(t):
        values = f_ref[to[t]]
        if rows > values.shape[0]:
            values = jnp.concatenate([values, jnp.ones((rows - values.shape[0], CELLS), BF16)], axis=0)
        acc_ref[tw[t]] += lax.dot_general(
            values, w_ref[t], (((1,), (1,)), ((), ())), preferred_element_type=F32
        )

    each_tile(w_ref.shape[0], step)


def first_kernel(tw, to, ob, w_ref, signs_ref, base_ref, noise_ref, cluster_ref, z_ref, wo_ref, x_ref, acc_ref):
    reps = signs_ref.shape[0]
    flips = flip_table(signs_ref)
    for b in range(WORK_BLOCKS):
        row = slice(b, b + 1)
        value = outcome(flips, base_ref[row], noise_ref[row], cluster_ref[row])
        wo_ref[b] = value
        x_ref[b, :reps] = value.astype(BF16)
        x_ref[b, reps:] = jnp.ones((EXTRA, CELLS), BF16)
    push_tiles(tw, to, w_ref, x_ref, acc_ref)
    place = lax.broadcasted_iota(jnp.int32, (EXTRA, CELLS), 0)

    def finish(o):
        z_ref[o, :reps] = acc_ref[o, :reps].astype(BF16)
        mass = acc_ref[o, reps:]
        high = mass.astype(BF16).astype(F32)
        middle = (mass - high).astype(BF16).astype(F32)
        low = (mass - high) - middle
        flag = ob[0, o].astype(F32)
        tail = jnp.where(place == 0, high, jnp.where(place == 1, middle, jnp.where(place == 2, low, flag)))
        z_ref[o, reps:] = tail.astype(BF16)

    each_tile(acc_ref.shape[0], finish)


def sweep_kernel(measure, last, *refs):
    if measure:
        tw, to, w_ref, f_ref, wo_ref, z_ref, inv_ref, accw_ref, x_ref, accz_ref = refs
    elif last:
        tw, to, w_ref, f_ref, wo_ref, inv_ref, z_ref, out_ref, accw_ref, x_ref, accz_ref = refs
    else:
        tw, to, w_ref, f_ref, wo_ref, inv_ref, z_ref, accw_ref, x_ref, accz_ref = refs
    reps = f_ref.shape[1]
    pull_tiles(tw, to, w_ref, f_ref, accw_ref)
    for b in range(WORK_BLOCKS):
        if measure:
            inverse = 1.0 / (1.0 + accw_ref[b, reps : reps + 8])
            inv_ref[b] = inverse
            inverse = inverse[:1]
        else:
            inverse = inv_ref[b, :1]
        worker = wo_ref[b] - accw_ref[b, :reps] * inverse
        if last:
            out_ref[:, b * CELLS : (b + 1) * CELLS] = worker
        x_ref[b] = worker.astype(BF16)
    push_tiles(tw, to, w_ref, x_ref, accz_ref)
    z_ref[...] = accz_ref[...].astype(BF16)


def gather_sums(z_ref, flags_ref, reps):
    zero = jnp.zeros((reps, CELLS), F32)

    def body(s, carry):
        first, second = carry
        part = z_ref[s, :reps].astype(F32)
        upper = jnp.broadcast_to(flags_ref[s, :1], part.shape) > 0.5
        return first + jnp.where(upper, 0.0, part), second + jnp.where(upper, part, 0.0)

    return lax.fori_loop(0, z_ref.shape[0], body, (zero, zero), unroll=4)


def scatter_firms(firms, flags_ref, send_ref):
    first, second = firms

    def step(s):
        upper = jnp.broadcast_to(flags_ref[s, :1], first.shape) > 0.5
        send_ref[s] = jnp.where(upper, second, first).astype(BF16)

    each_tile(send_ref.shape[0], step)


def open_firm_kernel(z_ref, signs_ref, base_ref, noise_ref, cluster_ref, send_ref, fo_ref, inv_ref, flags_ref, now_ref):
    reps = signs_ref.shape[0]
    owners = z_ref.shape[0]
    mass = [jnp.zeros((1, CELLS), F32), jnp.zeros((1, CELLS), F32)]
    for s in range(owners):
        tail = z_ref[s, reps:].astype(F32)
        flags_ref[s] = jnp.broadcast_to(tail[3:4], (8, CELLS))
        part = tail[0:1] + tail[1:2] + tail[2:3]
        upper = tail[3:4] > 0.5
        mass = [mass[0] + jnp.where(upper, 0.0, part), mass[1] + jnp.where(upper, part, 0.0)]
    sums = gather_sums(z_ref, flags_ref, reps)
    flips = flip_table(signs_ref)
    firms = []
    for j in range(FIRM_BLOCKS):
        row = slice(j, j + 1)
        inverse = 1.0 / (1.0 + mass[j])
        value = outcome(flips, base_ref[row], noise_ref[row], cluster_ref[row])
        fo_ref[j] = value
        inv_ref[j] = jnp.broadcast_to(inverse, (8, CELLS))
        firm = value - sums[j] * inverse
        now_ref[j] = firm
        firms.append(firm)
    scatter_firms(firms, flags_ref, send_ref)


def next_firms(omega, z_ref, fo_ref, inv_ref, flags_ref, older_ref):
    sums = gather_sums(z_ref, flags_ref, z_ref.shape[1])
    firms = []
    for j in range(FIRM_BLOCKS):
        target = fo_ref[j] - sums[j] * inv_ref[j, :1]
        if older_ref is None:
            firms.append(omega * target)
        else:
            firms.append(older_ref[j] + omega * (target - older_ref[j]))
    return firms


def firm_kernel(omega, has_older, *refs):
    if has_older:
        z_ref, fo_ref, inv_ref, flags_ref, older_ref, send_ref, now_ref = refs
    else:
        (z_ref, fo_ref, inv_ref, flags_ref, send_ref, now_ref), older_ref = refs, None
    firms = next_firms(omega, z_ref, fo_ref, inv_ref, flags_ref, older_ref)
    for j in range(FIRM_BLOCKS):
        now_ref[j] = firms[j]
    scatter_firms(firms, flags_ref, send_ref)


def close_firm_kernel(omega, z_ref, fo_ref, inv_ref, flags_ref, older_ref, cov_ref, white_ref, firm_ref, part_ref):
    firms = next_firms(omega, z_ref, fo_ref, inv_ref, flags_ref, older_ref)
    for j in range(FIRM_BLOCKS):
        firm_ref[:, j * CELLS : (j + 1) * CELLS] = firms[j]
    projected = jnp.dot(firm_ref[...], cov_ref[...], precision=HIGHEST, preferred_element_type=F32)
    whitened = lax.dot_general(
        projected, white_ref[...], (((1,), (1,)), ((), ())), precision=HIGHEST, preferred_element_type=F32
    )
    reps = whitened.shape[0]
    columns = whitened.shape[1] // CELLS
    for c in range(columns):
        part_ref[pl.ds(c, reps, stride=columns)] = whitened[:, c * CELLS : (c + 1) * CELLS]


def total_kernel(part_ref, out_ref):
    total = jnp.sum(part_ref[...], axis=0)
    for s in range(out_ref.shape[0]):
        out_ref[s] = total


def closing_kernel(owners, index, all_ref, coef_ref, moment_ref, rows_ref, order_ref):
    share, me = index[0], index[1]
    reps, covars = coef_ref.shape
    columns = covars // CELLS
    rows = all_ref.shape[0] // columns
    spread = rows // reps
    per = reps // owners
    for c in range(columns):
        for i in range(per):
            start = me * (per * columns) + i * columns + c
            piece = all_ref[pl.ds(start, owners, stride=spread * per * columns)]
            order_ref[pl.ds(i, owners, stride=per)] = piece
        coef_ref[:, c * CELLS : (c + 1) * CELLS] = order_ref[...]
    share_rows = moment_ref.shape[0]
    in_block = CELLS // share_rows
    own = all_ref[pl.ds(share // in_block, rows, stride=columns)]
    for c in range(columns):
        other = all_ref[pl.ds(c, rows, stride=columns)]
        rows_ref[:, c * CELLS : (c + 1) * CELLS] = lax.dot_general(
            own, other, (((0,), (0,)), ((), ())), precision=HIGHEST, preferred_element_type=F32
        )
    start = pl.multiple_of((share % in_block) * share_rows, share_rows)
    moment_ref[...] = rows_ref[pl.ds(start, share_rows)] / rows


def call(kernel, inputs, outputs, scratch=(), scalars=0, name=None):
    return pl.pallas_call(
        kernel,
        in_specs=[SMEM] * scalars + [VMEM] * (len(inputs) - scalars),
        out_specs=[VMEM] * len(outputs),
        out_shape=[jax.ShapeDtypeStruct(shape, dtype) for shape, dtype in outputs],
        scratch_shapes=[pltpu.VMEM(shape, dtype) for shape, dtype in scratch],
        compiler_params=PARAMS,
        name=name,
    )(*inputs)


def body(
    tiles_w,
    tile_worker,
    tile_owner,
    owner_block,
    worker_base,
    worker_noise,
    worker_cluster,
    firm_base,
    firm_noise,
    firm_cluster,
    signs,
    covariates,
    whitening,
):
    owners = lax.axis_size("tiles")
    groups = lax.axis_size("reps")
    reps = signs.shape[0]
    covars = whitening.shape[0]
    omegas = chebyshev_weights(SWEEPS)

    def exchange(values, axes="tiles"):
        return lax.all_to_all(values, axes, 0, 0, tiled=True)

    def rows(values):
        return values.reshape(-1, CELLS)

    push_shape = ((owners, reps, CELLS), BF16)
    work_shape = ((WORK_BLOCKS, reps, CELLS), F32)
    firm_shape = ((FIRM_BLOCKS, reps, CELLS), F32)
    z, worker_outcome = call(
        first_kernel,
        (tile_worker, tile_owner, owner_block, tiles_w, signs, rows(worker_base), rows(worker_noise), rows(worker_cluster)),
        (((owners, reps + EXTRA, CELLS), BF16), work_shape),
        (((WORK_BLOCKS, reps + EXTRA, CELLS), BF16), ((owners, reps + EXTRA, CELLS), F32)),
        scalars=3,
        name="first_push",
    )
    z = exchange(z)
    send, firm_outcome, firm_inverse, flags, newer = call(
        open_firm_kernel,
        (z, signs, rows(firm_base), rows(firm_noise), rows(firm_cluster)),
        (push_shape, firm_shape, ((FIRM_BLOCKS, 8, CELLS), F32), ((owners, 8, CELLS), F32), firm_shape),
        name="first_firm",
    )
    older = None
    worker_inverse = None
    scratch = (((WORK_BLOCKS, reps, CELLS), BF16), ((owners, reps, CELLS), F32))
    for k in range(1, SWEEPS):
        measure, last = k == 1, k == SWEEPS - 1
        f = exchange(send)
        inputs = (tile_worker, tile_owner, tiles_w, f, worker_outcome)
        outputs = (push_shape,)
        if measure:
            outputs += (((WORK_BLOCKS, 8, CELLS), F32),)
        else:
            inputs += (worker_inverse,)
        if last:
            outputs += (((reps, WORK_BLOCKS * CELLS), F32),)
        work_rows = reps + EXTRA if measure else reps
        results = call(
            lambda *refs, m=measure, e=last: sweep_kernel(m, e, *refs),
            inputs,
            outputs,
            (((WORK_BLOCKS, work_rows, CELLS), F32),) + scratch,
            scalars=2,
            name="sweep_open" if measure else "sweep_close" if last else "sweep",
        )
        z = results[0]
        if measure:
            worker_inverse = results[1]
        if last:
            worker_effect = results[1]
        z = exchange(z)
        inputs = (z, firm_outcome, firm_inverse, flags) + (() if older is None else (older,))
        if not last:
            send, now = call(
                lambda *refs, w=omegas[k], h=older is not None: firm_kernel(w, h, *refs),
                inputs,
                (push_shape, firm_shape),
                name="firm",
            )
            older, newer = newer, now
        else:
            firm_effect, part = call(
                lambda *refs, w=omegas[k]: close_firm_kernel(w, *refs),
                inputs + (covariates, whitening),
                (((reps, FIRM_BLOCKS * CELLS), F32), ((reps * covars // CELLS, CELLS), F32)),
                name="close_firm",
            )
    part = exchange(part.reshape(owners, -1, CELLS))
    (spread,) = call(total_kernel, (part,), (((owners * groups,) + part.shape[1:], F32),), name="total")
    everything = exchange(spread, ("tiles", "reps"))
    index = jnp.stack([lax.axis_index("tiles"), lax.axis_index("reps")]).astype(jnp.int32)
    coefficients, covariance = call(
        lambda *refs: closing_kernel(owners, *refs),
        (index, everything.reshape(-1, CELLS)),
        (((reps, covars), F32), ((covars // owners, covars), F32)),
        (((CELLS, covars), F32), ((reps, CELLS), F32)),
        scalars=1,
        name="closing",
    )
    return (worker_effect, firm_effect, coefficients, covariance)


def solution(mesh):
    placed = (
        P("tiles", None, None),
        P("tiles"),
        P("tiles"),
        P("tiles", None),
        P("tiles"),
        P("tiles"),
        P("tiles"),
        P("tiles"),
        P("tiles"),
        P("tiles"),
        P("reps", None),
        P("tiles", None),
        P(),
    )
    return jax.shard_map(
        body,
        mesh=mesh,
        in_specs=placed,
        out_specs=(P("reps", "tiles"), P("reps", "tiles"), P("reps", None), P("tiles", None)),
        check_vma=False,
    )
```

time: 1040 us -> 268 us (0.26)
  waiting for transfers between devices: 703 us -> 13.1 us
  matrix products: 103 us -> 0 us
  Pallas kernels: 0 us -> 56.3 us
  local copies, waits for them, and re-layouts: 51.7 us -> 7.11 us
  blocking collectives: 146 us -> 182 us
  between operations: 15.5 us -> 0.78 us
  other arithmetic: 13.9 us -> 0.08 us
    reduce_scatter x6 -> x0, waiting for transfers between devices: 390 us -> none  [body(): lax.psum_scatter(jnp.einsum('nt,rtf->rnf', dense_hot, pushed, precision=h...]
    all_gather x5 -> x0, waiting for transfers between devices: 212 us -> none  [body(): every_firm = lax.all_gather(firm_round, 'tiles', axis=1, tiled=True)]
    all_to_all x0 -> x12, blocking collectives: none -> 182 us  [exchange(): return lax.all_to_all(values, axes, 0, 0, tiled=True)]
    unnamed x1 -> x0, blocking collectives: 129 us -> none
    dot_general x29 -> x0, matrix products: 103 us -> none  [the longest x5 28.8 us: body(): jnp.einsum('twf,rtf->rtw', tiles_w, tile_firm, preferred_element_type=jnp...]
    psum x1 -> x0, waiting for transfers between devices: 101 us -> none  [body(): summed = lax.psum(local_term, 'tiles')]
    pallas_call x0 -> x14, Pallas kernels: none -> 56.3 us  [call(): pl.pallas_call(kernel, in_specs=[SMEM] * scalars + [VMEM] * (len(inputs)...]
    gather x11 -> x0, local copies, waits for them, and re-layouts: 29.8 us -> none  [the longest x5 16.9 us: body(): tile_firm = jnp.take(every_firm, tile_block, axis=1)]
  transfers between devices with their start and end apart: 12 -> 1, of which waited for: 11 -> 1; matrix products, arithmetic and copies ran while one was open for 1% -> 0% of each run, Pallas kernels for 0% -> 0%
where the time goes in v1:
time: 268 us; the launch traced here: 266 us
  blocking collectives  182 us (68%)
  Pallas kernels  56.3 us (21%)
  waiting for transfers between devices  13.1 us (5%)
  starting transfers between devices  7.35 us (3%)
  local copies, waits for them, and re-layouts  7.11 us (3%)
    all_to_all x12, blocking collectives, exchange(): return lax.all_to_all(values, axes, 0, 0, tiled=True)  182 us
    pallas_call x14, Pallas kernels, call(): pl.pallas_call(kernel, in_specs=[SMEM] * scalars + [VMEM] * (len(inputs)...  56.3 us
    all_to_all x1, waiting for transfers between devices, exchange(): return lax.all_to_all(values, axes, 0, 0, tiled=True)  13.1 us
    all_to_all x1, starting transfers between devices, exchange(): return lax.all_to_all(values, axes, 0, 0, tiled=True)  7.35 us
    unnamed x28, local copies, waits for them, and re-layouts  7.11 us
  transfers between devices with their start and end apart: 1, of which 1 were waited for; matrix products, arithmetic and copies ran while one was open for 0% of the time, Pallas kernels for 0%

profile of v1, /device:TPU:0, one launch (start us, length us, event | category | flops | bytes accessed | tf_op | source)
XLA Modules:
  0.0 266.3 jit_solution(17133736894774781429)
XLA Ops:
  0.6 0.0 copy-start.10
  0.6 0.0 copy-start.11
  0.7 0.0 copy-start.12
  0.7 0.0 copy-start
  0.7 2.2 copy-done
  2.9 0.0 copy-start.4
  2.9 0.8 copy-done.4
  3.7 0.0 copy-start.5
  3.7 0.7 copy-done.5
  4.4 0.0 copy-start.6
  4.4 0.7 copy-done.6
  5.0 0.0 copy-start.7
  5.0 0.7 copy-done.7
  5.7 0.0 copy-start.8
  5.7 0.7 copy-done.8
  6.4 0.0 copy-start.9
  6.4 0.7 copy-done.9
  7.1 0.0 copy-start.13
  7.1 0.7 copy-done.13
  7.8 0.0 copy-start.1
  7.8 5.0 %first_push.1 = (bf16[32,80,128]{2,1,0:T(8,128)(2,1)S(1)}, f32[16,64,128]{2,1,0:T(8,128)S(1)}) custom-call(s32[128]{0:T(128)S(1)} %copy-done.5, s32[128]{0:T(128)S(1)} %copy-done.6, s32[1,32]{1,0:T(1,128)S(1)} %copy-done.13, bf16[128,128,128]{2,1,0:T(8,128)(2,1)S(1)} %copy-done, s32[64,256]{1,0:T(8,128)S(1)} %copy-done.4, f32[16,128]{1,0:T(8,128)S(1)} %bitcast.12, ...), custom_call_target="tpu_custom_call" | custom-call | tf_op jit(solution)/shard_map/first_push/pallas_call | solution.py:239
  12.8 19.8 %all_to_all.65.z_ref = bf16[32,80,128]{2,1,0:T(8,128)(2,1)S(1)} all-to-all(bf16[32,80,128]{2,1,0:T(8,128)(2,1)S(1)} %get-tuple-element.26), channel_id=1, replica_groups=mesh['tiles'=32,'reps'=4] {'tiles'}, dimensions={0} | all-to-all | bytes 1310720 | tf_op jit(solution)/shard_map/all_to_all | solution.py:272
  32.5 0.0 copy-done.10
  32.5 0.0 copy-done.11
  32.6 0.0 copy-done.12
  32.6 0.5 first_firm.1
  33.1 15.0 %all_to_all.66.refs_3_ = bf16[32,64,128]{2,1,0:T(8,128)(2,1)S(1)} all-to-all(bf16[32,64,128]{2,1,0:T(8,128)(2,1)S(1)} %get-tuple-element.27), channel_id=1, replica_groups=mesh['tiles'=32,'reps'=4] {'tiles'}, dimensions={0} | all-to-all | bytes 1048576 | tf_op jit(solution)/shard_map/all_to_all | solution.py:272
  48.0 0.0 copy-done.1
  48.0 9.1 %sweep_open.1 = (bf16[32,64,128]{2,1,0:T(8,128)(2,1)S(1)}, f32[16,8,128]{2,1,0:T(8,128)S(1)}) custom-call(s32[128]{0:T(128)S(1)} %copy-done.5, s32[128]{0:T(128)S(1)} %copy-done.6, bf16[128,128,128]{2,1,0:T(8,128)(2,1)S(1)} %copy-done.1, bf16[32,64,128]{2,1,0:T(8,128)(2,1)S(1)} %all_to_all.66.refs_3_, f32[16,64,128]{2,1,0:T(8,128)S(1)} %get-tuple-element.28.refs_4_), custom_call_target="tpu_custom_call" | custom-call | tf_op jit(solution)/shard_map/sweep_open/pallas_call | solution.py:239
  57.2 15.0 %all_to_all.67.refs_0_ = bf16[32,64,128]{2,1,0:T(8,128)(2,1)S(1)} all-to-all(bf16[32,64,128]{2,1,0:T(8,128)(2,1)S(1)} %get-tuple-element.29), channel_id=1, replica_groups=mesh['tiles'=32,'reps'=4] {'tiles'}, dimensions={0} | all-to-all | bytes 1048576 | tf_op jit(solution)/shard_map/all_to_all | solution.py:272
  72.2 0.3 firm.4
  72.5 15.0 %all_to_all.68.refs_3_ = bf16[32,64,128]{2,1,0:T(8,128)(2,1)S(1)} all-to-all(bf16[32,64,128]{2,1,0:T(8,128)(2,1)S(1)} %get-tuple-element.33), channel_id=1, replica_groups=mesh['tiles'=32,'reps'=4] {'tiles'}, dimensions={0} | all-to-all | bytes 1048576 | tf_op jit(solution)/shard_map/all_to_all | solution.py:272
  87.5 8.7 %sweep.3 = bf16[32,64,128]{2,1,0:T(8,128)(2,1)S(1)} custom-call(s32[128]{0:T(128)S(1)} %copy-done.5, s32[128]{0:T(128)S(1)} %copy-done.6, bf16[128,128,128]{2,1,0:T(8,128)(2,1)S(1)} %copy-done.1, bf16[32,64,128]{2,1,0:T(8,128)(2,1)S(1)} %all_to_all.68.refs_3_, f32[16,64,128]{2,1,0:T(8,128)S(1)} %get-tuple-element.28.refs_4_, ...), custom_call_target="tpu_custom_call" | custom-call | tf_op jit(solution)/shard_map/sweep/pallas_call | solution.py:239
  96.2 15.0 %all_to_all.69.refs_0_ = bf16[32,64,128]{2,1,0:T(8,128)(2,1)S(1)} all-to-all(bf16[32,64,128]{2,1,0:T(8,128)(2,1)S(1)} %sweep.3), channel_id=1, replica_groups=mesh['tiles'=32,'reps'=4] {'tiles'}, dimensions={0} | all-to-all | bytes 1048576 | tf_op jit(solution)/shard_map/all_to_all | solution.py:272
  111.2 0.3 firm.5
  111.5 15.0 %all_to_all.70.refs_3_ = bf16[32,64,128]{2,1,0:T(8,128)(2,1)S(1)} all-to-all(bf16[32,64,128]{2,1,0:T(8,128)(2,1)S(1)} %get-tuple-element.36), channel_id=1, replica_groups=mesh['tiles'=32,'reps'=4] {'tiles'}, dimensions={0} | all-to-all | bytes 1048576 | tf_op jit(solution)/shard_map/all_to_all | solution.py:272
  126.5 8.7 %sweep.4 = bf16[32,64,128]{2,1,0:T(8,128)(2,1)S(1)} custom-call(s32[128]{0:T(128)S(1)} %copy-done.5, s32[128]{0:T(128)S(1)} %copy-done.6, bf16[128,128,128]{2,1,0:T(8,128)(2,1)S(1)} %copy-done.1, bf16[32,64,128]{2,1,0:T(8,128)(2,1)S(1)} %all_to_all.70.refs_3_, f32[16,64,128]{2,1,0:T(8,128)S(1)} %get-tuple-element.28.refs_4_, ...), custom_call_target="tpu_custom_call" | custom-call | tf_op jit(solution)/shard_map/sweep/pallas_call | solution.py:239
  135.3 15.0 %all_to_all.71.refs_0_ = bf16[32,64,128]{2,1,0:T(8,128)(2,1)S(1)} all-to-all(bf16[32,64,128]{2,1,0:T(8,128)(2,1)S(1)} %sweep.4), channel_id=1, replica_groups=mesh['tiles'=32,'reps'=4] {'tiles'}, dimensions={0} | all-to-all | bytes 1048576 | tf_op jit(solution)/shard_map/all_to_all | solution.py:272
  150.3 0.3 firm.6
  150.6 15.0 %all_to_all.72.refs_3_ = bf16[32,64,128]{2,1,0:T(8,128)(2,1)S(1)} all-to-all(bf16[32,64,128]{2,1,0:T(8,128)(2,1)S(1)} %get-tuple-element.38), channel_id=1, replica_groups=mesh['tiles'=32,'reps'=4] {'tiles'}, dimensions={0} | all-to-all | bytes 1048576 | tf_op jit(solution)/shard_map/all_to_all | solution.py:272
  165.6 8.7 %sweep.5 = bf16[32,64,128]{2,1,0:T(8,128)(2,1)S(1)} custom-call(s32[128]{0:T(128)S(1)} %copy-done.5, s32[128]{0:T(128)S(1)} %copy-done.6, bf16[128,128,128]{2,1,0:T(8,128)(2,1)S(1)} %copy-done.1, bf16[32,64,128]{2,1,0:T(8,128)(2,1)S(1)} %all_to_all.72.refs_3_, f32[16,64,128]{2,1,0:T(8,128)S(1)} %get-tuple-element.28.refs_4_, ...), custom_call_target="tpu_custom_call" | custom-call | tf_op jit(solution)/shard_map/sweep/pallas_call | solution.py:239
  174.3 15.0 %all_to_all.73.refs_0_ = bf16[32,64,128]{2,1,0:T(8,128)(2,1)S(1)} all-to-all(bf16[32,64,128]{2,1,0:T(8,128)(2,1)S(1)} %sweep.5), channel_id=1, replica_groups=mesh['tiles'=32,'reps'=4] {'tiles'}, dimensions={0} | all-to-all | bytes 1048576 | tf_op jit(solution)/shard_map/all_to_all | solution.py:272
  189.3 0.0 copy-start.2
  189.3 0.0 copy-start.3
  189.3 0.9 firm.7
  190.2 15.0 %all_to_all.74.refs_3_ = bf16[32,64,128]{2,1,0:T(8,128)(2,1)S(1)} all-to-all(bf16[32,64,128]{2,1,0:T(8,128)(2,1)S(1)} %get-tuple-element.40), channel_id=1, replica_groups=mesh['tiles'=32,'reps'=4] {'tiles'}, dimensions={0} | all-to-all | bytes 1048576 | tf_op jit(solution)/shard_map/all_to_all | solution.py:272
  205.2 9.3 %sweep_close.1 = (bf16[32,64,128]{2,1,0:T(8,128)(2,1)S(1)}, f32[64,2048]{1,0:T(8,128)}) custom-call(s32[128]{0:T(128)S(1)} %copy-done.5, s32[128]{0:T(128)S(1)} %copy-done.6, bf16[128,128,128]{2,1,0:T(8,128)(2,1)S(1)} %copy-done.1, bf16[32,64,128]{2,1,0:T(8,128)(2,1)S(1)} %all_to_all.74.refs_3_, f32[16,64,128]{2,1,0:T(8,128)S(1)} %get-tuple-element.28.refs_4_, ...), custom_call_target="tpu_custom_call" | custom-call | tf_op jit(solution)/shard_map/sweep_close/pallas_call | solution.py:239
  214.5 15.0 %all_to_all.75.refs_0_ = bf16[32,64,128]{2,1,0:T(8,128)(2,1)S(1)} all-to-all(bf16[32,64,128]{2,1,0:T(8,128)(2,1)S(1)} %get-tuple-element.42), channel_id=1, replica_groups=mesh['tiles'=32,'reps'=4] {'tiles'}, dimensions={0} | all-to-all | bytes 1048576 | tf_op jit(solution)/shard_map/all_to_all | solution.py:272
  229.5 0.0 copy-done.2
  229.5 0.0 copy-done.3
  229.5 1.7 close_firm.1
  231.2 11.8 %all_to_all.76.part_ref = f32[32,8,128]{2,1,0:T(8,128)S(1)} all-to-all(f32[32,8,128]{2,1,0:T(8,128)S(1)} %bitcast.11), channel_id=1, replica_groups=mesh['tiles'=32,'reps'=4] {'tiles'}, dimensions={0} | all-to-all | bytes 262144 | tf_op jit(solution)/shard_map/all_to_all | solution.py:272
  243.0 0.9 total.1
  243.8 7.3 %all-to-all-start.12 = ((f32[128,8,128]{2,1,0:T(8,128)}), f32[128,8,128]{2,1,0:T(8,128)S(1)}, u32[]{:S(2)}, u32[]{:S(2)}) async-start(f32[128,8,128]{2,1,0:T(8,128)} %total.1), calls=%async_computation.12 | async-start | bytes 1048576 | tf_op jit(solution)/shard_map/all_to_all | solution.py:272
  251.2 0.1 pad_add_fusion.refs_0_
  251.3 13.1 %all-to-all-done.12 = f32[128,8,128]{2,1,0:T(8,128)S(1)} async-done(((f32[128,8,128]{2,1,0:T(8,128)}), f32[128,8,128]{2,1,0:T(8,128)S(1)}, u32[]{:S(2)}, u32[]{:S(2)}) %all-to-all-start.12) | async-done | bytes 524320 | tf_op jit(solution)/shard_map/all_to_all | solution.py:272
  264.4 1.9 closing.1
Async XLA Ops:
  0.6 31.9 %copy-start.10 = (f32[256]{0:T(256)S(1)}, f32[256]{0:T(256)}, u32[]{:S(2)}) copy-start(f32[256]{0:T(256)} %param.20) | copy-start | bytes 3076
  0.6 31.9 %copy-start.11 = (f32[256]{0:T(256)S(1)}, f32[256]{0:T(256)}, u32[]{:S(2)}) copy-start(f32[256]{0:T(256)} %param.21) | copy-start | bytes 3076
  0.7 31.9 %copy-start.12 = (s32[256]{0:T(256)S(1)}, s32[256]{0:T(256)}, u32[]{:S(2)}) copy-start(s32[256]{0:T(256)} %param.22) | copy-start | bytes 3076
  0.7 2.2 copy-start
  2.9 0.8 copy-start.4
  3.7 0.7 copy-start.5
  4.4 0.7 copy-start.6
  5.0 0.7 copy-start.7
  5.7 0.7 copy-start.8
  6.4 0.7 copy-start.9
  7.1 0.7 copy-start.13
  7.8 40.3 %copy-start.1 = (bf16[128,128,128]{2,1,0:T(8,128)(2,1)S(1)}, bf16[128,128,128]{2,1,0:T(8,128)(2,1)}, u32[]{:S(2)}) copy-start(bf16[128,128,128]{2,1,0:T(8,128)(2,1)} %refs_2_.9) | copy-start | bytes 12582916
  189.3 40.2 %copy-start.2 = (f32[512,512]{1,0:T(8,128)S(1)}, f32[512,512]{1,0:T(8,128)}, u32[]{:S(2)}) copy-start(f32[512,512]{1,0:T(8,128)} %refs_6_.1) | copy-start | bytes 3145732
  189.3 40.2 %copy-start.3 = (f32[256,512]{1,0:T(8,128)S(1)}, f32[256,512]{1,0:T(8,128)}, u32[]{:S(2)}) copy-start(f32[256,512]{1,0:T(8,128)} %refs_5_.1) | copy-start | bytes 1572868
  243.8 20.6 %all-to-all-start.12 = ((f32[128,8,128]{2,1,0:T(8,128)}), f32[128,8,128]{2,1,0:T(8,128)S(1)}, u32[]{:S(2)}, u32[]{:S(2)}) async-start(f32[128,8,128]{2,1,0:T(8,128)} %total.1), calls=%async_computation.12 | async-start | bytes 1048576 | tf_op jit(solution)/shard_map/all_to_all | solution.py:272

commit v2 on v1

--- a/solution.py
+++ b/solution.py
@@ -11,7 +11,8 @@
 CELLS = 128
 EXTRA = 16
 SPECTRAL = 0.8
-UNROLL = 8
+UNROLL = 64
+CHUNKS = 4
 
 F32 = jnp.float32
 BF16 = jnp.bfloat16
@@ -19,7 +20,8 @@
 
 VMEM = pl.BlockSpec(memory_space=pltpu.VMEM)
 SMEM = pl.BlockSpec(memory_space=pltpu.SMEM)
-PARAMS = pltpu.CompilerParams(vmem_limit_bytes=40 << 20)
+HBM = pl.BlockSpec(memory_space=pltpu.HBM)
+PARAMS = pltpu.CompilerParams(vmem_limit_bytes=20 << 20)
 
 
 def chebyshev_weights(count):
@@ -39,39 +41,48 @@
     return base + noise * values
 
 
-def each_tile(count, step):
+def each_tile(count, step, unroll=UNROLL):
     def body(index, carry):
         step(index)
         return carry
 
-    lax.fori_loop(0, count, body, 0, unroll=UNROLL)
-
-
-def push_tiles(tw, to, w_ref, x_ref, acc_ref):
+    lax.fori_loop(0, count, body, 0, unroll=min(unroll, count))
+
+
+def add_tiles(first, count, source, target, w_ref, x_ref, acc_ref):
+    def step(i):
+        t = first + i
+        acc_ref[target[t]] += jnp.dot(x_ref[source[t]], w_ref[t], preferred_element_type=F32)
+
+    each_tile(count, step)
+
+
+def first_kernel(
+    tw_hbm, to_hbm, ob_hbm, w_hbm, signs_hbm, base_hbm, noise_hbm, cluster_hbm,
+    z_ref, wo_ref, turned_ref, inv_ref,
+    tw, to, ob, signs_ref, base_ref, noise_ref, cluster_ref, w_ref, x_ref, acc_ref, mass_ref, sems,
+):
+    small = [
+        (signs_hbm, signs_ref),
+        (cluster_hbm, cluster_ref),
+        (base_hbm, base_ref),
+        (noise_hbm, noise_ref),
+        (tw_hbm, tw),
+        (to_hbm, to),
+        (ob_hbm, ob),
+    ]
+    copies = [pltpu.make_async_copy(source, target, sems.at[i]) for i, (source, target) in enumerate(small)]
+    chunk = w_ref.shape[0] // CHUNKS
+    loads = []
+    for c in range(CHUNKS):
+        part = pl.ds(c * chunk, chunk)
+        loads.append(pltpu.make_async_copy(w_hbm.at[part], w_ref.at[part], sems.at[len(small) + c]))
+    for copy in copies + loads:
+        copy.start()
     acc_ref[...] = jnp.zeros_like(acc_ref)
-
-    def step(t):
-        acc_ref[to[t]] += jnp.dot(x_ref[tw[t]], w_ref[t], preferred_element_type=F32)
-
-    each_tile(w_ref.shape[0], step)
-
-
-def pull_tiles(tw, to, w_ref, f_ref, acc_ref):
-    acc_ref[...] = jnp.zeros_like(acc_ref)
-    rows = acc_ref.shape[1]
-
-    def step(t):
-        values = f_ref[to[t]]
-        if rows > values.shape[0]:
-            values = jnp.concatenate([values, jnp.ones((rows - values.shape[0], CELLS), BF16)], axis=0)
-        acc_ref[tw[t]] += lax.dot_general(
-            values, w_ref[t], (((1,), (1,)), ((), ())), preferred_element_type=F32
-        )
-
-    each_tile(w_ref.shape[0], step)
-
-
-def first_kernel(tw, to, ob, w_ref, signs_ref, base_ref, noise_ref, cluster_ref, z_ref, wo_ref, x_ref, acc_ref):
+    mass_ref[...] = jnp.zeros_like(mass_ref)
+    for copy in copies:
+        copy.wait()
     reps = signs_ref.shape[0]
     flips = flip_table(signs_ref)
     for b in range(WORK_BLOCKS):
@@ -80,7 +91,20 @@
         wo_ref[b] = value
         x_ref[b, :reps] = value.astype(BF16)
         x_ref[b, reps:] = jnp.ones((EXTRA, CELLS), BF16)
-    push_tiles(tw, to, w_ref, x_ref, acc_ref)
+
+    def step(t):
+        tile = w_ref[t]
+        acc_ref[to[t]] += jnp.dot(x_ref[tw[t]], tile, preferred_element_type=F32)
+        turned = tile.T
+        turned_ref[t] = turned
+        mass_ref[tw[t]] += jnp.sum(turned.astype(F32).reshape(CELLS // 8, 8, CELLS), axis=0)
+
+    for c in range(CHUNKS):
+        loads[c].wait()
+        each_tile(chunk, lambda i, c=c: step(c * chunk + i))
+    for b in range(WORK_BLOCKS):
+        inverse = 1.0 / (1.0 + jnp.sum(mass_ref[b], axis=0, keepdims=True))
+        inv_ref[b] = jnp.broadcast_to(inverse, (8, CELLS))
     place = lax.broadcasted_iota(jnp.int32, (EXTRA, CELLS), 0)
 
     def finish(o):
@@ -93,31 +117,30 @@
         tail = jnp.where(place == 0, high, jnp.where(place == 1, middle, jnp.where(place == 2, low, flag)))
         z_ref[o, reps:] = tail.astype(BF16)
 
-    each_tile(acc_ref.shape[0], finish)
-
-
-def sweep_kernel(measure, last, *refs):
-    if measure:
-        tw, to, w_ref, f_ref, wo_ref, z_ref, inv_ref, accw_ref, x_ref, accz_ref = refs
-    elif last:
-        tw, to, w_ref, f_ref, wo_ref, inv_ref, z_ref, out_ref, accw_ref, x_ref, accz_ref = refs
+    each_tile(acc_ref.shape[0], finish, 8)
+
+
+def sweep_kernel(last, *refs):
+    if last:
+        tw, to, w_ref, turned_ref, f_ref, wo_ref, inv_ref, z_ref, out_hbm, accw_ref, x_ref, accz_ref, out_ref, sem = refs
     else:
-        tw, to, w_ref, f_ref, wo_ref, inv_ref, z_ref, accw_ref, x_ref, accz_ref = refs
-    reps = f_ref.shape[1]
-    pull_tiles(tw, to, w_ref, f_ref, accw_ref)
+        tw, to, w_ref, turned_ref, f_ref, wo_ref, inv_ref, z_ref, accw_ref, x_ref, accz_ref = refs
+    tiles = w_ref.shape[0]
+    accw_ref[...] = jnp.zeros_like(accw_ref)
+    accz_ref[...] = jnp.zeros_like(accz_ref)
+    add_tiles(0, tiles, to, tw, turned_ref, f_ref, accw_ref)
     for b in range(WORK_BLOCKS):
-        if measure:
-            inverse = 1.0 / (1.0 + accw_ref[b, reps : reps + 8])
-            inv_ref[b] = inverse
-            inverse = inverse[:1]
-        else:
-            inverse = inv_ref[b, :1]
-        worker = wo_ref[b] - accw_ref[b, :reps] * inverse
+        worker = wo_ref[b] - accw_ref[b] * inv_ref[b, :1]
         if last:
             out_ref[:, b * CELLS : (b + 1) * CELLS] = worker
         x_ref[b] = worker.astype(BF16)
-    push_tiles(tw, to, w_ref, x_ref, accz_ref)
+    if last:
+        copy = pltpu.make_async_copy(out_ref, out_hbm, sem)
+        copy.start()
+    add_tiles(0, tiles, tw, to, w_ref, x_ref, accz_ref)
     z_ref[...] = accz_ref[...].astype(BF16)
+    if last:
+        copy.wait()
 
 
 def gather_sums(z_ref, flags_ref, reps):
@@ -139,7 +162,7 @@
         upper = jnp.broadcast_to(flags_ref[s, :1], first.shape) > 0.5
         send_ref[s] = jnp.where(upper, second, first).astype(BF16)
 
-    each_tile(send_ref.shape[0], step)
+    each_tile(send_ref.shape[0], step, 8)
 
 
 def open_firm_kernel(z_ref, signs_ref, base_ref, noise_ref, cluster_ref, send_ref, fo_ref, inv_ref, flags_ref, now_ref):
@@ -210,38 +233,33 @@
         out_ref[s] = total
 
 
-def closing_kernel(owners, index, all_ref, coef_ref, moment_ref, rows_ref, order_ref):
-    share, me = index[0], index[1]
+def moment_kernel(share, all_ref, coef_ref, moment_ref, rows_ref):
     reps, covars = coef_ref.shape
     columns = covars // CELLS
-    rows = all_ref.shape[0] // columns
-    spread = rows // reps
-    per = reps // owners
-    for c in range(columns):
-        for i in range(per):
-            start = me * (per * columns) + i * columns + c
-            piece = all_ref[pl.ds(start, owners, stride=spread * per * columns)]
-            order_ref[pl.ds(i, owners, stride=per)] = piece
-        coef_ref[:, c * CELLS : (c + 1) * CELLS] = order_ref[...]
     share_rows = moment_ref.shape[0]
     in_block = CELLS // share_rows
-    own = all_ref[pl.ds(share // in_block, rows, stride=columns)]
+    own = all_ref[pl.ds(share[0] // in_block, reps, stride=columns)]
     for c in range(columns):
-        other = all_ref[pl.ds(c, rows, stride=columns)]
+        other = all_ref[pl.ds(c, reps, stride=columns)]
+        coef_ref[:, c * CELLS : (c + 1) * CELLS] = other
         rows_ref[:, c * CELLS : (c + 1) * CELLS] = lax.dot_general(
             own, other, (((0,), (0,)), ((), ())), precision=HIGHEST, preferred_element_type=F32
         )
-    start = pl.multiple_of((share % in_block) * share_rows, share_rows)
-    moment_ref[...] = rows_ref[pl.ds(start, share_rows)] / rows
-
-
-def call(kernel, inputs, outputs, scratch=(), scalars=0, name=None):
+    start = pl.multiple_of((share[0] % in_block) * share_rows, share_rows)
+    moment_ref[...] = rows_ref[pl.ds(start, share_rows)]
+
+
+def keep(value):
+    return pltpu.with_memory_space_constraint(value, pltpu.VMEM)
+
+
+def call(kernel, inputs, outputs, scratch=(), scalars=0, name=None, specs=None, out_specs=None):
     return pl.pallas_call(
         kernel,
-        in_specs=[SMEM] * scalars + [VMEM] * (len(inputs) - scalars),
-        out_specs=[VMEM] * len(outputs),
-        out_shape=[jax.ShapeDtypeStruct(shape, dtype) for shape, dtype in outputs],
-        scratch_shapes=[pltpu.VMEM(shape, dtype) for shape, dtype in scratch],
+        in_specs=specs or [SMEM] * scalars + [VMEM] * (len(inputs) - scalars),
+        out_specs=out_specs or [VMEM] * len(outputs),
+        out_shape=[pltpu.VMEM(*item[:2]) if len(item) > 2 else jax.ShapeDtypeStruct(*item) for item in outputs],
+        scratch_shapes=[item if not isinstance(item, tuple) else pltpu.VMEM(*item) for item in scratch],
         compiler_params=PARAMS,
         name=name,
     )(*inputs)
@@ -277,14 +295,33 @@
     push_shape = ((owners, reps, CELLS), BF16)
     work_shape = ((WORK_BLOCKS, reps, CELLS), F32)
     firm_shape = ((FIRM_BLOCKS, reps, CELLS), F32)
-    z, worker_outcome = call(
+    tiles = tiles_w.shape[0]
+    inverse_shape = ((WORK_BLOCKS, 8, CELLS), F32)
+    inputs = (tile_worker, tile_owner, owner_block, tiles_w, signs)
+    inputs += (rows(worker_base), rows(worker_noise), rows(worker_cluster))
+    z, worker_outcome, turned, worker_inverse = call(
         first_kernel,
-        (tile_worker, tile_owner, owner_block, tiles_w, signs, rows(worker_base), rows(worker_noise), rows(worker_cluster)),
-        (((owners, reps + EXTRA, CELLS), BF16), work_shape),
-        (((WORK_BLOCKS, reps + EXTRA, CELLS), BF16), ((owners, reps + EXTRA, CELLS), F32)),
-        scalars=3,
+        tuple(pltpu.with_memory_space_constraint(x, pltpu.HBM) for x in inputs),
+        (((owners, reps + EXTRA, CELLS), BF16), work_shape, (tiles_w.shape, BF16, "keep"), inverse_shape),
+        (
+            pltpu.SMEM((tiles,), jnp.int32),
+            pltpu.SMEM((tiles,), jnp.int32),
+            pltpu.SMEM(owner_block.shape, jnp.int32),
+            (signs.shape, jnp.int32),
+            ((WORK_BLOCKS, CELLS), F32),
+            ((WORK_BLOCKS, CELLS), F32),
+            ((WORK_BLOCKS, CELLS), jnp.int32),
+            (tiles_w.shape, BF16),
+            ((WORK_BLOCKS, reps + EXTRA, CELLS), BF16),
+            ((owners, reps + EXTRA, CELLS), F32),
+            inverse_shape,
+            pltpu.SemaphoreType.DMA((7 + CHUNKS,)),
+        ),
+        specs=[HBM] * 8,
         name="first_push",
     )
+    share = lax.axis_index("tiles").astype(jnp.int32).reshape(1)
+    share, z = lax.optimization_barrier((share, z))
     z = exchange(z)
     send, firm_outcome, firm_inverse, flags, newer = call(
         open_firm_kernel,
@@ -293,33 +330,25 @@
         name="first_firm",
     )
     older = None
-    worker_inverse = None
-    scratch = (((WORK_BLOCKS, reps, CELLS), BF16), ((owners, reps, CELLS), F32))
+    scratch = (work_shape, ((WORK_BLOCKS, reps, CELLS), BF16), ((owners, reps, CELLS), F32))
     for k in range(1, SWEEPS):
-        measure, last = k == 1, k == SWEEPS - 1
+        last = k == SWEEPS - 1
         f = exchange(send)
-        inputs = (tile_worker, tile_owner, tiles_w, f, worker_outcome)
-        outputs = (push_shape,)
-        if measure:
-            outputs += (((WORK_BLOCKS, 8, CELLS), F32),)
-        else:
-            inputs += (worker_inverse,)
+        outputs, more, out_specs = (push_shape,), (), [VMEM]
         if last:
-            outputs += (((reps, WORK_BLOCKS * CELLS), F32),)
-        work_rows = reps + EXTRA if measure else reps
-        results = call(
-            lambda *refs, m=measure, e=last: sweep_kernel(m, e, *refs),
-            inputs,
+            whole = ((reps, WORK_BLOCKS * CELLS), F32)
+            outputs += (whole,)
+            more = (whole, pltpu.SemaphoreType.DMA)
+            out_specs.append(HBM)
+        z, *rest = call(
+            lambda *refs, e=last: sweep_kernel(e, *refs),
+            (tile_worker, tile_owner, tiles_w, keep(turned), f, worker_outcome, worker_inverse),
             outputs,
-            (((WORK_BLOCKS, work_rows, CELLS), F32),) + scratch,
+            scratch + more,
             scalars=2,
-            name="sweep_open" if measure else "sweep_close" if last else "sweep",
+            out_specs=out_specs,
+            name="sweep_close" if last else "sweep",
         )
-        z = results[0]
-        if measure:
-            worker_inverse = results[1]
-        if last:
-            worker_effect = results[1]
         z = exchange(z)
         inputs = (z, firm_outcome, firm_inverse, flags) + (() if older is None else (older,))
         if not last:
@@ -338,18 +367,23 @@
                 name="close_firm",
             )
     part = exchange(part.reshape(owners, -1, CELLS))
-    (spread,) = call(total_kernel, (part,), (((owners * groups,) + part.shape[1:], F32),), name="total")
-    everything = exchange(spread, ("tiles", "reps"))
-    index = jnp.stack([lax.axis_index("tiles"), lax.axis_index("reps")]).astype(jnp.int32)
-    coefficients, covariance = call(
-        lambda *refs: closing_kernel(owners, *refs),
-        (index, everything.reshape(-1, CELLS)),
+    (spread,) = call(total_kernel, (part,), ((part.shape, F32),), name="total")
+    everything = exchange(spread)
+    coefficients, moment = call(
+        moment_kernel,
+        (share, everything.reshape(-1, CELLS)),
         (((reps, covars), F32), ((covars // owners, covars), F32)),
-        (((CELLS, covars), F32), ((reps, CELLS), F32)),
+        (((CELLS, covars), F32),),
         scalars=1,
-        name="closing",
-    )
-    return (worker_effect, firm_effect, coefficients, covariance)
+        name="moment",
+    )
+    step = 1
+    while step < groups:
+        flip = step if step == 1 else 2 * step - 1
+        moment = moment + lax.ppermute(moment, "reps", [(g, g ^ flip) for g in range(groups)])
+        step *= 2
+    covariance = moment / (reps * groups)
+    return (rest[0], firm_effect, coefficients, covariance)
 
 
 def solution(mesh):

time: 268 us -> 231 us (0.86)
  Pallas kernels: 56.3 us -> 26.4 us
  blocking collectives: 182 us -> 193 us
  waiting for transfers between devices: 13.1 us -> 3.88 us
  local copies, waits for them, and re-layouts: 7.11 us -> 0.04 us
    pallas_call x14, Pallas kernels: 56.3 us -> 26.4 us  [call(): pl.pallas_call(kernel, in_specs=specs or [SMEM] * scalars + [VMEM] * (len...]
    all_to_all x1 -> x0, waiting for transfers between devices: 13.1 us -> none  [exchange(): return lax.all_to_all(values, axes, 0, 0, tiled=True)]
    all_to_all x12 -> x13, blocking collectives: 182 us -> 193 us  [exchange(): return lax.all_to_all(values, axes, 0, 0, tiled=True)]
    all_to_all x1 -> x0, starting transfers between devices: 7.35 us -> none  [exchange(): return lax.all_to_all(values, axes, 0, 0, tiled=True)]
    unnamed x28 -> x18, local copies, waits for them, and re-layouts: 7.11 us -> 0.04 us
    ppermute x0 -> x2, starting transfers between devices: none -> 5.97 us  [body(): lax.ppermute(moment, 'reps', [(g, g ^ flip) for g in range(groups)])]
    ppermute x0 -> x2, waiting for transfers between devices: none -> 3.88 us  [body(): lax.ppermute(moment, 'reps', [(g, g ^ flip) for g in range(groups)])]
  transfers between devices with their start and end apart: 1 -> 2, of which waited for: 1 -> 2; matrix products, arithmetic and copies ran while one was open for 0% -> 0% of each run, Pallas kernels for 0% -> 0%
where the time goes in v2:
time: 231 us
  blocking collectives  193 us (84%)
  Pallas kernels  26.4 us (11%)
  starting transfers between devices  5.97 us (3%)
  waiting for transfers between devices  3.88 us (2%)
    all_to_all x13, blocking collectives, exchange(): return lax.all_to_all(values, axes, 0, 0, tiled=True)  193 us
    pallas_call x14, Pallas kernels, call(): pl.pallas_call(kernel, in_specs=specs or [SMEM] * scalars + [VMEM] * (len...  26.4 us
    ppermute x2, starting transfers between devices, body(): lax.ppermute(moment, 'reps', [(g, g ^ flip) for g in range(groups)])  5.97 us
  transfers between devices with their start and end apart: 2, of which 2 were waited for; matrix products, arithmetic and copies ran while one was open for 0% of the time, Pallas kernels for 0%

profile of v2, /device:TPU:0, one launch (start us, length us, event | category | flops | bytes accessed | tf_op | source)
XLA Modules:
  0.0 230.6 jit_solution(11742230478739049161)
XLA Ops:
  0.6 0.0 copy-start.5
  0.6 0.0 copy-start.4
  0.7 0.0 copy-start.3
  0.7 0.0 copy-start.8
  0.7 0.0 copy-start.7
  0.7 0.0 copy-start.6
  0.7 0.0 copy-start
  0.7 3.8 %first_push.1 = (bf16[32,80,128]{2,1,0:T(8,128)(2,1)S(1)}, f32[16,64,128]{2,1,0:T(8,128)S(1)}, bf16[128,128,128]{2,1,0:T(8,128)(2,1)S(1)}, f32[16,8,128]{2,1,0:T(8,128)S(1)}) custom-call(s32[128]{0:T(128)} %refs_0_.9, s32[128]{0:T(128)} %refs_1_.9, s32[1,32]{1,0:T(1,128)} %ob_hbm.1, bf16[128,128,128]{2,1,0:T(8,128)(2,1)} %refs_2_.9, s32[64,256]{1,0:T(8,128)} %signs_ref.1, ...), custom_call_target="tpu_custom_call" | custom-call | tf_op jit(solution)/shard_map/first_push/pallas_call | solution.py:257
  4.5 19.8 %all_to_all.65.z_ref = bf16[32,80,128]{2,1,0:T(8,128)(2,1)S(1)} all-to-all(bf16[32,80,128]{2,1,0:T(8,128)(2,1)S(1)} %get-tuple-element.30), channel_id=1, replica_groups=mesh['tiles'=32,'reps'=4] {'tiles'}, dimensions={0} | all-to-all | bytes 1310720 | tf_op jit(solution)/shard_map/all_to_all | solution.py:290
  24.2 0.0 copy-done.3
  24.3 0.0 copy-done.8
  24.3 0.0 copy-done.7
  24.3 0.0 copy-done.6
  24.3 0.5 first_firm.1
  24.8 15.0 %all_to_all.66.refs_4_ = bf16[32,64,128]{2,1,0:T(8,128)(2,1)S(1)} all-to-all(bf16[32,64,128]{2,1,0:T(8,128)(2,1)S(1)} %get-tuple-element.31), channel_id=1, replica_groups=mesh['tiles'=32,'reps'=4] {'tiles'}, dimensions={0} | all-to-all | bytes 1048576 | tf_op jit(solution)/shard_map/all_to_all | solution.py:290
  39.8 0.0 copy-done.5
  39.8 0.0 copy-done.4
  39.8 0.0 copy-done
  39.8 3.6 %sweep.4 = bf16[32,64,128]{2,1,0:T(8,128)(2,1)S(1)} custom-call(s32[128]{0:T(128)S(1)} %copy-done.4, s32[128]{0:T(128)S(1)} %copy-done.5, bf16[128,128,128]{2,1,0:T(8,128)(2,1)S(1)} %copy-done, bf16[128,128,128]{2,1,0:T(8,128)(2,1)S(1)} %get-tuple-element.28.refs_3_, bf16[32,64,128]{2,1,0:T(8,128)(2,1)S(1)} %all_to_all.66.refs_4_, ...), custom_call_target="tpu_custom_call" | custom-call | tf_op jit(solution)/shard_map/sweep/pallas_call | solution.py:257
  43.3 15.0 %all_to_all.67.refs_0_ = bf16[32,64,128]{2,1,0:T(8,128)(2,1)S(1)} all-to-all(bf16[32,64,128]{2,1,0:T(8,128)(2,1)S(1)} %sweep.4), channel_id=1, replica_groups=mesh['tiles'=32,'reps'=4] {'tiles'}, dimensions={0} | all-to-all | bytes 1048576 | tf_op jit(solution)/shard_map/all_to_all | solution.py:290
  58.4 0.3 firm.4
  58.6 15.0 %all_to_all.68.refs_4_ = bf16[32,64,128]{2,1,0:T(8,128)(2,1)S(1)} all-to-all(bf16[32,64,128]{2,1,0:T(8,128)(2,1)S(1)} %get-tuple-element.37), channel_id=1, replica_groups=mesh['tiles'=32,'reps'=4] {'tiles'}, dimensions={0} | all-to-all | bytes 1048576 | tf_op jit(solution)/shard_map/all_to_all | solution.py:290
  73.7 3.6 %sweep.5 = bf16[32,64,128]{2,1,0:T(8,128)(2,1)S(1)} custom-call(s32[128]{0:T(128)S(1)} %copy-done.4, s32[128]{0:T(128)S(1)} %copy-done.5, bf16[128,128,128]{2,1,0:T(8,128)(2,1)S(1)} %copy-done, bf16[128,128,128]{2,1,0:T(8,128)(2,1)S(1)} %get-tuple-element.28.refs_3_, bf16[32,64,128]{2,1,0:T(8,128)(2,1)S(1)} %all_to_all.68.refs_4_, ...), custom_call_target="tpu_custom_call" | custom-call | tf_op jit(solution)/shard_map/sweep/pallas_call | solution.py:257
  77.2 15.0 %all_to_all.69.refs_0_ = bf16[32,64,128]{2,1,0:T(8,128)(2,1)S(1)} all-to-all(bf16[32,64,128]{2,1,0:T(8,128)(2,1)S(1)} %sweep.5), channel_id=1, replica_groups=mesh['tiles'=32,'reps'=4] {'tiles'}, dimensions={0} | all-to-all | bytes 1048576 | tf_op jit(solution)/shard_map/all_to_all | solution.py:290
  92.2 0.3 firm.5
  92.5 15.0 %all_to_all.70.refs_4_ = bf16[32,64,128]{2,1,0:T(8,128)(2,1)S(1)} all-to-all(bf16[32,64,128]{2,1,0:T(8,128)(2,1)S(1)} %get-tuple-element.39), channel_id=1, replica_groups=mesh['tiles'=32,'reps'=4] {'tiles'}, dimensions={0} | all-to-all | bytes 1048576 | tf_op jit(solution)/shard_map/all_to_all | solution.py:290
  107.6 3.6 %sweep.6 = bf16[32,64,128]{2,1,0:T(8,128)(2,1)S(1)} custom-call(s32[128]{0:T(128)S(1)} %copy-done.4, s32[128]{0:T(128)S(1)} %copy-done.5, bf16[128,128,128]{2,1,0:T(8,128)(2,1)S(1)} %copy-done, bf16[128,128,128]{2,1,0:T(8,128)(2,1)S(1)} %get-tuple-element.28.refs_3_, bf16[32,64,128]{2,1,0:T(8,128)(2,1)S(1)} %all_to_all.70.refs_4_, ...), custom_call_target="tpu_custom_call" | custom-call | tf_op jit(solution)/shard_map/sweep/pallas_call | solution.py:257
  111.1 15.0 %all_to_all.71.refs_0_ = bf16[32,64,128]{2,1,0:T(8,128)(2,1)S(1)} all-to-all(bf16[32,64,128]{2,1,0:T(8,128)(2,1)S(1)} %sweep.6), channel_id=1, replica_groups=mesh['tiles'=32,'reps'=4] {'tiles'}, dimensions={0} | all-to-all | bytes 1048576 | tf_op jit(solution)/shard_map/all_to_all | solution.py:290
  126.1 0.3 firm.6
  126.4 15.0 %all_to_all.72.refs_4_ = bf16[32,64,128]{2,1,0:T(8,128)(2,1)S(1)} all-to-all(bf16[32,64,128]{2,1,0:T(8,128)(2,1)S(1)} %get-tuple-element.41), channel_id=1, replica_groups=mesh['tiles'=32,'reps'=4] {'tiles'}, dimensions={0} | all-to-all | bytes 1048576 | tf_op jit(solution)/shard_map/all_to_all | solution.py:290
  141.5 3.6 %sweep.7 = bf16[32,64,128]{2,1,0:T(8,128)(2,1)S(1)} custom-call(s32[128]{0:T(128)S(1)} %copy-done.4, s32[128]{0:T(128)S(1)} %copy-done.5, bf16[128,128,128]{2,1,0:T(8,128)(2,1)S(1)} %copy-done, bf16[128,128,128]{2,1,0:T(8,128)(2,1)S(1)} %get-tuple-element.28.refs_3_, bf16[32,64,128]{2,1,0:T(8,128)(2,1)S(1)} %all_to_all.72.refs_4_, ...), custom_call_target="tpu_custom_call" | custom-call | tf_op jit(solution)/shard_map/sweep/pallas_call | solution.py:257
  145.0 15.0 %all_to_all.73.refs_0_ = bf16[32,64,128]{2,1,0:T(8,128)(2,1)S(1)} all-to-all(bf16[32,64,128]{2,1,0:T(8,128)(2,1)S(1)} %sweep.7), channel_id=1, replica_groups=mesh['tiles'=32,'reps'=4] {'tiles'}, dimensions={0} | all-to-all | bytes 1048576 | tf_op jit(solution)/shard_map/all_to_all | solution.py:290
  160.0 0.9 firm.7
  161.0 15.0 %all_to_all.74.refs_4_ = bf16[32,64,128]{2,1,0:T(8,128)(2,1)S(1)} all-to-all(bf16[32,64,128]{2,1,0:T(8,128)(2,1)S(1)} %get-tuple-element.43), channel_id=1, replica_groups=mesh['tiles'=32,'reps'=4] {'tiles'}, dimensions={0} | all-to-all | bytes 1048576 | tf_op jit(solution)/shard_map/all_to_all | solution.py:290
  176.0 0.0 copy-start.1
  176.0 0.0 copy-start.2
  176.0 3.6 %sweep_close.1 = (bf16[32,64,128]{2,1,0:T(8,128)(2,1)S(1)}, f32[64,2048]{1,0:T(8,128)}) custom-call(s32[128]{0:T(128)S(1)} %copy-done.4, s32[128]{0:T(128)S(1)} %copy-done.5, bf16[128,128,128]{2,1,0:T(8,128)(2,1)S(1)} %copy-done, bf16[128,128,128]{2,1,0:T(8,128)(2,1)S(1)} %get-tuple-element.28.refs_3_, bf16[32,64,128]{2,1,0:T(8,128)(2,1)S(1)} %all_to_all.74.refs_4_, ...), custom_call_target="tpu_custom_call" | custom-call | tf_op jit(solution)/shard_map/sweep_close/pallas_call | solution.py:257
  179.5 15.0 %all_to_all.75.refs_0_ = bf16[32,64,128]{2,1,0:T(8,128)(2,1)S(1)} all-to-all(bf16[32,64,128]{2,1,0:T(8,128)(2,1)S(1)} %get-tuple-element.45), channel_id=1, replica_groups=mesh['tiles'=32,'reps'=4] {'tiles'}, dimensions={0} | all-to-all | bytes 1048576 | tf_op jit(solution)/shard_map/all_to_all | solution.py:290
  194.6 0.0 copy-done.1
  194.6 0.0 copy-done.2
  194.6 1.7 close_firm.1
  196.3 11.8 %all_to_all.76.part_ref = f32[32,8,128]{2,1,0:T(8,128)S(1)} all-to-all(f32[32,8,128]{2,1,0:T(8,128)S(1)} %bitcast.10), channel_id=1, replica_groups=mesh['tiles'=32,'reps'=4] {'tiles'}, dimensions={0} | all-to-all | bytes 262144 | tf_op jit(solution)/shard_map/all_to_all | solution.py:290
  208.1 11.2 %all_to_all.77 = f32[32,8,128]{2,1,0:T(8,128)S(1)} all-to-all(f32[32,8,128]{2,1,0:T(8,128)S(1)} %total.1), channel_id=1, replica_groups=mesh['tiles'=32,'reps'=4] {'tiles'}, dimensions={0} | all-to-all | bytes 262144 | tf_op jit(solution)/shard_map/all_to_all | solution.py:290
  219.3 0.8 moment.1
  220.1 1.9 collective-permute-start
  222.0 2.0 collective-permute-done
  224.0 4.0 %collective-permute-start.1 = (f32[16,512]{1,0:T(8,128)S(1)}, f32[16,512]{1,0:T(8,128)S(1)}, u32[]{:S(2)}, u32[]{:S(2)}) collective-permute-start(f32[16,512]{1,0:T(8,128)S(1)} %add.6), channel_id=1, source_target_pairs={{0,3},{1,2},{2,1},{3,0},{4,7},{5,6},{6,5},{7,4},{8,11},{9,10},{10,... | collective-permute-start | bytes 98312 | tf_op jit(solution)/shard_map/ppermute | solution.py:383
  228.1 1.9 collective-permute-done.1
  230.0 0.6 add_multiply_fusion
  (2 shorter events, 0.0 us)
Async XLA Ops:
  0.6 39.1 %copy-start.5 = (s32[128]{0:T(128)S(1)}, s32[128]{0:T(128)}, u32[]{:S(2)}) copy-start(s32[128]{0:T(128)} %refs_1_.9) | copy-start | bytes 1540
  0.6 39.1 %copy-start.4 = (s32[128]{0:T(128)S(1)}, s32[128]{0:T(128)}, u32[]{:S(2)}) copy-start(s32[128]{0:T(128)} %refs_0_.9) | copy-start | bytes 1540
  0.7 23.6 %copy-start.3 = (s32[64,256]{1,0:T(8,128)S(1)}, s32[64,256]{1,0:T(8,128)}, u32[]{:S(2)}) copy-start(s32[64,256]{1,0:T(8,128)} %signs_ref.1) | copy-start | bytes 196612
  0.7 23.6 %copy-start.8 = (s32[256]{0:T(256)S(1)}, s32[256]{0:T(256)}, u32[]{:S(2)}) copy-start(s32[256]{0:T(256)} %param.22) | copy-start | bytes 3076
  0.7 23.6 %copy-start.7 = (f32[256]{0:T(256)S(1)}, f32[256]{0:T(256)}, u32[]{:S(2)}) copy-start(f32[256]{0:T(256)} %param.21) | copy-start | bytes 3076
  0.7 23.6 %copy-start.6 = (f32[256]{0:T(256)S(1)}, f32[256]{0:T(256)}, u32[]{:S(2)}) copy-start(f32[256]{0:T(256)} %param.20) | copy-start | bytes 3076
  0.7 39.1 %copy-start = (bf16[128,128,128]{2,1,0:T(8,128)(2,1)S(1)}, bf16[128,128,128]{2,1,0:T(8,128)(2,1)}, u32[]{:S(2)}) copy-start(bf16[128,128,128]{2,1,0:T(8,128)(2,1)} %refs_2_.9) | copy-start | bytes 12582916
  176.0 18.6 %copy-start.1 = (f32[512,512]{1,0:T(8,128)S(1)}, f32[512,512]{1,0:T(8,128)}, u32[]{:S(2)}) copy-start(f32[512,512]{1,0:T(8,128)} %refs_6_.1) | copy-start | bytes 3145732
  176.0 18.6 %copy-start.2 = (f32[256,512]{1,0:T(8,128)S(1)}, f32[256,512]{1,0:T(8,128)}, u32[]{:S(2)}) copy-start(f32[256,512]{1,0:T(8,128)} %refs_5_.1) | copy-start | bytes 1572868
  220.1 3.9 %collective-permute-start = (f32[16,512]{1,0:T(8,128)S(1)}, f32[16,512]{1,0:T(8,128)S(1)}, u32[]{:S(2)}, u32[]{:S(2)}) collective-permute-start(f32[16,512]{1,0:T(8,128)S(1)} %get-tuple-element.51), channel_id=1, source_target_pairs={{0,1},{1,0},{2,3},{3,2},{4,5},{5,4},{6,7},{7,6},{8,9},{9,8},{10,11... | collective-permute-start | bytes 98312 | tf_op jit(solution)/shard_map/ppermute | solution.py:383
  224.0 5.9 %collective-permute-start.1 = (f32[16,512]{1,0:T(8,128)S(1)}, f32[16,512]{1,0:T(8,128)S(1)}, u32[]{:S(2)}, u32[]{:S(2)}) collective-permute-start(f32[16,512]{1,0:T(8,128)S(1)} %add.6), channel_id=1, source_target_pairs={{0,3},{1,2},{2,1},{3,0},{4,7},{5,6},{6,5},{7,4},{8,11},{9,10},{10,... | collective-permute-start | bytes 98312 | tf_op jit(solution)/shard_map/ppermute | solution.py:383

commit v3 on v2

--- a/solution.py
+++ b/solution.py
@@ -9,7 +9,7 @@
 FIRM_BLOCKS = 2
 SWEEPS = 6
 CELLS = 128
-EXTRA = 16
+EXTRA = 8
 SPECTRAL = 0.8
 UNROLL = 64
 CHUNKS = 4
@@ -203,13 +203,13 @@
 
 
 def firm_kernel(omega, has_older, *refs):
-    if has_older:
-        z_ref, fo_ref, inv_ref, flags_ref, older_ref, send_ref, now_ref = refs
-    else:
-        (z_ref, fo_ref, inv_ref, flags_ref, send_ref, now_ref), older_ref = refs, None
+    (z_ref, fo_ref, inv_ref, flags_ref), refs = refs[:4], refs[4:]
+    older_ref = refs[0] if has_older else None
+    send_ref, *now_ref = refs[1:] if has_older else refs
     firms = next_firms(omega, z_ref, fo_ref, inv_ref, flags_ref, older_ref)
-    for j in range(FIRM_BLOCKS):
-        now_ref[j] = firms[j]
+    if now_ref:
+        for j in range(FIRM_BLOCKS):
+            now_ref[0][j] = firms[j]
     scatter_firms(firms, flags_ref, send_ref)
 
 
@@ -352,13 +352,13 @@
         z = exchange(z)
         inputs = (z, firm_outcome, firm_inverse, flags) + (() if older is None else (older,))
         if not last:
-            send, now = call(
+            send, *now = call(
                 lambda *refs, w=omegas[k], h=older is not None: firm_kernel(w, h, *refs),
                 inputs,
-                (push_shape, firm_shape),
+                (push_shape, firm_shape) if k < SWEEPS - 2 else (push_shape,),
                 name="firm",
             )
-            older, newer = newer, now
+            older, newer = newer, now[0] if now else None
         else:
             firm_effect, part = call(
                 lambda *refs, w=omegas[k]: close_firm_kernel(w, *refs),
@@ -377,12 +377,8 @@
         scalars=1,
         name="moment",
     )
-    step = 1
-    while step < groups:
-        flip = step if step == 1 else 2 * step - 1
-        moment = moment + lax.ppermute(moment, "reps", [(g, g ^ flip) for g in range(groups)])
-        step *= 2
-    covariance = moment / (reps * groups)
+    shifted = [lax.ppermute(moment, "reps", [(g, (g + d) % groups) for g in range(groups)]) for d in range(1, groups)]
+    covariance = ((moment + shifted[1]) + (shifted[0] + shifted[2])) / (reps * groups)
     return (rest[0], firm_effect, coefficients, covariance)
 
 

time: 231 us -> 230 us (level)
    ppermute x2 -> x3, starting transfers between devices: 5.97 us -> 5.9 us  [body(): lax.ppermute(moment, 'reps', [(g, (g + d) % groups) for g in range(groups)])]
  transfers between devices with their start and end apart: 2 -> 3, of which waited for: 2 -> 1; matrix products, arithmetic and copies ran while one was open for 0% -> 0% of each run, Pallas kernels for 0% -> 0%
where the time goes in v3:
time: 230 us; the launch traced here: 229 us
  blocking collectives  192 us (83%)
  Pallas kernels  25.8 us (11%)
  starting transfers between devices  5.9 us (3%)
  waiting for transfers between devices  3.62 us (2%)
    all_to_all x13, blocking collectives, exchange(): return lax.all_to_all(values, axes, 0, 0, tiled=True)  192 us
    pallas_call x14, Pallas kernels, call(): pl.pallas_call(kernel, in_specs=specs or [SMEM] * scalars + [VMEM] * (len...  25.8 us
    ppermute x3, starting transfers between devices, body(): lax.ppermute(moment, 'reps', [(g, (g + d) % groups) for g in range(groups)])  5.9 us
  transfers between devices with their start and end apart: 3, of which 1 were waited for; matrix products, arithmetic and copies ran while one was open for 0% of the time, Pallas kernels for 0%

profile of v3, /device:TPU:0, one launch (start us, length us, event | category | flops | bytes accessed | tf_op | source)
XLA Modules:
  0.0 229.0 jit_solution(6950835505663239984)
XLA Ops:
  0.6 0.0 copy-start.5
  0.6 0.0 copy-start.4
  0.7 0.0 copy-start.3
  0.7 0.0 copy-start.8
  0.7 0.0 copy-start.7
  0.7 0.0 copy-start.6
  0.7 0.0 copy-start
  0.7 3.8 %first_push.1 = (bf16[32,72,128]{2,1,0:T(8,128)(2,1)S(1)}, f32[16,64,128]{2,1,0:T(8,128)S(1)}, bf16[128,128,128]{2,1,0:T(8,128)(2,1)S(1)}, f32[16,8,128]{2,1,0:T(8,128)S(1)}) custom-call(s32[128]{0:T(128)} %refs_0_.9, s32[128]{0:T(128)} %refs_1_.9, s32[1,32]{1,0:T(1,128)} %ob_hbm.1, bf16[128,128,128]{2,1,0:T(8,128)(2,1)} %refs_2_.9, s32[64,256]{1,0:T(8,128)} %signs_ref.1, ...), custom_call_target="tpu_custom_call" | custom-call | tf_op jit(solution)/shard_map/first_push/pallas_call | solution.py:257
  4.5 19.0 %all_to_all.65.z_ref = bf16[32,72,128]{2,1,0:T(8,128)(2,1)S(1)} all-to-all(bf16[32,72,128]{2,1,0:T(8,128)(2,1)S(1)} %get-tuple-element.29), channel_id=1, replica_groups=mesh['tiles'=32,'reps'=4] {'tiles'}, dimensions={0} | all-to-all | bytes 1179648 | tf_op jit(solution)/shard_map/all_to_all | solution.py:290
  23.5 0.0 copy-done.3
  23.5 0.0 copy-done.8
  23.5 0.0 copy-done.7
  23.5 0.0 copy-done.6
  23.5 0.5 first_firm.1
  24.0 15.0 %all_to_all.66.refs_4_ = bf16[32,64,128]{2,1,0:T(8,128)(2,1)S(1)} all-to-all(bf16[32,64,128]{2,1,0:T(8,128)(2,1)S(1)} %get-tuple-element.30), channel_id=1, replica_groups=mesh['tiles'=32,'reps'=4] {'tiles'}, dimensions={0} | all-to-all | bytes 1048576 | tf_op jit(solution)/shard_map/all_to_all | solution.py:290
  39.1 0.0 copy-done.5
  39.1 0.0 copy-done.4
  39.1 0.0 copy-done
  39.1 3.6 %sweep.4 = bf16[32,64,128]{2,1,0:T(8,128)(2,1)S(1)} custom-call(s32[128]{0:T(128)S(1)} %copy-done.4, s32[128]{0:T(128)S(1)} %copy-done.5, bf16[128,128,128]{2,1,0:T(8,128)(2,1)S(1)} %copy-done, bf16[128,128,128]{2,1,0:T(8,128)(2,1)S(1)} %get-tuple-element.27.refs_3_, bf16[32,64,128]{2,1,0:T(8,128)(2,1)S(1)} %all_to_all.66.refs_4_, ...), custom_call_target="tpu_custom_call" | custom-call | tf_op jit(solution)/shard_map/sweep/pallas_call | solution.py:257
  42.7 15.0 %all_to_all.67.refs_0_ = bf16[32,64,128]{2,1,0:T(8,128)(2,1)S(1)} all-to-all(bf16[32,64,128]{2,1,0:T(8,128)(2,1)S(1)} %sweep.4), channel_id=1, replica_groups=mesh['tiles'=32,'reps'=4] {'tiles'}, dimensions={0} | all-to-all | bytes 1048576 | tf_op jit(solution)/shard_map/all_to_all | solution.py:290
  57.7 0.3 firm.4
  58.0 15.0 %all_to_all.68.refs_4_ = bf16[32,64,128]{2,1,0:T(8,128)(2,1)S(1)} all-to-all(bf16[32,64,128]{2,1,0:T(8,128)(2,1)S(1)} %get-tuple-element.36), channel_id=1, replica_groups=mesh['tiles'=32,'reps'=4] {'tiles'}, dimensions={0} | all-to-all | bytes 1048576 | tf_op jit(solution)/shard_map/all_to_all | solution.py:290
  73.0 3.6 %sweep.5 = bf16[32,64,128]{2,1,0:T(8,128)(2,1)S(1)} custom-call(s32[128]{0:T(128)S(1)} %copy-done.4, s32[128]{0:T(128)S(1)} %copy-done.5, bf16[128,128,128]{2,1,0:T(8,128)(2,1)S(1)} %copy-done, bf16[128,128,128]{2,1,0:T(8,128)(2,1)S(1)} %get-tuple-element.27.refs_3_, bf16[32,64,128]{2,1,0:T(8,128)(2,1)S(1)} %all_to_all.68.refs_4_, ...), custom_call_target="tpu_custom_call" | custom-call | tf_op jit(solution)/shard_map/sweep/pallas_call | solution.py:257
  76.6 15.0 %all_to_all.69.refs_0_ = bf16[32,64,128]{2,1,0:T(8,128)(2,1)S(1)} all-to-all(bf16[32,64,128]{2,1,0:T(8,128)(2,1)S(1)} %sweep.5), channel_id=1, replica_groups=mesh['tiles'=32,'reps'=4] {'tiles'}, dimensions={0} | all-to-all | bytes 1048576 | tf_op jit(solution)/shard_map/all_to_all | solution.py:290
  91.6 0.3 firm.5
  91.9 15.0 %all_to_all.70.refs_4_ = bf16[32,64,128]{2,1,0:T(8,128)(2,1)S(1)} all-to-all(bf16[32,64,128]{2,1,0:T(8,128)(2,1)S(1)} %get-tuple-element.38), channel_id=1, replica_groups=mesh['tiles'=32,'reps'=4] {'tiles'}, dimensions={0} | all-to-all | bytes 1048576 | tf_op jit(solution)/shard_map/all_to_all | solution.py:290
  106.9 3.6 %sweep.6 = bf16[32,64,128]{2,1,0:T(8,128)(2,1)S(1)} custom-call(s32[128]{0:T(128)S(1)} %copy-done.4, s32[128]{0:T(128)S(1)} %copy-done.5, bf16[128,128,128]{2,1,0:T(8,128)(2,1)S(1)} %copy-done, bf16[128,128,128]{2,1,0:T(8,128)(2,1)S(1)} %get-tuple-element.27.refs_3_, bf16[32,64,128]{2,1,0:T(8,128)(2,1)S(1)} %all_to_all.70.refs_4_, ...), custom_call_target="tpu_custom_call" | custom-call | tf_op jit(solution)/shard_map/sweep/pallas_call | solution.py:257
  110.5 15.0 %all_to_all.71.refs_0_ = bf16[32,64,128]{2,1,0:T(8,128)(2,1)S(1)} all-to-all(bf16[32,64,128]{2,1,0:T(8,128)(2,1)S(1)} %sweep.6), channel_id=1, replica_groups=mesh['tiles'=32,'reps'=4] {'tiles'}, dimensions={0} | all-to-all | bytes 1048576 | tf_op jit(solution)/shard_map/all_to_all | solution.py:290
  125.5 0.3 firm.6
  125.8 15.0 %all_to_all.72.refs_4_ = bf16[32,64,128]{2,1,0:T(8,128)(2,1)S(1)} all-to-all(bf16[32,64,128]{2,1,0:T(8,128)(2,1)S(1)} %get-tuple-element.40), channel_id=1, replica_groups=mesh['tiles'=32,'reps'=4] {'tiles'}, dimensions={0} | all-to-all | bytes 1048576 | tf_op jit(solution)/shard_map/all_to_all | solution.py:290
  140.8 3.6 %sweep.7 = bf16[32,64,128]{2,1,0:T(8,128)(2,1)S(1)} custom-call(s32[128]{0:T(128)S(1)} %copy-done.4, s32[128]{0:T(128)S(1)} %copy-done.5, bf16[128,128,128]{2,1,0:T(8,128)(2,1)S(1)} %copy-done, bf16[128,128,128]{2,1,0:T(8,128)(2,1)S(1)} %get-tuple-element.27.refs_3_, bf16[32,64,128]{2,1,0:T(8,128)(2,1)S(1)} %all_to_all.72.refs_4_, ...), custom_call_target="tpu_custom_call" | custom-call | tf_op jit(solution)/shard_map/sweep/pallas_call | solution.py:257
  144.3 15.0 %all_to_all.73.refs_0_ = bf16[32,64,128]{2,1,0:T(8,128)(2,1)S(1)} all-to-all(bf16[32,64,128]{2,1,0:T(8,128)(2,1)S(1)} %sweep.7), channel_id=1, replica_groups=mesh['tiles'=32,'reps'=4] {'tiles'}, dimensions={0} | all-to-all | bytes 1048576 | tf_op jit(solution)/shard_map/all_to_all | solution.py:290
  159.4 0.3 firm.7
  159.7 15.0 %all_to_all.74.refs_4_ = bf16[32,64,128]{2,1,0:T(8,128)(2,1)S(1)} all-to-all(bf16[32,64,128]{2,1,0:T(8,128)(2,1)S(1)} %firm.7), channel_id=1, replica_groups=mesh['tiles'=32,'reps'=4] {'tiles'}, dimensions={0} | all-to-all | bytes 1048576 | tf_op jit(solution)/shard_map/all_to_all | solution.py:290
  174.7 0.0 copy-start.1
  174.7 0.0 copy-start.2
  174.7 3.6 %sweep_close.1 = (bf16[32,64,128]{2,1,0:T(8,128)(2,1)S(1)}, f32[64,2048]{1,0:T(8,128)}) custom-call(s32[128]{0:T(128)S(1)} %copy-done.4, s32[128]{0:T(128)S(1)} %copy-done.5, bf16[128,128,128]{2,1,0:T(8,128)(2,1)S(1)} %copy-done, bf16[128,128,128]{2,1,0:T(8,128)(2,1)S(1)} %get-tuple-element.27.refs_3_, bf16[32,64,128]{2,1,0:T(8,128)(2,1)S(1)} %all_to_all.74.refs_4_, ...), custom_call_target="tpu_custom_call" | custom-call | tf_op jit(solution)/shard_map/sweep_close/pallas_call | solution.py:257
  178.3 15.0 %all_to_all.75.refs_0_ = bf16[32,64,128]{2,1,0:T(8,128)(2,1)S(1)} all-to-all(bf16[32,64,128]{2,1,0:T(8,128)(2,1)S(1)} %get-tuple-element.43), channel_id=1, replica_groups=mesh['tiles'=32,'reps'=4] {'tiles'}, dimensions={0} | all-to-all | bytes 1048576 | tf_op jit(solution)/shard_map/all_to_all | solution.py:290
  193.3 0.0 copy-done.1
  193.3 0.0 copy-done.2
  193.3 1.7 close_firm.1
  195.0 11.8 %all_to_all.76.part_ref = f32[32,8,128]{2,1,0:T(8,128)S(1)} all-to-all(f32[32,8,128]{2,1,0:T(8,128)S(1)} %bitcast.10), channel_id=1, replica_groups=mesh['tiles'=32,'reps'=4] {'tiles'}, dimensions={0} | all-to-all | bytes 262144 | tf_op jit(solution)/shard_map/all_to_all | solution.py:290
  206.8 11.2 %all_to_all.77 = f32[32,8,128]{2,1,0:T(8,128)S(1)} all-to-all(f32[32,8,128]{2,1,0:T(8,128)S(1)} %total.1), channel_id=1, replica_groups=mesh['tiles'=32,'reps'=4] {'tiles'}, dimensions={0} | all-to-all | bytes 262144 | tf_op jit(solution)/shard_map/all_to_all | solution.py:290
  218.0 0.8 moment.1
  218.8 4.0 %collective-permute-start.2 = (f32[16,512]{1,0:T(8,128)S(1)}, f32[16,512]{1,0:T(8,128)S(1)}, u32[]{:S(2)}, u32[]{:S(2)}) collective-permute-start(f32[16,512]{1,0:T(8,128)S(1)} %get-tuple-element.49), channel_id=1, source_target_pairs={{0,3},{1,0},{2,1},{3,2},{4,7},{5,4},{6,5},{7,6},{8,11},{9,8},{10,9... | collective-permute-start | bytes 98312 | tf_op jit(solution)/shard_map/ppermute | solution.py:380
  222.9 0.0 collective-permute-start.1
  222.9 1.9 collective-permute-start
  224.7 0.0 collective-permute-done.2
  224.7 3.6 %collective-permute-done.1 = f32[16,512]{1,0:T(8,128)S(1)} collective-permute-done((f32[16,512]{1,0:T(8,128)S(1)}, f32[16,512]{1,0:T(8,128)S(1)}, u32[]{:S(2)}, u32[]{:S(2)}) %collective-permute-start.1) | collective-permute-done | bytes 32800 | tf_op jit(solution)/shard_map/ppermute | solution.py:380
  228.3 0.0 collective-permute-done
  228.3 0.6 add_multiply_fusion
  (1 shorter events, 0.0 us)
Async XLA Ops:
  0.6 38.5 %copy-start.5 = (s32[128]{0:T(128)S(1)}, s32[128]{0:T(128)}, u32[]{:S(2)}) copy-start(s32[128]{0:T(128)} %refs_1_.9) | copy-start | bytes 1540
  0.6 38.4 %copy-start.4 = (s32[128]{0:T(128)S(1)}, s32[128]{0:T(128)}, u32[]{:S(2)}) copy-start(s32[128]{0:T(128)} %refs_0_.9) | copy-start | bytes 1540
  0.7 22.9 %copy-start.3 = (s32[64,256]{1,0:T(8,128)S(1)}, s32[64,256]{1,0:T(8,128)}, u32[]{:S(2)}) copy-start(s32[64,256]{1,0:T(8,128)} %signs_ref.1) | copy-start | bytes 196612
  0.7 22.8 %copy-start.8 = (s32[256]{0:T(256)S(1)}, s32[256]{0:T(256)}, u32[]{:S(2)}) copy-start(s32[256]{0:T(256)} %param.22) | copy-start | bytes 3076
  0.7 22.8 %copy-start.7 = (f32[256]{0:T(256)S(1)}, f32[256]{0:T(256)}, u32[]{:S(2)}) copy-start(f32[256]{0:T(256)} %param.21) | copy-start | bytes 3076
  0.7 22.8 %copy-start.6 = (f32[256]{0:T(256)S(1)}, f32[256]{0:T(256)}, u32[]{:S(2)}) copy-start(f32[256]{0:T(256)} %param.20) | copy-start | bytes 3076
  0.7 38.4 %copy-start = (bf16[128,128,128]{2,1,0:T(8,128)(2,1)S(1)}, bf16[128,128,128]{2,1,0:T(8,128)(2,1)}, u32[]{:S(2)}) copy-start(bf16[128,128,128]{2,1,0:T(8,128)(2,1)} %refs_2_.9) | copy-start | bytes 12582916
  174.7 18.6 %copy-start.1 = (f32[512,512]{1,0:T(8,128)S(1)}, f32[512,512]{1,0:T(8,128)}, u32[]{:S(2)}) copy-start(f32[512,512]{1,0:T(8,128)} %refs_6_.1) | copy-start | bytes 3145732
  174.7 18.6 %copy-start.2 = (f32[256,512]{1,0:T(8,128)S(1)}, f32[256,512]{1,0:T(8,128)}, u32[]{:S(2)}) copy-start(f32[256,512]{1,0:T(8,128)} %refs_5_.1) | copy-start | bytes 1572868
  218.8 5.9 %collective-permute-start.2 = (f32[16,512]{1,0:T(8,128)S(1)}, f32[16,512]{1,0:T(8,128)S(1)}, u32[]{:S(2)}, u32[]{:S(2)}) collective-permute-start(f32[16,512]{1,0:T(8,128)S(1)} %get-tuple-element.49), channel_id=1, source_target_pairs={{0,3},{1,0},{2,1},{3,2},{4,7},{5,4},{6,5},{7,6},{8,11},{9,8},{10,9... | collective-permute-start | bytes 98312 | tf_op jit(solution)/shard_map/ppermute | solution.py:380
  222.9 5.5 %collective-permute-start.1 = (f32[16,512]{1,0:T(8,128)S(1)}, f32[16,512]{1,0:T(8,128)S(1)}, u32[]{:S(2)}, u32[]{:S(2)}) collective-permute-start(f32[16,512]{1,0:T(8,128)S(1)} %get-tuple-element.49), channel_id=1, source_target_pairs={{0,1},{1,2},{2,3},{3,0},{4,5},{5,6},{6,7},{7,4},{8,9},{9,10},{10,1... | collective-permute-start | bytes 98312 | tf_op jit(solution)/shard_map/ppermute | solution.py:380
  222.9 5.5 %collective-permute-start = (f32[16,512]{1,0:T(8,128)S(1)}, f32[16,512]{1,0:T(8,128)S(1)}, u32[]{:S(2)}, u32[]{:S(2)}) collective-permute-start(f32[16,512]{1,0:T(8,128)S(1)} %get-tuple-element.49), channel_id=1, source_target_pairs={{0,2},{1,3},{2,0},{3,1},{4,6},{5,7},{6,4},{7,5},{8,10},{9,11},{10,... | collective-permute-start | bytes 98312 | tf_op jit(solution)/shard_map/ppermute | solution.py:380

commit v4 on v3

--- a/solution.py
+++ b/solution.py
@@ -59,8 +59,8 @@
 
 def first_kernel(
     tw_hbm, to_hbm, ob_hbm, w_hbm, signs_hbm, base_hbm, noise_hbm, cluster_hbm,
-    z_ref, wo_ref, turned_ref, inv_ref,
-    tw, to, ob, signs_ref, base_ref, noise_ref, cluster_ref, w_ref, x_ref, acc_ref, mass_ref, sems,
+    z_ref, wo_ref, w_ref, turned_ref, inv_ref,
+    tw, to, ob, signs_ref, base_ref, noise_ref, cluster_ref, x_ref, acc_ref, mass_ref, sems,
 ):
     small = [
         (signs_hbm, signs_ref),
@@ -143,6 +143,20 @@
         copy.wait()
 
 
+def halves(value):
+    high = value.astype(BF16)
+    return high, (value - high.astype(F32)).astype(BF16)
+
+
+def product(left, right, dims):
+    (a, b), (c, d) = halves(left), halves(right)
+
+    def dot(p, q):
+        return lax.dot_general(p, q, (dims, ((), ())), preferred_element_type=F32)
+
+    return (dot(a, d) + dot(b, c)) + dot(a, c)
+
+
 def gather_sums(z_ref, flags_ref, reps):
     zero = jnp.zeros((reps, CELLS), F32)
 
@@ -217,10 +231,8 @@
     firms = next_firms(omega, z_ref, fo_ref, inv_ref, flags_ref, older_ref)
     for j in range(FIRM_BLOCKS):
         firm_ref[:, j * CELLS : (j + 1) * CELLS] = firms[j]
-    projected = jnp.dot(firm_ref[...], cov_ref[...], precision=HIGHEST, preferred_element_type=F32)
-    whitened = lax.dot_general(
-        projected, white_ref[...], (((1,), (1,)), ((), ())), precision=HIGHEST, preferred_element_type=F32
-    )
+    projected = product(firm_ref[...], cov_ref[...], ((1,), (0,)))
+    whitened = product(projected, white_ref[...], ((1,), (1,)))
     reps = whitened.shape[0]
     columns = whitened.shape[1] // CELLS
     for c in range(columns):
@@ -236,7 +248,7 @@
 def moment_kernel(share, all_ref, coef_ref, moment_ref, rows_ref):
     reps, covars = coef_ref.shape
     columns = covars // CELLS
-    share_rows = moment_ref.shape[0]
+    share_rows = moment_ref.shape[1]
     in_block = CELLS // share_rows
     own = all_ref[pl.ds(share[0] // in_block, reps, stride=columns)]
     for c in range(columns):
@@ -246,7 +258,8 @@
             own, other, (((0,), (0,)), ((), ())), precision=HIGHEST, preferred_element_type=F32
         )
     start = pl.multiple_of((share[0] % in_block) * share_rows, share_rows)
-    moment_ref[...] = rows_ref[pl.ds(start, share_rows)]
+    for g in range(moment_ref.shape[0]):
+        moment_ref[g] = rows_ref[pl.ds(start, share_rows)]
 
 
 def keep(value):
@@ -296,13 +309,14 @@
     work_shape = ((WORK_BLOCKS, reps, CELLS), F32)
     firm_shape = ((FIRM_BLOCKS, reps, CELLS), F32)
     tiles = tiles_w.shape[0]
+    held_shape = (tiles_w.shape, BF16, "keep")
     inverse_shape = ((WORK_BLOCKS, 8, CELLS), F32)
     inputs = (tile_worker, tile_owner, owner_block, tiles_w, signs)
     inputs += (rows(worker_base), rows(worker_noise), rows(worker_cluster))
-    z, worker_outcome, turned, worker_inverse = call(
+    z, worker_outcome, held, turned, worker_inverse = call(
         first_kernel,
         tuple(pltpu.with_memory_space_constraint(x, pltpu.HBM) for x in inputs),
-        (((owners, reps + EXTRA, CELLS), BF16), work_shape, (tiles_w.shape, BF16, "keep"), inverse_shape),
+        (((owners, reps + EXTRA, CELLS), BF16), work_shape, held_shape, held_shape, inverse_shape),
         (
             pltpu.SMEM((tiles,), jnp.int32),
             pltpu.SMEM((tiles,), jnp.int32),
@@ -311,7 +325,6 @@
             ((WORK_BLOCKS, CELLS), F32),
             ((WORK_BLOCKS, CELLS), F32),
             ((WORK_BLOCKS, CELLS), jnp.int32),
-            (tiles_w.shape, BF16),
             ((WORK_BLOCKS, reps + EXTRA, CELLS), BF16),
             ((owners, reps + EXTRA, CELLS), F32),
             inverse_shape,
@@ -342,7 +355,7 @@
             out_specs.append(HBM)
         z, *rest = call(
             lambda *refs, e=last: sweep_kernel(e, *refs),
-            (tile_worker, tile_owner, tiles_w, keep(turned), f, worker_outcome, worker_inverse),
+            (tile_worker, tile_owner, keep(held), keep(turned), f, worker_outcome, worker_inverse),
             outputs,
             scratch + more,
             scalars=2,
@@ -369,16 +382,16 @@
     part = exchange(part.reshape(owners, -1, CELLS))
     (spread,) = call(total_kernel, (part,), ((part.shape, F32),), name="total")
     everything = exchange(spread)
-    coefficients, moment = call(
+    coefficients, moments = call(
         moment_kernel,
         (share, everything.reshape(-1, CELLS)),
-        (((reps, covars), F32), ((covars // owners, covars), F32)),
+        (((reps, covars), F32), ((groups, covars // owners, covars), F32)),
         (((CELLS, covars), F32),),
         scalars=1,
         name="moment",
     )
-    shifted = [lax.ppermute(moment, "reps", [(g, (g + d) % groups) for g in range(groups)]) for d in range(1, groups)]
-    covariance = ((moment + shifted[1]) + (shifted[0] + shifted[2])) / (reps * groups)
+    moments = exchange(moments, "reps")
+    covariance = jnp.sum(moments, axis=0) / (reps * groups)
     return (rest[0], firm_effect, coefficients, covariance)
 
 

time: 230 us -> 231 us (level)
  blocking collectives: 192 us -> 203 us
  starting transfers between devices: 5.9 us -> 0 us
  waiting for transfers between devices: 3.62 us -> 0 us
    all_to_all x13 -> x14, blocking collectives: 192 us -> 203 us  [exchange(): return lax.all_to_all(values, axes, 0, 0, tiled=True)]
    ppermute x3 -> x0, starting transfers between devices: 5.9 us -> none  [body(): lax.ppermute(moment, 'reps', [(g, (g + d) % groups) for g in range(groups)])]
    ppermute x3 -> x0, waiting for transfers between devices: 3.62 us -> none  [body(): lax.ppermute(moment, 'reps', [(g, (g + d) % groups) for g in range(groups)])]
  transfers between devices with their start and end apart: 3 -> 0, of which waited for: 1 -> 0; matrix products, arithmetic and copies ran while one was open for 0% -> 0% of each run, Pallas kernels for 0% -> 0%
where the time goes in v4:
time: 231 us; the launch traced here: 230 us
  blocking collectives  203 us (88%)
  Pallas kernels  25.2 us (11%)
    all_to_all x14, blocking collectives, exchange(): return lax.all_to_all(values, axes, 0, 0, tiled=True)  203 us
    pallas_call x14, Pallas kernels, call(): pl.pallas_call(kernel, in_specs=specs or [SMEM] * scalars + [VMEM] * (len...  25.2 us

profile of v4, /device:TPU:0, one launch (start us, length us, event | category | flops | bytes accessed | tf_op | source)
XLA Modules:
  0.0 229.9 jit_solution(4533842810006273650)
XLA Ops:
  0.6 0.0 copy-start.4
  0.6 0.0 copy-start.3
  0.7 0.0 copy-start.2
  0.7 0.0 copy-start.7
  0.7 0.0 copy-start.6
  0.7 0.0 copy-start.5
  0.7 3.7 %first_push.1 = (bf16[32,72,128]{2,1,0:T(8,128)(2,1)S(1)}, f32[16,64,128]{2,1,0:T(8,128)S(1)}, bf16[128,128,128]{2,1,0:T(8,128)(2,1)S(1)}, bf16[128,128,128]{2,1,0:T(8,128)(2,1)S(1)}, f32[16,8,128]{2,1,0:T(8,128)S(1)}) custom-call(s32[128]{0:T(128)} %refs_0_.9, s32[128]{0:T(128)} %refs_1_.9, s32[1,32]{1,0:T(1,128)} %ob_hbm.1, bf16[128,128,128]{2,1,0:T(8,128)(2,1)} %w_hbm.1, ...), custom_call_target="tpu_custom_call" | custom-call | tf_op jit(solution)/shard_map/first_push/pallas_call | solution.py:270
  4.4 19.0 %all_to_all.70.z_ref = bf16[32,72,128]{2,1,0:T(8,128)(2,1)S(1)} all-to-all(bf16[32,72,128]{2,1,0:T(8,128)(2,1)S(1)} %get-tuple-element.31), channel_id=1, replica_groups=mesh['tiles'=32,'reps'=4] {'tiles'}, dimensions={0} | all-to-all | bytes 1179648 | tf_op jit(solution)/shard_map/all_to_all | solution.py:303
  23.4 0.0 copy-done.2
  23.4 0.0 copy-done.7
  23.4 0.0 copy-done.6
  23.4 0.0 copy-done.5
  23.4 0.5 first_firm.1
  23.9 15.0 %all_to_all.71.refs_4_ = bf16[32,64,128]{2,1,0:T(8,128)(2,1)S(1)} all-to-all(bf16[32,64,128]{2,1,0:T(8,128)(2,1)S(1)} %get-tuple-element.32), channel_id=1, replica_groups=mesh['tiles'=32,'reps'=4] {'tiles'}, dimensions={0} | all-to-all | bytes 1048576 | tf_op jit(solution)/shard_map/all_to_all | solution.py:303
  39.0 0.0 copy-done.4
  39.0 0.0 copy-done.3
  39.0 3.5 %sweep.4 = bf16[32,64,128]{2,1,0:T(8,128)(2,1)S(1)} custom-call(s32[128]{0:T(128)S(1)} %copy-done.3, s32[128]{0:T(128)S(1)} %copy-done.4, bf16[128,128,128]{2,1,0:T(8,128)(2,1)S(1)} %get-tuple-element.28.refs_2_, bf16[128,128,128]{2,1,0:T(8,128)(2,1)S(1)} %get-tuple-element.29.refs_3_, bf16[32,64,128]{2,1,0:T(8,128)(2,1)S(1)} %all_to_all.71.refs_4_, ...), custom_call_target="tpu_custom_call" | custom-call | tf_op jit(solution)/shard_map/sweep/pallas_call | solution.py:270
  42.5 15.0 %all_to_all.72.refs_0_ = bf16[32,64,128]{2,1,0:T(8,128)(2,1)S(1)} all-to-all(bf16[32,64,128]{2,1,0:T(8,128)(2,1)S(1)} %sweep.4), channel_id=1, replica_groups=mesh['tiles'=32,'reps'=4] {'tiles'}, dimensions={0} | all-to-all | bytes 1048576 | tf_op jit(solution)/shard_map/all_to_all | solution.py:303
  57.5 0.3 firm.4
  57.8 15.0 %all_to_all.73.refs_4_ = bf16[32,64,128]{2,1,0:T(8,128)(2,1)S(1)} all-to-all(bf16[32,64,128]{2,1,0:T(8,128)(2,1)S(1)} %get-tuple-element.38), channel_id=1, replica_groups=mesh['tiles'=32,'reps'=4] {'tiles'}, dimensions={0} | all-to-all | bytes 1048576 | tf_op jit(solution)/shard_map/all_to_all | solution.py:303
  72.8 3.5 %sweep.5 = bf16[32,64,128]{2,1,0:T(8,128)(2,1)S(1)} custom-call(s32[128]{0:T(128)S(1)} %copy-done.3, s32[128]{0:T(128)S(1)} %copy-done.4, bf16[128,128,128]{2,1,0:T(8,128)(2,1)S(1)} %get-tuple-element.28.refs_2_, bf16[128,128,128]{2,1,0:T(8,128)(2,1)S(1)} %get-tuple-element.29.refs_3_, bf16[32,64,128]{2,1,0:T(8,128)(2,1)S(1)} %all_to_all.73.refs_4_, ...), custom_call_target="tpu_custom_call" | custom-call | tf_op jit(solution)/shard_map/sweep/pallas_call | solution.py:270
  76.4 15.0 %all_to_all.74.refs_0_ = bf16[32,64,128]{2,1,0:T(8,128)(2,1)S(1)} all-to-all(bf16[32,64,128]{2,1,0:T(8,128)(2,1)S(1)} %sweep.5), channel_id=1, replica_groups=mesh['tiles'=32,'reps'=4] {'tiles'}, dimensions={0} | all-to-all | bytes 1048576 | tf_op jit(solution)/shard_map/all_to_all | solution.py:303
  91.4 0.3 firm.5
  91.7 15.0 %all_to_all.75.refs_4_ = bf16[32,64,128]{2,1,0:T(8,128)(2,1)S(1)} all-to-all(bf16[32,64,128]{2,1,0:T(8,128)(2,1)S(1)} %get-tuple-element.40), channel_id=1, replica_groups=mesh['tiles'=32,'reps'=4] {'tiles'}, dimensions={0} | all-to-all | bytes 1048576 | tf_op jit(solution)/shard_map/all_to_all | solution.py:303
  106.7 3.5 %sweep.6 = bf16[32,64,128]{2,1,0:T(8,128)(2,1)S(1)} custom-call(s32[128]{0:T(128)S(1)} %copy-done.3, s32[128]{0:T(128)S(1)} %copy-done.4, bf16[128,128,128]{2,1,0:T(8,128)(2,1)S(1)} %get-tuple-element.28.refs_2_, bf16[128,128,128]{2,1,0:T(8,128)(2,1)S(1)} %get-tuple-element.29.refs_3_, bf16[32,64,128]{2,1,0:T(8,128)(2,1)S(1)} %all_to_all.75.refs_4_, ...), custom_call_target="tpu_custom_call" | custom-call | tf_op jit(solution)/shard_map/sweep/pallas_call | solution.py:270
  110.2 15.0 %all_to_all.76.refs_0_ = bf16[32,64,128]{2,1,0:T(8,128)(2,1)S(1)} all-to-all(bf16[32,64,128]{2,1,0:T(8,128)(2,1)S(1)} %sweep.6), channel_id=1, replica_groups=mesh['tiles'=32,'reps'=4] {'tiles'}, dimensions={0} | all-to-all | bytes 1048576 | tf_op jit(solution)/shard_map/all_to_all | solution.py:303
  125.3 0.3 firm.6
  125.6 15.0 %all_to_all.77.refs_4_ = bf16[32,64,128]{2,1,0:T(8,128)(2,1)S(1)} all-to-all(bf16[32,64,128]{2,1,0:T(8,128)(2,1)S(1)} %get-tuple-element.42), channel_id=1, replica_groups=mesh['tiles'=32,'reps'=4] {'tiles'}, dimensions={0} | all-to-all | bytes 1048576 | tf_op jit(solution)/shard_map/all_to_all | solution.py:303
  140.6 3.5 %sweep.7 = bf16[32,64,128]{2,1,0:T(8,128)(2,1)S(1)} custom-call(s32[128]{0:T(128)S(1)} %copy-done.3, s32[128]{0:T(128)S(1)} %copy-done.4, bf16[128,128,128]{2,1,0:T(8,128)(2,1)S(1)} %get-tuple-element.28.refs_2_, bf16[128,128,128]{2,1,0:T(8,128)(2,1)S(1)} %get-tuple-element.29.refs_3_, bf16[32,64,128]{2,1,0:T(8,128)(2,1)S(1)} %all_to_all.77.refs_4_, ...), custom_call_target="tpu_custom_call" | custom-call | tf_op jit(solution)/shard_map/sweep/pallas_call | solution.py:270
  144.1 15.0 %all_to_all.78.refs_0_ = bf16[32,64,128]{2,1,0:T(8,128)(2,1)S(1)} all-to-all(bf16[32,64,128]{2,1,0:T(8,128)(2,1)S(1)} %sweep.7), channel_id=1, replica_groups=mesh['tiles'=32,'reps'=4] {'tiles'}, dimensions={0} | all-to-all | bytes 1048576 | tf_op jit(solution)/shard_map/all_to_all | solution.py:303
  159.1 0.3 firm.7
  159.4 15.0 %all_to_all.79.refs_4_ = bf16[32,64,128]{2,1,0:T(8,128)(2,1)S(1)} all-to-all(bf16[32,64,128]{2,1,0:T(8,128)(2,1)S(1)} %firm.7), channel_id=1, replica_groups=mesh['tiles'=32,'reps'=4] {'tiles'}, dimensions={0} | all-to-all | bytes 1048576 | tf_op jit(solution)/shard_map/all_to_all | solution.py:303
  174.4 0.0 copy-start
  174.4 0.0 copy-start.1
  174.4 3.6 %sweep_close.1 = (bf16[32,64,128]{2,1,0:T(8,128)(2,1)S(1)}, f32[64,2048]{1,0:T(8,128)}) custom-call(s32[128]{0:T(128)S(1)} %copy-done.3, s32[128]{0:T(128)S(1)} %copy-done.4, bf16[128,128,128]{2,1,0:T(8,128)(2,1)S(1)} %get-tuple-element.28.refs_2_, bf16[128,128,128]{2,1,0:T(8,128)(2,1)S(1)} %get-tuple-element.29.refs_3_, ...), custom_call_target="tpu_custom_call" | custom-call | tf_op jit(solution)/shard_map/sweep_close/pallas_call | solution.py:270
  178.0 15.0 %all_to_all.80.refs_0_ = bf16[32,64,128]{2,1,0:T(8,128)(2,1)S(1)} all-to-all(bf16[32,64,128]{2,1,0:T(8,128)(2,1)S(1)} %get-tuple-element.45), channel_id=1, replica_groups=mesh['tiles'=32,'reps'=4] {'tiles'}, dimensions={0} | all-to-all | bytes 1048576 | tf_op jit(solution)/shard_map/all_to_all | solution.py:303
  193.0 0.0 copy-done
  193.0 0.0 copy-done.1
  193.0 1.4 close_firm.1
  194.4 11.8 %all_to_all.81.part_ref = f32[32,8,128]{2,1,0:T(8,128)S(1)} all-to-all(f32[32,8,128]{2,1,0:T(8,128)S(1)} %bitcast.10), channel_id=1, replica_groups=mesh['tiles'=32,'reps'=4] {'tiles'}, dimensions={0} | all-to-all | bytes 262144 | tf_op jit(solution)/shard_map/all_to_all | solution.py:303
  206.2 11.2 %all_to_all.82 = f32[32,8,128]{2,1,0:T(8,128)S(1)} all-to-all(f32[32,8,128]{2,1,0:T(8,128)S(1)} %total.1), channel_id=1, replica_groups=mesh['tiles'=32,'reps'=4] {'tiles'}, dimensions={0} | all-to-all | bytes 262144 | tf_op jit(solution)/shard_map/all_to_all | solution.py:303
  217.4 0.8 moment.1
  218.2 11.1 %all_to_all.83 = f32[4,16,512]{2,1,0:T(8,128)S(1)} all-to-all(f32[4,16,512]{2,1,0:T(8,128)S(1)} %get-tuple-element.51), channel_id=1, replica_groups=mesh['tiles'=32,'reps'=4] {'reps'}, dimensions={0} | all-to-all | bytes 262144 | tf_op jit(solution)/shard_map/all_to_all | solution.py:303
  229.3 0.6 broadcast_multiply_fusion
  (2 shorter events, 0.1 us)
Async XLA Ops:
  0.6 38.3 %copy-start.4 = (s32[128]{0:T(128)S(1)}, s32[128]{0:T(128)}, u32[]{:S(2)}) copy-start(s32[128]{0:T(128)} %refs_1_.9) | copy-start | bytes 1540
  0.6 38.3 %copy-start.3 = (s32[128]{0:T(128)S(1)}, s32[128]{0:T(128)}, u32[]{:S(2)}) copy-start(s32[128]{0:T(128)} %refs_0_.9) | copy-start | bytes 1540
  0.7 22.7 %copy-start.2 = (s32[64,256]{1,0:T(8,128)S(1)}, s32[64,256]{1,0:T(8,128)}, u32[]{:S(2)}) copy-start(s32[64,256]{1,0:T(8,128)} %signs_ref.1) | copy-start | bytes 196612
  0.7 22.7 %copy-start.7 = (s32[256]{0:T(256)S(1)}, s32[256]{0:T(256)}, u32[]{:S(2)}) copy-start(s32[256]{0:T(256)} %param.22) | copy-start | bytes 3076
  0.7 22.7 %copy-start.6 = (f32[256]{0:T(256)S(1)}, f32[256]{0:T(256)}, u32[]{:S(2)}) copy-start(f32[256]{0:T(256)} %param.21) | copy-start | bytes 3076
  0.7 22.7 %copy-start.5 = (f32[256]{0:T(256)S(1)}, f32[256]{0:T(256)}, u32[]{:S(2)}) copy-start(f32[256]{0:T(256)} %param.20) | copy-start | bytes 3076
  174.4 18.6 %copy-start = (f32[512,512]{1,0:T(8,128)S(1)}, f32[512,512]{1,0:T(8,128)}, u32[]{:S(2)}) copy-start(f32[512,512]{1,0:T(8,128)} %refs_6_.1) | copy-start | bytes 3145732
  174.4 18.6 %copy-start.1 = (f32[256,512]{1,0:T(8,128)S(1)}, f32[256,512]{1,0:T(8,128)}, u32[]{:S(2)}) copy-start(f32[256,512]{1,0:T(8,128)} %refs_5_.1) | copy-start | bytes 1572868

commit v5 on v4

--- a/solution.py
+++ b/solution.py
@@ -21,6 +21,7 @@
 VMEM = pl.BlockSpec(memory_space=pltpu.VMEM)
 SMEM = pl.BlockSpec(memory_space=pltpu.SMEM)
 HBM = pl.BlockSpec(memory_space=pltpu.HBM)
+ANY = pl.BlockSpec(memory_space=pl.ANY)
 PARAMS = pltpu.CompilerParams(vmem_limit_bytes=20 << 20)
 
 
@@ -121,21 +122,28 @@
 
 
 def sweep_kernel(last, *refs):
+    (tw_any, to_any, w_ref, turned_ref, f_ref, wo_ref, inv_ref), (z_ref, *refs) = refs[:7], refs[7:]
     if last:
-        tw, to, w_ref, turned_ref, f_ref, wo_ref, inv_ref, z_ref, out_hbm, accw_ref, x_ref, accz_ref, out_ref, sem = refs
-    else:
-        tw, to, w_ref, turned_ref, f_ref, wo_ref, inv_ref, z_ref, accw_ref, x_ref, accz_ref = refs
+        out_hbm, *refs = refs
+    accw_ref, x_ref, accz_ref, tw, to, sems, *refs = refs
+    tables = [pltpu.make_async_copy(tw_any, tw, sems.at[0]), pltpu.make_async_copy(to_any, to, sems.at[1])]
+    for table in tables:
+        table.start()
     tiles = w_ref.shape[0]
     accw_ref[...] = jnp.zeros_like(accw_ref)
     accz_ref[...] = jnp.zeros_like(accz_ref)
+    for table in tables:
+        table.wait()
     add_tiles(0, tiles, to, tw, turned_ref, f_ref, accw_ref)
+    if last:
+        (out_ref,) = refs
     for b in range(WORK_BLOCKS):
         worker = wo_ref[b] - accw_ref[b] * inv_ref[b, :1]
         if last:
             out_ref[:, b * CELLS : (b + 1) * CELLS] = worker
         x_ref[b] = worker.astype(BF16)
     if last:
-        copy = pltpu.make_async_copy(out_ref, out_hbm, sem)
+        copy = pltpu.make_async_copy(out_ref, out_hbm, sems.at[2])
         copy.start()
     add_tiles(0, tiles, tw, to, w_ref, x_ref, accz_ref)
     z_ref[...] = accz_ref[...].astype(BF16)
@@ -227,11 +235,11 @@
     scatter_firms(firms, flags_ref, send_ref)
 
 
-def close_firm_kernel(omega, z_ref, fo_ref, inv_ref, flags_ref, older_ref, cov_ref, white_ref, firm_ref, part_ref):
+def close_firm_kernel(omega, z_ref, fo_ref, inv_ref, flags_ref, older_ref, cov_ref, white_ref, now_ref, part_ref):
     firms = next_firms(omega, z_ref, fo_ref, inv_ref, flags_ref, older_ref)
     for j in range(FIRM_BLOCKS):
-        firm_ref[:, j * CELLS : (j + 1) * CELLS] = firms[j]
-    projected = product(firm_ref[...], cov_ref[...], ((1,), (0,)))
+        now_ref[j] = firms[j]
+    projected = product(jnp.concatenate(firms, axis=1), cov_ref[...], ((1,), (0,)))
     whitened = product(projected, white_ref[...], ((1,), (1,)))
     reps = whitened.shape[0]
     columns = whitened.shape[1] // CELLS
@@ -245,21 +253,26 @@
         out_ref[s] = total
 
 
-def moment_kernel(share, all_ref, coef_ref, moment_ref, rows_ref):
-    reps, covars = coef_ref.shape
+def moment_kernel(share, all_ref, moment_ref, rows_ref):
+    share_rows, covars = moment_ref.shape
     columns = covars // CELLS
-    share_rows = moment_ref.shape[1]
+    reps = all_ref.shape[0] // columns
     in_block = CELLS // share_rows
     own = all_ref[pl.ds(share[0] // in_block, reps, stride=columns)]
     for c in range(columns):
         other = all_ref[pl.ds(c, reps, stride=columns)]
-        coef_ref[:, c * CELLS : (c + 1) * CELLS] = other
-        rows_ref[:, c * CELLS : (c + 1) * CELLS] = lax.dot_general(
-            own, other, (((0,), (0,)), ((), ())), precision=HIGHEST, preferred_element_type=F32
-        )
+        rows_ref[:, c * CELLS : (c + 1) * CELLS] = product(own, other, ((0,), (0,)))
     start = pl.multiple_of((share[0] % in_block) * share_rows, share_rows)
-    for g in range(moment_ref.shape[0]):
-        moment_ref[g] = rows_ref[pl.ds(start, share_rows)]
+    moment_ref[...] = rows_ref[pl.ds(start, share_rows)]
+
+
+def emit_kernel(all_ref, now_ref, coef_ref, firm_ref):
+    reps, covars = coef_ref.shape
+    columns = covars // CELLS
+    for c in range(columns):
+        coef_ref[:, c * CELLS : (c + 1) * CELLS] = all_ref[pl.ds(c, reps, stride=columns)]
+    for j in range(FIRM_BLOCKS):
+        firm_ref[:, j * CELLS : (j + 1) * CELLS] = now_ref[j]
 
 
 def keep(value):
@@ -344,6 +357,7 @@
     )
     older = None
     scratch = (work_shape, ((WORK_BLOCKS, reps, CELLS), BF16), ((owners, reps, CELLS), F32))
+    scratch += (pltpu.SMEM((tiles,), jnp.int32), pltpu.SMEM((tiles,), jnp.int32), pltpu.SemaphoreType.DMA((3,)))
     for k in range(1, SWEEPS):
         last = k == SWEEPS - 1
         f = exchange(send)
@@ -351,14 +365,14 @@
         if last:
             whole = ((reps, WORK_BLOCKS * CELLS), F32)
             outputs += (whole,)
-            more = (whole, pltpu.SemaphoreType.DMA)
+            more = (whole,)
             out_specs.append(HBM)
         z, *rest = call(
             lambda *refs, e=last: sweep_kernel(e, *refs),
             (tile_worker, tile_owner, keep(held), keep(turned), f, worker_outcome, worker_inverse),
             outputs,
             scratch + more,
-            scalars=2,
+            specs=[ANY] * 2 + [VMEM] * 5,
             out_specs=out_specs,
             name="sweep_close" if last else "sweep",
         )
@@ -373,25 +387,31 @@
             )
             older, newer = newer, now[0] if now else None
         else:
-            firm_effect, part = call(
+            firms, part = call(
                 lambda *refs, w=omegas[k]: close_firm_kernel(w, *refs),
                 inputs + (covariates, whitening),
-                (((reps, FIRM_BLOCKS * CELLS), F32), ((reps * covars // CELLS, CELLS), F32)),
+                (firm_shape, ((reps * covars // CELLS, CELLS), F32)),
                 name="close_firm",
             )
     part = exchange(part.reshape(owners, -1, CELLS))
     (spread,) = call(total_kernel, (part,), ((part.shape, F32),), name="total")
-    everything = exchange(spread)
-    coefficients, moments = call(
+    everything = exchange(spread).reshape(-1, CELLS)
+    (moment,) = call(
         moment_kernel,
-        (share, everything.reshape(-1, CELLS)),
-        (((reps, covars), F32), ((groups, covars // owners, covars), F32)),
+        (share, everything),
+        (((covars // owners, covars), F32),),
         (((CELLS, covars), F32),),
         scalars=1,
         name="moment",
     )
-    moments = exchange(moments, "reps")
-    covariance = jnp.sum(moments, axis=0) / (reps * groups)
+    coefficients, firm_effect = call(
+        emit_kernel,
+        (everything, firms),
+        (((reps, covars), F32), ((reps, FIRM_BLOCKS * CELLS), F32)),
+        name="emit",
+    )
+    shifted = [lax.ppermute(moment, "reps", [(g, (g + d) % groups) for g in range(groups)]) for d in range(1, groups)]
+    covariance = ((moment + shifted[1]) + (shifted[0] + shifted[2])) / (reps * groups)
     return (rest[0], firm_effect, coefficients, covariance)
 
 

time: 231 us -> 228 us (0.987)
  blocking collectives: 203 us -> 192 us
  starting transfers between devices: 0 us -> 5.97 us
  waiting for transfers between devices: 0 us -> 2.92 us
    all_to_all x14 -> x13, blocking collectives: 203 us -> 192 us  [exchange(): return lax.all_to_all(values, axes, 0, 0, tiled=True)]
    ppermute x0 -> x3, starting transfers between devices: none -> 5.97 us  [body(): lax.ppermute(moment, 'reps', [(g, (g + d) % groups) for g in range(groups)])]
    ppermute x0 -> x3, waiting for transfers between devices: none -> 2.92 us  [body(): lax.ppermute(moment, 'reps', [(g, (g + d) % groups) for g in range(groups)])]
    pallas_call x14 -> x15, Pallas kernels: 25.2 us -> 24.8 us  [call(): pl.pallas_call(kernel, in_specs=specs or [SMEM] * scalars + [VMEM] * (len...]
  transfers between devices with their start and end apart: 0 -> 3, of which waited for: 0 -> 1; matrix products, arithmetic and copies ran while one was open for 0% -> 0% of each run, Pallas kernels for 0% -> 0%
where the time goes in v5:
time: 228 us; the launch traced here: 227 us
  blocking collectives  192 us (84%)
  Pallas kernels  24.8 us (11%)
  starting transfers between devices  5.97 us (3%)
  waiting for transfers between devices  2.92 us (1%)
    all_to_all x13, blocking collectives, exchange(): return lax.all_to_all(values, axes, 0, 0, tiled=True)  192 us
    pallas_call x15, Pallas kernels, call(): pl.pallas_call(kernel, in_specs=specs or [SMEM] * scalars + [VMEM] * (len...  24.8 us
    ppermute x3, starting transfers between devices, body(): lax.ppermute(moment, 'reps', [(g, (g + d) % groups) for g in range(groups)])  5.97 us
  transfers between devices with their start and end apart: 3, of which 1 were waited for; matrix products, arithmetic and copies ran while one was open for 0% of the time, Pallas kernels for 0%

profile of v5, /device:TPU:0, one launch (start us, length us, event | category | flops | bytes accessed | tf_op | source)
XLA Modules:
  0.0 227.3 jit_solution(2106004818516586844)
XLA Ops:
  0.6 0.0 copy-start.4
  0.6 0.0 copy-start.3
  0.7 0.0 copy-start.2
  0.7 0.0 copy-start.7
  0.7 0.0 copy-start.6
  0.7 0.0 copy-start.5
  0.7 3.7 %first_push.1 = (bf16[32,72,128]{2,1,0:T(8,128)(2,1)S(1)}, f32[16,64,128]{2,1,0:T(8,128)S(1)}, bf16[128,128,128]{2,1,0:T(8,128)(2,1)S(1)}, bf16[128,128,128]{2,1,0:T(8,128)(2,1)S(1)}, f32[16,8,128]{2,1,0:T(8,128)S(1)}) custom-call(s32[128]{0:T(128)} %refs_0_.9, s32[128]{0:T(128)} %refs_1_.9, s32[1,32]{1,0:T(1,128)} %ob_hbm.1, bf16[128,128,128]{2,1,0:T(8,128)(2,1)} %w_hbm.1, ...), custom_call_target="tpu_custom_call" | custom-call | tf_op jit(solution)/shard_map/first_push/pallas_call | solution.py:283
  4.4 19.0 %all_to_all.65.z_ref = bf16[32,72,128]{2,1,0:T(8,128)(2,1)S(1)} all-to-all(bf16[32,72,128]{2,1,0:T(8,128)(2,1)S(1)} %get-tuple-element.31), channel_id=1, replica_groups=mesh['tiles'=32,'reps'=4] {'tiles'}, dimensions={0} | all-to-all | bytes 1179648 | tf_op jit(solution)/shard_map/all_to_all | solution.py:316
  23.4 0.0 copy-done.2
  23.4 0.0 copy-done.7
  23.4 0.0 copy-done.6
  23.4 0.0 copy-done.5
  23.4 0.5 first_firm.1
  23.9 15.0 %all_to_all.66.refs_4_ = bf16[32,64,128]{2,1,0:T(8,128)(2,1)S(1)} all-to-all(bf16[32,64,128]{2,1,0:T(8,128)(2,1)S(1)} %get-tuple-element.32), channel_id=1, replica_groups=mesh['tiles'=32,'reps'=4] {'tiles'}, dimensions={0} | all-to-all | bytes 1048576 | tf_op jit(solution)/shard_map/all_to_all | solution.py:316
  39.0 0.0 copy-done.4
  39.0 0.0 copy-done.3
  39.0 3.5 %sweep.4 = bf16[32,64,128]{2,1,0:T(8,128)(2,1)S(1)} custom-call(s32[128]{0:T(128)S(1)} %copy-done.3, s32[128]{0:T(128)S(1)} %copy-done.4, bf16[128,128,128]{2,1,0:T(8,128)(2,1)S(1)} %get-tuple-element.28.refs_2_, bf16[128,128,128]{2,1,0:T(8,128)(2,1)S(1)} %get-tuple-element.29.refs_3_, bf16[32,64,128]{2,1,0:T(8,128)(2,1)S(1)} %all_to_all.66.refs_4_, ...), custom_call_target="tpu_custom_call" | custom-call | tf_op jit(solution)/shard_map/sweep/pallas_call | solution.py:283
  42.4 15.0 %all_to_all.67.refs_0_ = bf16[32,64,128]{2,1,0:T(8,128)(2,1)S(1)} all-to-all(bf16[32,64,128]{2,1,0:T(8,128)(2,1)S(1)} %sweep.4), channel_id=1, replica_groups=mesh['tiles'=32,'reps'=4] {'tiles'}, dimensions={0} | all-to-all | bytes 1048576 | tf_op jit(solution)/shard_map/all_to_all | solution.py:316
  57.5 0.3 firm.4
  57.8 15.0 %all_to_all.68.refs_4_ = bf16[32,64,128]{2,1,0:T(8,128)(2,1)S(1)} all-to-all(bf16[32,64,128]{2,1,0:T(8,128)(2,1)S(1)} %get-tuple-element.38), channel_id=1, replica_groups=mesh['tiles'=32,'reps'=4] {'tiles'}, dimensions={0} | all-to-all | bytes 1048576 | tf_op jit(solution)/shard_map/all_to_all | solution.py:316
  72.8 3.5 %sweep.5 = bf16[32,64,128]{2,1,0:T(8,128)(2,1)S(1)} custom-call(s32[128]{0:T(128)S(1)} %copy-done.3, s32[128]{0:T(128)S(1)} %copy-done.4, bf16[128,128,128]{2,1,0:T(8,128)(2,1)S(1)} %get-tuple-element.28.refs_2_, bf16[128,128,128]{2,1,0:T(8,128)(2,1)S(1)} %get-tuple-element.29.refs_3_, bf16[32,64,128]{2,1,0:T(8,128)(2,1)S(1)} %all_to_all.68.refs_4_, ...), custom_call_target="tpu_custom_call" | custom-call | tf_op jit(solution)/shard_map/sweep/pallas_call | solution.py:283
  76.2 15.0 %all_to_all.69.refs_0_ = bf16[32,64,128]{2,1,0:T(8,128)(2,1)S(1)} all-to-all(bf16[32,64,128]{2,1,0:T(8,128)(2,1)S(1)} %sweep.5), channel_id=1, replica_groups=mesh['tiles'=32,'reps'=4] {'tiles'}, dimensions={0} | all-to-all | bytes 1048576 | tf_op jit(solution)/shard_map/all_to_all | solution.py:316
  91.3 0.3 firm.5
  91.6 15.0 %all_to_all.70.refs_4_ = bf16[32,64,128]{2,1,0:T(8,128)(2,1)S(1)} all-to-all(bf16[32,64,128]{2,1,0:T(8,128)(2,1)S(1)} %get-tuple-element.40), channel_id=1, replica_groups=mesh['tiles'=32,'reps'=4] {'tiles'}, dimensions={0} | all-to-all | bytes 1048576 | tf_op jit(solution)/shard_map/all_to_all | solution.py:316
  106.6 3.5 %sweep.6 = bf16[32,64,128]{2,1,0:T(8,128)(2,1)S(1)} custom-call(s32[128]{0:T(128)S(1)} %copy-done.3, s32[128]{0:T(128)S(1)} %copy-done.4, bf16[128,128,128]{2,1,0:T(8,128)(2,1)S(1)} %get-tuple-element.28.refs_2_, bf16[128,128,128]{2,1,0:T(8,128)(2,1)S(1)} %get-tuple-element.29.refs_3_, bf16[32,64,128]{2,1,0:T(8,128)(2,1)S(1)} %all_to_all.70.refs_4_, ...), custom_call_target="tpu_custom_call" | custom-call | tf_op jit(solution)/shard_map/sweep/pallas_call | solution.py:283
  110.0 15.0 %all_to_all.71.refs_0_ = bf16[32,64,128]{2,1,0:T(8,128)(2,1)S(1)} all-to-all(bf16[32,64,128]{2,1,0:T(8,128)(2,1)S(1)} %sweep.6), channel_id=1, replica_groups=mesh['tiles'=32,'reps'=4] {'tiles'}, dimensions={0} | all-to-all | bytes 1048576 | tf_op jit(solution)/shard_map/all_to_all | solution.py:316
  125.1 0.3 firm.6
  125.4 15.0 %all_to_all.72.refs_4_ = bf16[32,64,128]{2,1,0:T(8,128)(2,1)S(1)} all-to-all(bf16[32,64,128]{2,1,0:T(8,128)(2,1)S(1)} %get-tuple-element.42), channel_id=1, replica_groups=mesh['tiles'=32,'reps'=4] {'tiles'}, dimensions={0} | all-to-all | bytes 1048576 | tf_op jit(solution)/shard_map/all_to_all | solution.py:316
  140.4 3.5 %sweep.7 = bf16[32,64,128]{2,1,0:T(8,128)(2,1)S(1)} custom-call(s32[128]{0:T(128)S(1)} %copy-done.3, s32[128]{0:T(128)S(1)} %copy-done.4, bf16[128,128,128]{2,1,0:T(8,128)(2,1)S(1)} %get-tuple-element.28.refs_2_, bf16[128,128,128]{2,1,0:T(8,128)(2,1)S(1)} %get-tuple-element.29.refs_3_, bf16[32,64,128]{2,1,0:T(8,128)(2,1)S(1)} %all_to_all.72.refs_4_, ...), custom_call_target="tpu_custom_call" | custom-call | tf_op jit(solution)/shard_map/sweep/pallas_call | solution.py:283
  143.8 15.0 %all_to_all.73.refs_0_ = bf16[32,64,128]{2,1,0:T(8,128)(2,1)S(1)} all-to-all(bf16[32,64,128]{2,1,0:T(8,128)(2,1)S(1)} %sweep.7), channel_id=1, replica_groups=mesh['tiles'=32,'reps'=4] {'tiles'}, dimensions={0} | all-to-all | bytes 1048576 | tf_op jit(solution)/shard_map/all_to_all | solution.py:316
  158.9 0.3 firm.7
  159.2 15.0 %all_to_all.74.refs_4_ = bf16[32,64,128]{2,1,0:T(8,128)(2,1)S(1)} all-to-all(bf16[32,64,128]{2,1,0:T(8,128)(2,1)S(1)} %firm.7), channel_id=1, replica_groups=mesh['tiles'=32,'reps'=4] {'tiles'}, dimensions={0} | all-to-all | bytes 1048576 | tf_op jit(solution)/shard_map/all_to_all | solution.py:316
  174.2 0.0 copy-start
  174.2 0.0 copy-start.1
  174.2 3.5 %sweep_close.1 = (bf16[32,64,128]{2,1,0:T(8,128)(2,1)S(1)}, f32[64,2048]{1,0:T(8,128)}) custom-call(s32[128]{0:T(128)S(1)} %copy-done.3, s32[128]{0:T(128)S(1)} %copy-done.4, bf16[128,128,128]{2,1,0:T(8,128)(2,1)S(1)} %get-tuple-element.28.refs_2_, bf16[128,128,128]{2,1,0:T(8,128)(2,1)S(1)} %get-tuple-element.29.refs_3_, ...), custom_call_target="tpu_custom_call" | custom-call | tf_op jit(solution)/shard_map/sweep_close/pallas_call | solution.py:283
  177.7 15.0 %all_to_all.75.refs_0_ = bf16[32,64,128]{2,1,0:T(8,128)(2,1)S(1)} all-to-all(bf16[32,64,128]{2,1,0:T(8,128)(2,1)S(1)} %get-tuple-element.45), channel_id=1, replica_groups=mesh['tiles'=32,'reps'=4] {'tiles'}, dimensions={0} | all-to-all | bytes 1048576 | tf_op jit(solution)/shard_map/all_to_all | solution.py:316
  192.7 0.0 copy-done
  192.7 0.0 copy-done.1
  192.7 1.0 close_firm.1
  193.7 11.8 %all_to_all.76.part_ref = f32[32,8,128]{2,1,0:T(8,128)S(1)} all-to-all(f32[32,8,128]{2,1,0:T(8,128)S(1)} %bitcast.11), channel_id=1, replica_groups=mesh['tiles'=32,'reps'=4] {'tiles'}, dimensions={0} | all-to-all | bytes 262144 | tf_op jit(solution)/shard_map/all_to_all | solution.py:316
  205.5 11.2 %all_to_all.77 = f32[32,8,128]{2,1,0:T(8,128)S(1)} all-to-all(f32[32,8,128]{2,1,0:T(8,128)S(1)} %total.1), channel_id=1, replica_groups=mesh['tiles'=32,'reps'=4] {'tiles'}, dimensions={0} | all-to-all | bytes 262144 | tf_op jit(solution)/shard_map/all_to_all | solution.py:316
  216.8 0.3 moment.1
  217.1 4.1 %collective-permute-start.2 = (f32[16,512]{1,0:T(8,128)S(1)}, f32[16,512]{1,0:T(8,128)S(1)}, u32[]{:S(2)}, u32[]{:S(2)}) collective-permute-start(f32[16,512]{1,0:T(8,128)S(1)} %moment.1), channel_id=1, source_target_pairs={{0,3},{1,0},{2,1},{3,2},{4,7},{5,4},{6,5},{7,6},{8,11},{9,8},{10,9... | collective-permute-start | bytes 98312 | tf_op jit(solution)/shard_map/ppermute | solution.py:413
  221.2 0.0 collective-permute-start.1
  221.2 1.9 collective-permute-start
  223.1 0.7 emit.1
  223.7 0.0 collective-permute-done.2
  223.7 2.9 %collective-permute-done.1 = f32[16,512]{1,0:T(8,128)S(1)} collective-permute-done((f32[16,512]{1,0:T(8,128)S(1)}, f32[16,512]{1,0:T(8,128)S(1)}, u32[]{:S(2)}, u32[]{:S(2)}) %collective-permute-start.1) | collective-permute-done | bytes 32800 | tf_op jit(solution)/shard_map/ppermute | solution.py:413
  226.7 0.0 collective-permute-done
  226.7 0.6 add_multiply_fusion
  (1 shorter events, 0.0 us)
Async XLA Ops:
  0.6 38.3 %copy-start.4 = (s32[128]{0:T(128)S(1)}, s32[128]{0:T(128)}, u32[]{:S(2)}) copy-start(s32[128]{0:T(128)} %refs_1_.9) | copy-start | bytes 1540
  0.6 38.3 %copy-start.3 = (s32[128]{0:T(128)S(1)}, s32[128]{0:T(128)}, u32[]{:S(2)}) copy-start(s32[128]{0:T(128)} %refs_0_.9) | copy-start | bytes 1540
  0.7 22.7 %copy-start.2 = (s32[64,256]{1,0:T(8,128)S(1)}, s32[64,256]{1,0:T(8,128)}, u32[]{:S(2)}) copy-start(s32[64,256]{1,0:T(8,128)} %signs_ref.1) | copy-start | bytes 196612
  0.7 22.7 %copy-start.7 = (s32[256]{0:T(256)S(1)}, s32[256]{0:T(256)}, u32[]{:S(2)}) copy-start(s32[256]{0:T(256)} %param.22) | copy-start | bytes 3076
  0.7 22.7 %copy-start.6 = (f32[256]{0:T(256)S(1)}, f32[256]{0:T(256)}, u32[]{:S(2)}) copy-start(f32[256]{0:T(256)} %param.21) | copy-start | bytes 3076
  0.7 22.7 %copy-start.5 = (f32[256]{0:T(256)S(1)}, f32[256]{0:T(256)}, u32[]{:S(2)}) copy-start(f32[256]{0:T(256)} %param.20) | copy-start | bytes 3076
  174.2 18.5 %copy-start = (f32[512,512]{1,0:T(8,128)S(1)}, f32[512,512]{1,0:T(8,128)}, u32[]{:S(2)}) copy-start(f32[512,512]{1,0:T(8,128)} %refs_6_.1) | copy-start | bytes 3145732
  174.2 18.5 %copy-start.1 = (f32[256,512]{1,0:T(8,128)S(1)}, f32[256,512]{1,0:T(8,128)}, u32[]{:S(2)}) copy-start(f32[256,512]{1,0:T(8,128)} %refs_5_.1) | copy-start | bytes 1572868
  217.1 6.7 %collective-permute-start.2 = (f32[16,512]{1,0:T(8,128)S(1)}, f32[16,512]{1,0:T(8,128)S(1)}, u32[]{:S(2)}, u32[]{:S(2)}) collective-permute-start(f32[16,512]{1,0:T(8,128)S(1)} %moment.1), channel_id=1, source_target_pairs={{0,3},{1,0},{2,1},{3,2},{4,7},{5,4},{6,5},{7,6},{8,11},{9,8},{10,9... | collective-permute-start | bytes 98312 | tf_op jit(solution)/shard_map/ppermute | solution.py:413
  221.2 5.5 %collective-permute-start.1 = (f32[16,512]{1,0:T(8,128)S(1)}, f32[16,512]{1,0:T(8,128)S(1)}, u32[]{:S(2)}, u32[]{:S(2)}) collective-permute-start(f32[16,512]{1,0:T(8,128)S(1)} %moment.1), channel_id=1, source_target_pairs={{0,1},{1,2},{2,3},{3,0},{4,5},{5,6},{6,7},{7,4},{8,9},{9,10},{10,1... | collective-permute-start | bytes 98312 | tf_op jit(solution)/shard_map/ppermute | solution.py:413
  221.2 5.5 %collective-permute-start = (f32[16,512]{1,0:T(8,128)S(1)}, f32[16,512]{1,0:T(8,128)S(1)}, u32[]{:S(2)}, u32[]{:S(2)}) collective-permute-start(f32[16,512]{1,0:T(8,128)S(1)} %moment.1), channel_id=1, source_target_pairs={{0,2},{1,3},{2,0},{3,1},{4,6},{5,7},{6,4},{7,5},{8,10},{9,11},{10,... | collective-permute-start | bytes 98312 | tf_op jit(solution)/shard_map/ppermute | solution.py:413

commit v6 on v5

--- a/solution.py
+++ b/solution.py
@@ -50,18 +50,47 @@
     lax.fori_loop(0, count, body, 0, unroll=min(unroll, count))
 
 
-def add_tiles(first, count, source, target, w_ref, x_ref, acc_ref):
-    def step(i):
-        t = first + i
-        acc_ref[target[t]] += jnp.dot(x_ref[source[t]], w_ref[t], preferred_element_type=F32)
-
-    each_tile(count, step)
+def add_pairs(count, row, plan, w_ref, x_ref, acc_ref):
+    def step(p):
+        i = 2 * p
+        pair = jnp.concatenate([w_ref[plan[row, i]], w_ref[plan[row, i + 1]]], axis=1)
+        both = jnp.dot(x_ref[plan[row + 2, i]], pair, preferred_element_type=F32)
+        acc_ref[plan[row + 1, i]] += both[:, :CELLS]
+        acc_ref[plan[row + 1, i + 1]] += both[:, CELLS:]
+
+    each_tile(count, step, count)
+
+
+def pair_plan(source, target, spare, slots):
+    tiles = source.shape[1]
+    along = jnp.broadcast_to(source, (tiles, tiles))
+    down = along.T
+    targets = jnp.broadcast_to(target, (tiles, tiles)).T
+    row = lax.broadcasted_iota(jnp.int32, (tiles, tiles), 0)
+    column = lax.broadcasted_iota(jnp.int32, (tiles, tiles), 1)
+    same = along == down
+
+    def count(mask, axis):
+        return jnp.sum(jnp.where(mask, 1.0, 0.0), axis=axis, keepdims=True)
+
+    size = count(same, 0)
+    odd = size - 2.0 * jnp.floor(0.5 * size)
+    width = 1.0 + jnp.where(count(same & (row < column), 0) == 0.0, odd, 0.0)
+    place = jnp.sum(jnp.where(along < down, width, 0.0), axis=1, keepdims=True) + count(same & (column < row), 1)
+    numbers = row.astype(F32)
+    plans = ([], [], [])
+    for base in range(0, slots, tiles):
+        here = place == column.astype(F32) + base
+        plans[0].append(jnp.sum(jnp.where(here, numbers, 0.0), axis=0, keepdims=True))
+        plans[1].append(jnp.sum(jnp.where(here, targets - spare, 0.0), axis=0, keepdims=True) + spare)
+        plans[2].append(jnp.sum(jnp.where(here, down, 0.0), axis=0, keepdims=True))
+    return [jnp.concatenate(plan, axis=1).astype(jnp.int32) for plan in plans]
 
 
 def first_kernel(
     tw_hbm, to_hbm, ob_hbm, w_hbm, signs_hbm, base_hbm, noise_hbm, cluster_hbm,
-    z_ref, wo_ref, w_ref, turned_ref, inv_ref,
-    tw, to, ob, signs_ref, base_ref, noise_ref, cluster_ref, x_ref, acc_ref, mass_ref, sems,
+    z_ref, wo_ref, w_ref, turned_ref, inv_ref, plan_ref,
+    tw, to, tw_row, to_row, ob, signs_ref, base_ref, noise_ref, cluster_ref, x_ref, acc_ref, mass_ref, sems,
 ):
     small = [
         (signs_hbm, signs_ref),
@@ -71,6 +100,8 @@
         (tw_hbm, tw),
         (to_hbm, to),
         (ob_hbm, ob),
+        (tw_hbm, tw_row),
+        (to_hbm, to_row),
     ]
     copies = [pltpu.make_async_copy(source, target, sems.at[i]) for i, (source, target) in enumerate(small)]
     chunk = w_ref.shape[0] // CHUNKS
@@ -95,14 +126,20 @@
 
     def step(t):
         tile = w_ref[t]
-        acc_ref[to[t]] += jnp.dot(x_ref[tw[t]], tile, preferred_element_type=F32)
+        acc_ref[to[0, t]] += jnp.dot(x_ref[tw[0, t]], tile, preferred_element_type=F32)
         turned = tile.T
         turned_ref[t] = turned
-        mass_ref[tw[t]] += jnp.sum(turned.astype(F32).reshape(CELLS // 8, 8, CELLS), axis=0)
+        mass_ref[tw[0, t]] += jnp.sum(turned.astype(F32).reshape(CELLS // 8, 8, CELLS), axis=0)
 
     for c in range(CHUNKS):
         loads[c].wait()
         each_tile(chunk, lambda i, c=c: step(c * chunk + i))
+        if c == 0:
+            worker, owner = tw_row[...].astype(F32), to_row[...].astype(F32)
+            pull = pair_plan(owner, worker, WORK_BLOCKS, plan_ref.shape[1])
+            push = pair_plan(worker, owner, z_ref.shape[0], plan_ref.shape[1])
+            for r, values in enumerate(pull + push):
+                plan_ref[r : r + 1] = values
     for b in range(WORK_BLOCKS):
         inverse = 1.0 / (1.0 + jnp.sum(mass_ref[b], axis=0, keepdims=True))
         inv_ref[b] = jnp.broadcast_to(inverse, (8, CELLS))
@@ -122,19 +159,17 @@
 
 
 def sweep_kernel(last, *refs):
-    (tw_any, to_any, w_ref, turned_ref, f_ref, wo_ref, inv_ref), (z_ref, *refs) = refs[:7], refs[7:]
+    (plan_any, w_ref, turned_ref, f_ref, wo_ref, inv_ref), (z_ref, *refs) = refs[:6], refs[6:]
     if last:
         out_hbm, *refs = refs
-    accw_ref, x_ref, accz_ref, tw, to, sems, *refs = refs
-    tables = [pltpu.make_async_copy(tw_any, tw, sems.at[0]), pltpu.make_async_copy(to_any, to, sems.at[1])]
-    for table in tables:
-        table.start()
-    tiles = w_ref.shape[0]
+    accw_ref, x_ref, accz_ref, plan, sems, *refs = refs
+    tables = pltpu.make_async_copy(plan_any, plan, sems.at[0])
+    tables.start()
+    tiles, owners = w_ref.shape[0], z_ref.shape[0]
     accw_ref[...] = jnp.zeros_like(accw_ref)
     accz_ref[...] = jnp.zeros_like(accz_ref)
-    for table in tables:
-        table.wait()
-    add_tiles(0, tiles, to, tw, turned_ref, f_ref, accw_ref)
+    tables.wait()
+    add_pairs((tiles + owners) // 2, 0, plan, turned_ref, f_ref, accw_ref)
     if last:
         (out_ref,) = refs
     for b in range(WORK_BLOCKS):
@@ -143,10 +178,10 @@
             out_ref[:, b * CELLS : (b + 1) * CELLS] = worker
         x_ref[b] = worker.astype(BF16)
     if last:
-        copy = pltpu.make_async_copy(out_ref, out_hbm, sems.at[2])
+        copy = pltpu.make_async_copy(out_ref, out_hbm, sems.at[1])
         copy.start()
-    add_tiles(0, tiles, tw, to, w_ref, x_ref, accz_ref)
-    z_ref[...] = accz_ref[...].astype(BF16)
+    add_pairs((tiles + WORK_BLOCKS) // 2, 3, plan, w_ref, x_ref, accz_ref)
+    z_ref[...] = accz_ref[:owners].astype(BF16)
     if last:
         copy.wait()
 
@@ -322,17 +357,20 @@
     work_shape = ((WORK_BLOCKS, reps, CELLS), F32)
     firm_shape = ((FIRM_BLOCKS, reps, CELLS), F32)
     tiles = tiles_w.shape[0]
+    plan_shape = ((8, 2 * tiles), jnp.int32)
     held_shape = (tiles_w.shape, BF16, "keep")
     inverse_shape = ((WORK_BLOCKS, 8, CELLS), F32)
-    inputs = (tile_worker, tile_owner, owner_block, tiles_w, signs)
+    inputs = (rows(tile_worker), rows(tile_owner), owner_block, tiles_w, signs)
     inputs += (rows(worker_base), rows(worker_noise), rows(worker_cluster))
-    z, worker_outcome, held, turned, worker_inverse = call(
+    z, worker_outcome, held, turned, worker_inverse, plan = call(
         first_kernel,
         tuple(pltpu.with_memory_space_constraint(x, pltpu.HBM) for x in inputs),
-        (((owners, reps + EXTRA, CELLS), BF16), work_shape, held_shape, held_shape, inverse_shape),
+        (((owners, reps + EXTRA, CELLS), BF16), work_shape, held_shape, held_shape, inverse_shape, plan_shape),
         (
-            pltpu.SMEM((tiles,), jnp.int32),
-            pltpu.SMEM((tiles,), jnp.int32),
+            pltpu.SMEM((1, tiles), jnp.int32),
+            pltpu.SMEM((1, tiles), jnp.int32),
+            ((1, tiles), jnp.int32),
+            ((1, tiles), jnp.int32),
             pltpu.SMEM(owner_block.shape, jnp.int32),
             (signs.shape, jnp.int32),
             ((WORK_BLOCKS, CELLS), F32),
@@ -341,7 +379,7 @@
             ((WORK_BLOCKS, reps + EXTRA, CELLS), BF16),
             ((owners, reps + EXTRA, CELLS), F32),
             inverse_shape,
-            pltpu.SemaphoreType.DMA((7 + CHUNKS,)),
+            pltpu.SemaphoreType.DMA((9 + CHUNKS,)),
         ),
         specs=[HBM] * 8,
         name="first_push",
@@ -356,8 +394,8 @@
         name="first_firm",
     )
     older = None
-    scratch = (work_shape, ((WORK_BLOCKS, reps, CELLS), BF16), ((owners, reps, CELLS), F32))
-    scratch += (pltpu.SMEM((tiles,), jnp.int32), pltpu.SMEM((tiles,), jnp.int32), pltpu.SemaphoreType.DMA((3,)))
+    scratch = (((WORK_BLOCKS + 1, reps, CELLS), F32), ((WORK_BLOCKS, reps, CELLS), BF16))
+    scratch += (((owners + 1, reps, CELLS), F32), pltpu.SMEM(*plan_shape), pltpu.SemaphoreType.DMA((2,)))
     for k in range(1, SWEEPS):
         last = k == SWEEPS - 1
         f = exchange(send)
@@ -369,10 +407,10 @@
             out_specs.append(HBM)
         z, *rest = call(
             lambda *refs, e=last: sweep_kernel(e, *refs),
-            (tile_worker, tile_owner, keep(held), keep(turned), f, worker_outcome, worker_inverse),
+            (plan, keep(held), keep(turned), f, worker_outcome, worker_inverse),
             outputs,
             scratch + more,
-            specs=[ANY] * 2 + [VMEM] * 5,
+            specs=[ANY] + [VMEM] * 5,
             out_specs=out_specs,
             name="sweep_close" if last else "sweep",
         )

time: 228 us -> 228 us (level)
  no operation moved by 1% of the time
where the time goes in v6:
time: 228 us; the launch traced here: 227 us
  blocking collectives  192 us (84%)
  Pallas kernels  24.7 us (11%)
  starting transfers between devices  5.97 us (3%)
  waiting for transfers between devices  2.93 us (1%)
    all_to_all x13, blocking collectives, exchange(): return lax.all_to_all(values, axes, 0, 0, tiled=True)  192 us
    pallas_call x15, Pallas kernels, call(): pl.pallas_call(kernel, in_specs=specs or [SMEM] * scalars + [VMEM] * (len...  24.7 us
    ppermute x3, starting transfers between devices, body(): lax.ppermute(moment, 'reps', [(g, (g + d) % groups) for g in range(groups)])  5.97 us
  transfers between devices with their start and end apart: 3, of which 1 were waited for; matrix products, arithmetic and copies ran while one was open for 0% of the time, Pallas kernels for 0%

profile of v6, /device:TPU:0, one launch (start us, length us, event | category | flops | bytes accessed | tf_op | source)
XLA Modules:
  0.0 227.3 jit_solution(11772282961841247102)
XLA Ops:
  0.6 0.0 copy-start.2
  0.6 0.0 copy-start.5
  0.7 0.0 copy-start.4
  0.7 0.0 copy-start.3
  0.7 3.9 %first_push.1 = (bf16[32,72,128]{2,1,0:T(8,128)(2,1)S(1)}, f32[16,64,128]{2,1,0:T(8,128)S(1)}, bf16[128,128,128]{2,1,0:T(8,128)(2,1)S(1)}, bf16[128,128,128]{2,1...) custom-call(s32[1,128]{1,0:T(1,128)} %bitcast.20, s32[1,128]{1,0:T(1,128)} %bitcast.21, ...), custom_call_target="tpu_custom_call" | custom-call | tf_op jit(solution)/shard_map/first_push/pallas_call | solution.py:318
  4.6 19.0 %all_to_all.65.z_ref = bf16[32,72,128]{2,1,0:T(8,128)(2,1)S(1)} all-to-all(bf16[32,72,128]{2,1,0:T(8,128)(2,1)S(1)} %get-tuple-element.33), channel_id=1, replica_groups=mesh['tiles'=32,'reps'=4] {'tiles'}, dimensions={0} | all-to-all | bytes 1179648 | tf_op jit(solution)/shard_map/all_to_all | solution.py:351
  23.5 0.0 copy-done.2
  23.5 0.0 copy-done.5
  23.6 0.0 copy-done.4
  23.6 0.0 copy-done.3
  23.6 0.5 first_firm.1
  24.1 15.0 %all_to_all.66.refs_3_ = bf16[32,64,128]{2,1,0:T(8,128)(2,1)S(1)} all-to-all(bf16[32,64,128]{2,1,0:T(8,128)(2,1)S(1)} %get-tuple-element.34), channel_id=1, replica_groups=mesh['tiles'=32,'reps'=4] {'tiles'}, dimensions={0} | all-to-all | bytes 1048576 | tf_op jit(solution)/shard_map/all_to_all | solution.py:351
  39.1 3.3 %sweep.4 = bf16[32,64,128]{2,1,0:T(8,128)(2,1)S(1)} custom-call(s32[8,256]{1,0:T(8,128)S(1)} %get-tuple-element.29.refs_0_, bf16[128,128,128]{2,1,0:T(8,128)(2,1)S(1)} %get-tuple-element.30.refs_1_, bf16[128,128,128]{2,1,0:T(8,128)(2,1)S(1)} %get-tuple-element.31.refs_2_, bf16[32,64,128]{2,1,0:T(8,128)(2,1)S(1)} %all_to_all.66.refs_3_, ...), custom_call_target="tpu_custom_call" | custom-call | tf_op jit(solution)/shard_map/sweep/pallas_call | solution.py:318
  42.4 15.0 %all_to_all.67.refs_0_ = bf16[32,64,128]{2,1,0:T(8,128)(2,1)S(1)} all-to-all(bf16[32,64,128]{2,1,0:T(8,128)(2,1)S(1)} %sweep.4), channel_id=1, replica_groups=mesh['tiles'=32,'reps'=4] {'tiles'}, dimensions={0} | all-to-all | bytes 1048576 | tf_op jit(solution)/shard_map/all_to_all | solution.py:351
  57.5 0.3 firm.4
  57.8 15.0 %all_to_all.68.refs_3_ = bf16[32,64,128]{2,1,0:T(8,128)(2,1)S(1)} all-to-all(bf16[32,64,128]{2,1,0:T(8,128)(2,1)S(1)} %get-tuple-element.40), channel_id=1, replica_groups=mesh['tiles'=32,'reps'=4] {'tiles'}, dimensions={0} | all-to-all | bytes 1048576 | tf_op jit(solution)/shard_map/all_to_all | solution.py:351
  72.8 3.3 %sweep.5 = bf16[32,64,128]{2,1,0:T(8,128)(2,1)S(1)} custom-call(s32[8,256]{1,0:T(8,128)S(1)} %get-tuple-element.29.refs_0_, bf16[128,128,128]{2,1,0:T(8,128)(2,1)S(1)} %get-tuple-element.30.refs_1_, bf16[128,128,128]{2,1,0:T(8,128)(2,1)S(1)} %get-tuple-element.31.refs_2_, bf16[32,64,128]{2,1,0:T(8,128)(2,1)S(1)} %all_to_all.68.refs_3_, ...), custom_call_target="tpu_custom_call" | custom-call | tf_op jit(solution)/shard_map/sweep/pallas_call | solution.py:318
  76.1 15.0 %all_to_all.69.refs_0_ = bf16[32,64,128]{2,1,0:T(8,128)(2,1)S(1)} all-to-all(bf16[32,64,128]{2,1,0:T(8,128)(2,1)S(1)} %sweep.5), channel_id=1, replica_groups=mesh['tiles'=32,'reps'=4] {'tiles'}, dimensions={0} | all-to-all | bytes 1048576 | tf_op jit(solution)/shard_map/all_to_all | solution.py:351
  91.1 0.3 firm.5
  91.4 15.0 %all_to_all.70.refs_3_ = bf16[32,64,128]{2,1,0:T(8,128)(2,1)S(1)} all-to-all(bf16[32,64,128]{2,1,0:T(8,128)(2,1)S(1)} %get-tuple-element.42), channel_id=1, replica_groups=mesh['tiles'=32,'reps'=4] {'tiles'}, dimensions={0} | all-to-all | bytes 1048576 | tf_op jit(solution)/shard_map/all_to_all | solution.py:351
  106.4 3.3 %sweep.6 = bf16[32,64,128]{2,1,0:T(8,128)(2,1)S(1)} custom-call(s32[8,256]{1,0:T(8,128)S(1)} %get-tuple-element.29.refs_0_, bf16[128,128,128]{2,1,0:T(8,128)(2,1)S(1)} %get-tuple-element.30.refs_1_, bf16[128,128,128]{2,1,0:T(8,128)(2,1)S(1)} %get-tuple-element.31.refs_2_, bf16[32,64,128]{2,1,0:T(8,128)(2,1)S(1)} %all_to_all.70.refs_3_, ...), custom_call_target="tpu_custom_call" | custom-call | tf_op jit(solution)/shard_map/sweep/pallas_call | solution.py:318
  109.7 15.0 %all_to_all.71.refs_0_ = bf16[32,64,128]{2,1,0:T(8,128)(2,1)S(1)} all-to-all(bf16[32,64,128]{2,1,0:T(8,128)(2,1)S(1)} %sweep.6), channel_id=1, replica_groups=mesh['tiles'=32,'reps'=4] {'tiles'}, dimensions={0} | all-to-all | bytes 1048576 | tf_op jit(solution)/shard_map/all_to_all | solution.py:351
  124.7 0.3 firm.6
  125.0 15.0 %all_to_all.72.refs_3_ = bf16[32,64,128]{2,1,0:T(8,128)(2,1)S(1)} all-to-all(bf16[32,64,128]{2,1,0:T(8,128)(2,1)S(1)} %get-tuple-element.44), channel_id=1, replica_groups=mesh['tiles'=32,'reps'=4] {'tiles'}, dimensions={0} | all-to-all | bytes 1048576 | tf_op jit(solution)/shard_map/all_to_all | solution.py:351
  140.1 3.3 %sweep.7 = bf16[32,64,128]{2,1,0:T(8,128)(2,1)S(1)} custom-call(s32[8,256]{1,0:T(8,128)S(1)} %get-tuple-element.29.refs_0_, bf16[128,128,128]{2,1,0:T(8,128)(2,1)S(1)} %get-tuple-element.30.refs_1_, bf16[128,128,128]{2,1,0:T(8,128)(2,1)S(1)} %get-tuple-element.31.refs_2_, bf16[32,64,128]{2,1,0:T(8,128)(2,1)S(1)} %all_to_all.72.refs_3_, ...), custom_call_target="tpu_custom_call" | custom-call | tf_op jit(solution)/shard_map/sweep/pallas_call | solution.py:318
  143.3 15.0 %all_to_all.73.refs_0_ = bf16[32,64,128]{2,1,0:T(8,128)(2,1)S(1)} all-to-all(bf16[32,64,128]{2,1,0:T(8,128)(2,1)S(1)} %sweep.7), channel_id=1, replica_groups=mesh['tiles'=32,'reps'=4] {'tiles'}, dimensions={0} | all-to-all | bytes 1048576 | tf_op jit(solution)/shard_map/all_to_all | solution.py:351
  158.4 0.3 firm.7
  158.7 15.0 %all_to_all.74.refs_3_ = bf16[32,64,128]{2,1,0:T(8,128)(2,1)S(1)} all-to-all(bf16[32,64,128]{2,1,0:T(8,128)(2,1)S(1)} %firm.7), channel_id=1, replica_groups=mesh['tiles'=32,'reps'=4] {'tiles'}, dimensions={0} | all-to-all | bytes 1048576 | tf_op jit(solution)/shard_map/all_to_all | solution.py:351
  173.7 0.0 copy-start
  173.7 0.0 copy-start.1
  173.7 4.0 %sweep_close.1 = (bf16[32,64,128]{2,1,0:T(8,128)(2,1)S(1)}, f32[64,2048]{1,0:T(8,128)}) custom-call(s32[8,256]{1,0:T(8,128)S(1)} %get-tuple-element.29.refs_0_, bf16[128,128,128]{2,1,0:T(8,128)(2,1)S(1)} %get-tuple-element.30.refs_1_, bf16[128,128,128]{2,1,0:T(8,128)(2,1)S(1)} %get-tuple-element.31.refs_2_, bf16[32,64,128]{2,1,0:T(8,128)(2,1)S(1)} %all_to_all.74.refs_3_, ...), custom_call_target="tpu_custom_call" | custom-call | tf_op jit(solution)/shard_map/sweep_close/pallas_call | solution.py:318
  177.7 15.0 %all_to_all.75.refs_0_ = bf16[32,64,128]{2,1,0:T(8,128)(2,1)S(1)} all-to-all(bf16[32,64,128]{2,1,0:T(8,128)(2,1)S(1)} %get-tuple-element.47), channel_id=1, replica_groups=mesh['tiles'=32,'reps'=4] {'tiles'}, dimensions={0} | all-to-all | bytes 1048576 | tf_op jit(solution)/shard_map/all_to_all | solution.py:351
  192.7 0.0 copy-done
  192.7 0.0 copy-done.1
  192.7 1.0 close_firm.1
  193.8 11.8 %all_to_all.76.part_ref = f32[32,8,128]{2,1,0:T(8,128)S(1)} all-to-all(f32[32,8,128]{2,1,0:T(8,128)S(1)} %bitcast.13), channel_id=1, replica_groups=mesh['tiles'=32,'reps'=4] {'tiles'}, dimensions={0} | all-to-all | bytes 262144 | tf_op jit(solution)/shard_map/all_to_all | solution.py:351
  205.6 11.2 %all_to_all.77 = f32[32,8,128]{2,1,0:T(8,128)S(1)} all-to-all(f32[32,8,128]{2,1,0:T(8,128)S(1)} %total.1), channel_id=1, replica_groups=mesh['tiles'=32,'reps'=4] {'tiles'}, dimensions={0} | all-to-all | bytes 262144 | tf_op jit(solution)/shard_map/all_to_all | solution.py:351
  216.8 0.3 moment.1
  217.1 4.1 %collective-permute-start.2 = (f32[16,512]{1,0:T(8,128)S(1)}, f32[16,512]{1,0:T(8,128)S(1)}, u32[]{:S(2)}, u32[]{:S(2)}) collective-permute-start(f32[16,512]{1,0:T(8,128)S(1)} %moment.1), channel_id=1, source_target_pairs={{0,3},{1,0},{2,1},{3,2},{4,7},{5,4},{6,5},{7,6},{8,11},{9,8},{10,9... | collective-permute-start | bytes 98312 | tf_op jit(solution)/shard_map/ppermute | solution.py:451
  221.2 0.0 collective-permute-start.1
  221.2 1.9 collective-permute-start
  223.1 0.7 emit.1
  223.8 0.0 collective-permute-done.2
  223.8 2.9 %collective-permute-done.1 = f32[16,512]{1,0:T(8,128)S(1)} collective-permute-done((f32[16,512]{1,0:T(8,128)S(1)}, f32[16,512]{1,0:T(8,128)S(1)}, u32[]{:S(2)}, u32[]{:S(2)}) %collective-permute-start.1) | collective-permute-done | bytes 32800 | tf_op jit(solution)/shard_map/ppermute | solution.py:451
  226.7 0.0 collective-permute-done
  226.7 0.6 add_multiply_fusion
  (1 shorter events, 0.0 us)
Async XLA Ops:
  0.6 22.9 %copy-start.2 = (s32[64,256]{1,0:T(8,128)S(1)}, s32[64,256]{1,0:T(8,128)}, u32[]{:S(2)}) copy-start(s32[64,256]{1,0:T(8,128)} %signs_ref.1) | copy-start | bytes 196612
  0.6 22.9 %copy-start.5 = (s32[256]{0:T(256)S(1)}, s32[256]{0:T(256)}, u32[]{:S(2)}) copy-start(s32[256]{0:T(256)} %param.22) | copy-start | bytes 3076
  0.7 22.9 %copy-start.4 = (f32[256]{0:T(256)S(1)}, f32[256]{0:T(256)}, u32[]{:S(2)}) copy-start(f32[256]{0:T(256)} %param.21) | copy-start | bytes 3076
  0.7 22.9 %copy-start.3 = (f32[256]{0:T(256)S(1)}, f32[256]{0:T(256)}, u32[]{:S(2)}) copy-start(f32[256]{0:T(256)} %param.20) | copy-start | bytes 3076
  173.7 19.0 %copy-start = (f32[512,512]{1,0:T(8,128)S(1)}, f32[512,512]{1,0:T(8,128)}, u32[]{:S(2)}) copy-start(f32[512,512]{1,0:T(8,128)} %refs_6_.1) | copy-start | bytes 3145732
  173.7 19.0 %copy-start.1 = (f32[256,512]{1,0:T(8,128)S(1)}, f32[256,512]{1,0:T(8,128)}, u32[]{:S(2)}) copy-start(f32[256,512]{1,0:T(8,128)} %refs_5_.1) | copy-start | bytes 1572868
  217.1 6.7 %collective-permute-start.2 = (f32[16,512]{1,0:T(8,128)S(1)}, f32[16,512]{1,0:T(8,128)S(1)}, u32[]{:S(2)}, u32[]{:S(2)}) collective-permute-start(f32[16,512]{1,0:T(8,128)S(1)} %moment.1), channel_id=1, source_target_pairs={{0,3},{1,0},{2,1},{3,2},{4,7},{5,4},{6,5},{7,6},{8,11},{9,8},{10,9... | collective-permute-start | bytes 98312 | tf_op jit(solution)/shard_map/ppermute | solution.py:451
  221.2 5.5 %collective-permute-start.1 = (f32[16,512]{1,0:T(8,128)S(1)}, f32[16,512]{1,0:T(8,128)S(1)}, u32[]{:S(2)}, u32[]{:S(2)}) collective-permute-start(f32[16,512]{1,0:T(8,128)S(1)} %moment.1), channel_id=1, source_target_pairs={{0,1},{1,2},{2,3},{3,0},{4,5},{5,6},{6,7},{7,4},{8,9},{9,10},{10,1... | collective-permute-start | bytes 98312 | tf_op jit(solution)/shard_map/ppermute | solution.py:451
  221.2 5.5 %collective-permute-start = (f32[16,512]{1,0:T(8,128)S(1)}, f32[16,512]{1,0:T(8,128)S(1)}, u32[]{:S(2)}, u32[]{:S(2)}) collective-permute-start(f32[16,512]{1,0:T(8,128)S(1)} %moment.1), channel_id=1, source_target_pairs={{0,2},{1,3},{2,0},{3,1},{4,6},{5,7},{6,4},{7,5},{8,10},{9,11},{10,... | collective-permute-start | bytes 98312 | tf_op jit(solution)/shard_map/ppermute | solution.py:451

commit v7 on v5

--- a/solution.py
+++ b/solution.py
@@ -7,6 +7,7 @@
 
 WORK_BLOCKS = 16
 FIRM_BLOCKS = 2
+CORES = 2
 SWEEPS = 6
 CELLS = 128
 EXTRA = 8
@@ -165,79 +166,102 @@
     return (dot(a, d) + dot(b, c)) + dot(a, c)
 
 
-def gather_sums(z_ref, flags_ref, reps):
+def chip_sums(z_ref, flags_ref, reps, out_ref):
     zero = jnp.zeros((reps, CELLS), F32)
-
-    def body(s, carry):
-        first, second = carry
-        part = z_ref[s, :reps].astype(F32)
-        upper = jnp.broadcast_to(flags_ref[s, :1], part.shape) > 0.5
-        return first + jnp.where(upper, 0.0, part), second + jnp.where(upper, part, 0.0)
-
-    return lax.fori_loop(0, z_ref.shape[0], body, (zero, zero), unroll=4)
+    for owner in range(CORES):
+
+        def body(i, carry, owner=owner):
+            first, second = carry
+            part = z_ref[CORES * i + owner, :reps].astype(F32)
+            upper = jnp.broadcast_to(flags_ref[CORES * i + owner, :1], part.shape) > 0.5
+            return first + jnp.where(upper, 0.0, part), second + jnp.where(upper, part, 0.0)
+
+        sums = lax.fori_loop(0, z_ref.shape[0] // CORES, body, (zero, zero), unroll=4)
+        for j in range(FIRM_BLOCKS):
+            out_ref[FIRM_BLOCKS * owner + j] = sums[j]
 
 
 def scatter_firms(firms, flags_ref, send_ref):
-    first, second = firms
-
-    def step(s):
-        upper = jnp.broadcast_to(flags_ref[s, :1], first.shape) > 0.5
-        send_ref[s] = jnp.where(upper, second, first).astype(BF16)
-
-    each_tile(send_ref.shape[0], step, 8)
-
-
-def open_firm_kernel(z_ref, signs_ref, base_ref, noise_ref, cluster_ref, send_ref, fo_ref, inv_ref, flags_ref, now_ref):
+    for owner in range(CORES):
+        first, second = firms[FIRM_BLOCKS * owner : FIRM_BLOCKS * (owner + 1)]
+
+        def step(i, owner=owner, first=first, second=second):
+            upper = jnp.broadcast_to(flags_ref[CORES * i + owner, :1], first.shape) > 0.5
+            send_ref[CORES * i + owner] = jnp.where(upper, second, first).astype(BF16)
+
+        each_tile(send_ref.shape[0] // CORES, step, 8)
+
+
+def open_sum_kernel(z_ref, signs_ref, base_ref, noise_ref, cluster_ref, pack_ref, flags_ref):
     reps = signs_ref.shape[0]
-    owners = z_ref.shape[0]
-    mass = [jnp.zeros((1, CELLS), F32), jnp.zeros((1, CELLS), F32)]
-    for s in range(owners):
-        tail = z_ref[s, reps:].astype(F32)
-        flags_ref[s] = jnp.broadcast_to(tail[3:4], (8, CELLS))
+    blocks = CORES * FIRM_BLOCKS
+    mass = [jnp.zeros((1, CELLS), F32)] * blocks
+    for n in range(z_ref.shape[0]):
+        tail = z_ref[n, reps:].astype(F32)
+        flags_ref[n] = jnp.broadcast_to(tail[3:4], (8, CELLS))
         part = tail[0:1] + tail[1:2] + tail[2:3]
         upper = tail[3:4] > 0.5
-        mass = [mass[0] + jnp.where(upper, 0.0, part), mass[1] + jnp.where(upper, part, 0.0)]
-    sums = gather_sums(z_ref, flags_ref, reps)
+        q = FIRM_BLOCKS * (n % CORES)
+        mass[q] = mass[q] + jnp.where(upper, 0.0, part)
+        mass[q + 1] = mass[q + 1] + jnp.where(upper, part, 0.0)
+    chip_sums(z_ref, flags_ref, reps, pack_ref)
     flips = flip_table(signs_ref)
+    for j in range(FIRM_BLOCKS):
+        row = slice(j, j + 1)
+        pack_ref[blocks + j] = outcome(flips, base_ref[row], noise_ref[row], cluster_ref[row])
+    pack_ref[blocks + FIRM_BLOCKS] = jnp.zeros((reps, CELLS), F32)
+    for q in range(blocks):
+        pack_ref[blocks + FIRM_BLOCKS, q : q + 1] = mass[q]
+
+
+def open_firm_kernel(share, mine_ref, theirs_ref, flags_ref, send_ref, fo_ref, inv_ref, now_ref):
+    blocks = CORES * FIRM_BLOCKS
+    core = share[0] % CORES
+    last = blocks + FIRM_BLOCKS
+    firms = []
+    for q in range(blocks):
+        own = q // FIRM_BLOCKS == core
+        j = blocks + q % FIRM_BLOCKS
+        value = jnp.where(own, mine_ref[j], theirs_ref[j])
+        inverse = 1.0 / (1.0 + (mine_ref[last, q : q + 1] + theirs_ref[last, q : q + 1]))
+        fo_ref[q] = value
+        inv_ref[q] = jnp.broadcast_to(inverse, (8, CELLS))
+        firm = value - (mine_ref[q] + theirs_ref[q]) * inverse
+        now_ref[q] = firm
+        firms.append(firm)
+    scatter_firms(firms, flags_ref, send_ref)
+
+
+def sum_kernel(z_ref, flags_ref, out_ref):
+    chip_sums(z_ref, flags_ref, z_ref.shape[1], out_ref)
+
+
+def next_firm(omega, q, mine_ref, theirs_ref, fo_ref, inv_ref, older_ref):
+    target = fo_ref[q] - (mine_ref[q] + theirs_ref[q]) * inv_ref[q, :1]
+    if older_ref is None:
+        return omega * target
+    return older_ref[q] + omega * (target - older_ref[q])
+
+
+def firm_kernel(omega, has_older, *refs):
+    (mine_ref, theirs_ref, fo_ref, inv_ref, flags_ref), refs = refs[:5], refs[5:]
+    older_ref = refs[0] if has_older else None
+    send_ref, *now_ref = refs[1:] if has_older else refs
+    firms = []
+    for q in range(CORES * FIRM_BLOCKS):
+        firms.append(next_firm(omega, q, mine_ref, theirs_ref, fo_ref, inv_ref, older_ref))
+        if now_ref:
+            now_ref[0][q] = firms[q]
+    scatter_firms(firms, flags_ref, send_ref)
+
+
+def close_firm_kernel(
+    omega, share, mine_ref, theirs_ref, fo_ref, inv_ref, older_ref, cov_ref, white_ref, now_ref, part_ref
+):
     firms = []
     for j in range(FIRM_BLOCKS):
-        row = slice(j, j + 1)
-        inverse = 1.0 / (1.0 + mass[j])
-        value = outcome(flips, base_ref[row], noise_ref[row], cluster_ref[row])
-        fo_ref[j] = value
-        inv_ref[j] = jnp.broadcast_to(inverse, (8, CELLS))
-        firm = value - sums[j] * inverse
-        now_ref[j] = firm
-        firms.append(firm)
-    scatter_firms(firms, flags_ref, send_ref)
-
-
-def next_firms(omega, z_ref, fo_ref, inv_ref, flags_ref, older_ref):
-    sums = gather_sums(z_ref, flags_ref, z_ref.shape[1])
-    firms = []
-    for j in range(FIRM_BLOCKS):
-        target = fo_ref[j] - sums[j] * inv_ref[j, :1]
-        if older_ref is None:
-            firms.append(omega * target)
-        else:
-            firms.append(older_ref[j] + omega * (target - older_ref[j]))
-    return firms
-
-
-def firm_kernel(omega, has_older, *refs):
-    (z_ref, fo_ref, inv_ref, flags_ref), refs = refs[:4], refs[4:]
-    older_ref = refs[0] if has_older else None
-    send_ref, *now_ref = refs[1:] if has_older else refs
-    firms = next_firms(omega, z_ref, fo_ref, inv_ref, flags_ref, older_ref)
-    if now_ref:
-        for j in range(FIRM_BLOCKS):
-            now_ref[0][j] = firms[j]
-    scatter_firms(firms, flags_ref, send_ref)
-
-
-def close_firm_kernel(omega, z_ref, fo_ref, inv_ref, flags_ref, older_ref, cov_ref, white_ref, now_ref, part_ref):
-    firms = next_firms(omega, z_ref, fo_ref, inv_ref, flags_ref, older_ref)
-    for j in range(FIRM_BLOCKS):
+        q = FIRM_BLOCKS * (share[0] % CORES) + j
+        firms.append(next_firm(omega, q, mine_ref, theirs_ref, fo_ref, inv_ref, older_ref))
         now_ref[j] = firms[j]
     projected = product(jnp.concatenate(firms, axis=1), cov_ref[...], ((1,), (0,)))
     whitened = product(projected, white_ref[...], ((1,), (1,)))
@@ -315,12 +339,23 @@
     def exchange(values, axes="tiles"):
         return lax.all_to_all(values, axes, 0, 0, tiled=True)
 
+    def swap(values):
+        return lax.ppermute(values, "tiles", [(t, t ^ 1) for t in range(owners)])
+
+    def chips(values):
+        groups_of = [list(range(c, owners, CORES)) for c in range(CORES)]
+        joined = values.reshape(owners // CORES, -1, CELLS)
+        moved = lax.all_to_all(joined, "tiles", 0, 0, tiled=True, axis_index_groups=groups_of)
+        return moved.reshape(values.shape)
+
     def rows(values):
         return values.reshape(-1, CELLS)
 
     push_shape = ((owners, reps, CELLS), BF16)
     work_shape = ((WORK_BLOCKS, reps, CELLS), F32)
     firm_shape = ((FIRM_BLOCKS, reps, CELLS), F32)
+    chip_shape = ((CORES * FIRM_BLOCKS, reps, CELLS), F32)
+    flags_shape = ((owners, 8, CELLS), F32)
     tiles = tiles_w.shape[0]
     held_shape = (tiles_w.shape, BF16, "keep")
     inverse_shape = ((WORK_BLOCKS, 8, CELLS), F32)
@@ -348,11 +383,18 @@
     )
     share = lax.axis_index("tiles").astype(jnp.int32).reshape(1)
     share, z = lax.optimization_barrier((share, z))
-    z = exchange(z)
-    send, firm_outcome, firm_inverse, flags, newer = call(
+    z = chips(z)
+    pack, flags = call(
+        open_sum_kernel,
+        (z, signs, rows(firm_base), rows(firm_noise), rows(firm_cluster)),
+        (((CORES * FIRM_BLOCKS + FIRM_BLOCKS + 1, reps, CELLS), F32), flags_shape),
+        name="first_sum",
+    )
+    send, firm_outcome, firm_inverse, newer = call(
         open_firm_kernel,
-        (z, signs, rows(firm_base), rows(firm_noise), rows(firm_cluster)),
-        (push_shape, firm_shape, ((FIRM_BLOCKS, 8, CELLS), F32), ((owners, 8, CELLS), F32), firm_shape),
+        (share, pack, swap(pack), flags),
+        (push_shape, chip_shape, ((CORES * FIRM_BLOCKS, 8, CELLS), F32), chip_shape),
+        scalars=1,
         name="first_firm",
     )
     older = None
@@ -360,7 +402,7 @@
     scratch += (pltpu.SMEM((tiles,), jnp.int32), pltpu.SMEM((tiles,), jnp.int32), pltpu.SemaphoreType.DMA((3,)))
     for k in range(1, SWEEPS):
         last = k == SWEEPS - 1
-        f = exchange(send)
+        f = chips(send)
         outputs, more, out_specs = (push_shape,), (), [VMEM]
         if last:
             whole = ((reps, WORK_BLOCKS * CELLS), F32)
@@ -376,21 +418,24 @@
             out_specs=out_specs,
             name="sweep_close" if last else "sweep",
         )
-        z = exchange(z)
-        inputs = (z, firm_outcome, firm_inverse, flags) + (() if older is None else (older,))
+        z = chips(z)
+        (sums,) = call(sum_kernel, (z, flags), (chip_shape,), name="sum")
+        inputs = (sums, swap(sums), firm_outcome, firm_inverse)
+        past = () if older is None else (older,)
         if not last:
             send, *now = call(
                 lambda *refs, w=omegas[k], h=older is not None: firm_kernel(w, h, *refs),
-                inputs,
-                (push_shape, firm_shape) if k < SWEEPS - 2 else (push_shape,),
+                inputs + (flags,) + past,
+                (push_shape, chip_shape) if k < SWEEPS - 2 else (push_shape,),
                 name="firm",
             )
             older, newer = newer, now[0] if now else None
         else:
             firms, part = call(
                 lambda *refs, w=omegas[k]: close_firm_kernel(w, *refs),
-                inputs + (covariates, whitening),
+                (share,) + inputs + past + (covariates, whitening),
                 (firm_shape, ((reps * covars // CELLS, CELLS), F32)),
+                scalars=1,
                 name="close_firm",
             )
     part = exchange(part.reshape(owners, -1, CELLS))

time: 228 us -> 231 us (1.013)
  waiting for transfers between devices: 2.92 us -> 11.1 us
  blocking collectives: 192 us -> 187 us
    all_to_all x13 -> x2, blocking collectives: 192 us -> 22.6 us  [exchange(): return lax.all_to_all(values, axes, 0, 0, tiled=True)]
    all_to_all x0 -> x11, blocking collectives: none -> 164 us  [chips(): lax.all_to_all(joined, 'tiles', 0, 0, tiled=True, axis_index_groups=group...]
    ppermute x0 -> x6, waiting for transfers between devices: none -> 8.15 us  [swap(): return lax.ppermute(values, 'tiles', [(t, t ^ 1) for t in range(owners)])]
    pallas_call x15 -> x21, Pallas kernels: 24.8 us -> 24.9 us  [call(): pl.pallas_call(kernel, in_specs=specs or [SMEM] * scalars + [VMEM] * (len...]
  transfers between devices with their start and end apart: 3 -> 9, of which waited for: 1 -> 7; matrix products, arithmetic and copies ran while one was open for 0% -> 0% of each run, Pallas kernels for 0% -> 0%
where the time goes in v7:
time: 231 us
  blocking collectives  187 us (81%)
  Pallas kernels  24.9 us (11%)
  waiting for transfers between devices  11.1 us (5%)
  starting transfers between devices  6.47 us (3%)
    all_to_all x11, blocking collectives, chips(): lax.all_to_all(joined, 'tiles', 0, 0, tiled=True, axis_index_groups=group...  164 us
    pallas_call x21, Pallas kernels, call(): pl.pallas_call(kernel, in_specs=specs or [SMEM] * scalars + [VMEM] * (len...  24.9 us
    all_to_all x2, blocking collectives, exchange(): return lax.all_to_all(values, axes, 0, 0, tiled=True)  22.6 us
    ppermute x6, waiting for transfers between devices, swap(): return lax.ppermute(values, 'tiles', [(t, t ^ 1) for t in range(owners)])  8.15 us
    ppermute x3, starting transfers between devices, body(): lax.ppermute(moment, 'reps', [(g, (g + d) % groups) for g in range(groups)])  5.96 us
  transfers between devices with their start and end apart: 9, of which 7 were waited for; matrix products, arithmetic and copies ran while one was open for 0% of the time, Pallas kernels for 0%

profile of v7, /device:TPU:0, one launch (start us, length us, event | category | flops | bytes accessed | tf_op | source)
XLA Modules:
  0.0 230.7 jit_solution(16895807027682019625)
XLA Ops:
  0.6 0.0 copy-start.4
  0.6 0.0 copy-start.3
  0.7 0.0 copy-start.2
  0.7 0.0 copy-start.7
  0.7 0.0 copy-start.6
  0.7 0.0 copy-start.5
  0.7 3.7 %first_push.1 = (bf16[32,72,128]{2,1,0:T(8,128)(2,1)S(1)}, f32[16,64,128]{2,1,0:T(8,128)S(1)}, bf16[128,128,128]{2,1,0:T(8,128)(2,1)S(1)}, bf16[128,128,128]{2,1,0:T(8,128)(2,1)S(1)}, f32[16,8,128]{2,1,0:T(8,128)S(1)}) custom-call(s32[128]{0:T(128)} %refs_0_.9, s32[128]{0:T(128)} %refs_1_.9, s32[1,32]{1,0:T(1,128)} %ob_hbm.1, bf16[128,128,128]{2,1,0:T(8,128)(2,1)} %w_hbm.1, ...), custom_call_target="tpu_custom_call" | custom-call | tf_op jit(solution)/shard_map/first_push/pallas_call | solution.py:307
  4.4 19.2 %all_to_all.65 = bf16[16,144,128]{2,1,0:T(8,128)(2,1)S(1)} all-to-all(bf16[16,144,128]{2,1,0:T(8,128)(2,1)S(1)} %bitcast.49), channel_id=1, replica_groups={{0,8,16,24,32,40,48,56,64,72,80,88,96,104,112,120},{4,12,20,28,36,44,52..., dimensions={0} | all-to-all | bytes 1179648 | tf_op jit(solution)/shard_map/all_to_all | solution.py:348
  23.6 0.0 copy-done.2
  23.6 0.0 copy-done.7
  23.6 0.0 copy-done.6
  23.6 0.0 copy-done.5
  23.6 0.4 first_sum.1
  24.0 0.1 collective-permute-start
  24.1 1.5 collective-permute-done.theirs_ref
  25.6 0.1 first_firm.1
  25.7 15.1 %all_to_all.66 = bf16[16,128,128]{2,1,0:T(8,128)(2,1)S(1)} all-to-all(bf16[16,128,128]{2,1,0:T(8,128)(2,1)S(1)} %bitcast.51), channel_id=1, replica_groups={{0,8,16,24,32,40,48,56,64,72,80,88,96,104,112,120},{4,12,20,28,36,44,52..., dimensions={0} | all-to-all | bytes 1048576 | tf_op jit(solution)/shard_map/all_to_all | solution.py:348
  40.8 0.0 copy-done.4
  40.8 3.5 %sweep.4 = bf16[32,64,128]{2,1,0:T(8,128)(2,1)S(1)} custom-call(s32[128]{0:T(128)S(1)} %copy-done.3, s32[128]{0:T(128)S(1)} %copy-done.4, bf16[128,128,128]{2,1,0:T(8,128)(2,1)S(1)} %get-tuple-element.29.refs_2_, bf16[128,128,128]{2,1,0:T(8,128)(2,1)S(1)} %get-tuple-element.30.refs_3_, bf16[32,64,128]{2,1,0:T(8,128)(2,1)S(1)} %bitcast.39, ...), custom_call_target="tpu_custom_call" | custom-call | tf_op jit(solution)/shard_map/sweep/pallas_call | solution.py:307
  44.3 13.9 %all_to_all.67 = bf16[16,128,128]{2,1,0:T(8,128)(2,1)S(1)} all-to-all(bf16[16,128,128]{2,1,0:T(8,128)(2,1)S(1)} %bitcast.40), channel_id=1, replica_groups={{0,8,16,24,32,40,48,56,64,72,80,88,96,104,112,120},{4,12,20,28,36,44,52..., dimensions={0} | all-to-all | bytes 1048576 | tf_op jit(solution)/shard_map/all_to_all | solution.py:348
  58.2 0.2 sum.5.refs_0_
  58.4 0.1 collective-permute-start.1
  58.5 1.3 collective-permute-done.1.refs_1_
  59.8 0.1 firm.4
  59.9 15.1 %all_to_all.68 = bf16[16,128,128]{2,1,0:T(8,128)(2,1)S(1)} all-to-all(bf16[16,128,128]{2,1,0:T(8,128)(2,1)S(1)} %bitcast.54), channel_id=1, replica_groups={{0,8,16,24,32,40,48,56,64,72,80,88,96,104,112,120},{4,12,20,28,36,44,52..., dimensions={0} | all-to-all | bytes 1048576 | tf_op jit(solution)/shard_map/all_to_all | solution.py:348
  75.0 3.5 %sweep.5 = bf16[32,64,128]{2,1,0:T(8,128)(2,1)S(1)} custom-call(s32[128]{0:T(128)S(1)} %copy-done.3, s32[128]{0:T(128)S(1)} %copy-done.4, bf16[128,128,128]{2,1,0:T(8,128)(2,1)S(1)} %get-tuple-element.29.refs_2_, bf16[128,128,128]{2,1,0:T(8,128)(2,1)S(1)} %get-tuple-element.30.refs_3_, bf16[32,64,128]{2,1,0:T(8,128)(2,1)S(1)} %bitcast.41, ...), custom_call_target="tpu_custom_call" | custom-call | tf_op jit(solution)/shard_map/sweep/pallas_call | solution.py:307
  78.4 13.9 %all_to_all.69 = bf16[16,128,128]{2,1,0:T(8,128)(2,1)S(1)} all-to-all(bf16[16,128,128]{2,1,0:T(8,128)(2,1)S(1)} %bitcast.42), channel_id=1, replica_groups={{0,8,16,24,32,40,48,56,64,72,80,88,96,104,112,120},{4,12,20,28,36,44,52..., dimensions={0} | all-to-all | bytes 1048576 | tf_op jit(solution)/shard_map/all_to_all | solution.py:348
  92.4 0.2 sum.6.refs_0_
  92.6 0.1 collective-permute-start.2
  92.7 1.3 collective-permute-done.2.refs_1_
  94.0 0.1 firm.5
  94.1 15.1 %all_to_all.70 = bf16[16,128,128]{2,1,0:T(8,128)(2,1)S(1)} all-to-all(bf16[16,128,128]{2,1,0:T(8,128)(2,1)S(1)} %bitcast.52), channel_id=1, replica_groups={{0,8,16,24,32,40,48,56,64,72,80,88,96,104,112,120},{4,12,20,28,36,44,52..., dimensions={0} | all-to-all | bytes 1048576 | tf_op jit(solution)/shard_map/all_to_all | solution.py:348
  109.2 3.5 %sweep.6 = bf16[32,64,128]{2,1,0:T(8,128)(2,1)S(1)} custom-call(s32[128]{0:T(128)S(1)} %copy-done.3, s32[128]{0:T(128)S(1)} %copy-done.4, bf16[128,128,128]{2,1,0:T(8,128)(2,1)S(1)} %get-tuple-element.29.refs_2_, bf16[128,128,128]{2,1,0:T(8,128)(2,1)S(1)} %get-tuple-element.30.refs_3_, bf16[32,64,128]{2,1,0:T(8,128)(2,1)S(1)} %bitcast.43, ...), custom_call_target="tpu_custom_call" | custom-call | tf_op jit(solution)/shard_map/sweep/pallas_call | solution.py:307
  112.6 13.9 %all_to_all.71 = bf16[16,128,128]{2,1,0:T(8,128)(2,1)S(1)} all-to-all(bf16[16,128,128]{2,1,0:T(8,128)(2,1)S(1)} %bitcast.44), channel_id=1, replica_groups={{0,8,16,24,32,40,48,56,64,72,80,88,96,104,112,120},{4,12,20,28,36,44,52..., dimensions={0} | all-to-all | bytes 1048576 | tf_op jit(solution)/shard_map/all_to_all | solution.py:348
  126.6 0.2 sum.7.refs_0_
  126.8 0.1 collective-permute-start.3
  126.9 1.3 collective-permute-done.3.refs_1_
  128.2 0.1 firm.6
  128.3 15.1 %all_to_all.72 = bf16[16,128,128]{2,1,0:T(8,128)(2,1)S(1)} all-to-all(bf16[16,128,128]{2,1,0:T(8,128)(2,1)S(1)} %bitcast.53), channel_id=1, replica_groups={{0,8,16,24,32,40,48,56,64,72,80,88,96,104,112,120},{4,12,20,28,36,44,52..., dimensions={0} | all-to-all | bytes 1048576 | tf_op jit(solution)/shard_map/all_to_all | solution.py:348
  143.4 3.5 %sweep.7 = bf16[32,64,128]{2,1,0:T(8,128)(2,1)S(1)} custom-call(s32[128]{0:T(128)S(1)} %copy-done.3, s32[128]{0:T(128)S(1)} %copy-done.4, bf16[128,128,128]{2,1,0:T(8,128)(2,1)S(1)} %get-tuple-element.29.refs_2_, bf16[128,128,128]{2,1,0:T(8,128)(2,1)S(1)} %get-tuple-element.30.refs_3_, bf16[32,64,128]{2,1,0:T(8,128)(2,1)S(1)} %bitcast.45, ...), custom_call_target="tpu_custom_call" | custom-call | tf_op jit(solution)/shard_map/sweep/pallas_call | solution.py:307
  146.9 13.9 %all_to_all.73 = bf16[16,128,128]{2,1,0:T(8,128)(2,1)S(1)} all-to-all(bf16[16,128,128]{2,1,0:T(8,128)(2,1)S(1)} %bitcast.46), channel_id=1, replica_groups={{0,8,16,24,32,40,48,56,64,72,80,88,96,104,112,120},{4,12,20,28,36,44,52..., dimensions={0} | all-to-all | bytes 1048576 | tf_op jit(solution)/shard_map/all_to_all | solution.py:348
  160.8 0.2 sum.8.refs_0_
  161.0 0.1 collective-permute-start.4
  161.1 1.3 collective-permute-done.4.refs_1_
  162.4 0.1 firm.7
  162.5 15.1 %all_to_all.74 = bf16[16,128,128]{2,1,0:T(8,128)(2,1)S(1)} all-to-all(bf16[16,128,128]{2,1,0:T(8,128)(2,1)S(1)} %bitcast.33), channel_id=1, replica_groups={{0,8,16,24,32,40,48,56,64,72,80,88,96,104,112,120},{4,12,20,28,36,44,52..., dimensions={0} | all-to-all | bytes 1048576 | tf_op jit(solution)/shard_map/all_to_all | solution.py:348
  177.6 3.5 %sweep_close.1 = (bf16[32,64,128]{2,1,0:T(8,128)(2,1)S(1)}, f32[64,2048]{1,0:T(8,128)}) custom-call(s32[128]{0:T(128)S(1)} %copy-done.3, s32[128]{0:T(128)S(1)} %copy-done.4, bf16[128,128,128]{2,1,0:T(8,128)(2,1)S(1)} %get-tuple-element.29.refs_2_, bf16[128,128,128]{2,1,0:T(8,128)(2,1)S(1)} %get-tuple-element.30.refs_3_, bf16[32,64,128]{2,1,0:T(8,128)(2,1)S(1)} %bitcast.32, ...), custom_call_target="tpu_custom_call" | custom-call | tf_op jit(solution)/shard_map/sweep_close/pallas_call | solution.py:307
  181.1 13.9 %all_to_all.75 = bf16[16,128,128]{2,1,0:T(8,128)(2,1)S(1)} all-to-all(bf16[16,128,128]{2,1,0:T(8,128)(2,1)S(1)} %bitcast.50), channel_id=1, replica_groups={{0,8,16,24,32,40,48,56,64,72,80,88,96,104,112,120},{4,12,20,28,36,44,52..., dimensions={0} | all-to-all | bytes 1048576 | tf_op jit(solution)/shard_map/all_to_all | solution.py:348
  195.0 0.2 sum.9.refs_1_
  195.2 0.1 collective-permute-start.5
  195.3 1.3 collective-permute-done.5.refs_2_
  196.6 0.0 copy-done
  196.7 0.8 close_firm.1
  197.5 11.4 %all_to_all.76.part_ref = f32[32,8,128]{2,1,0:T(8,128)S(1)} all-to-all(f32[32,8,128]{2,1,0:T(8,128)S(1)} %bitcast.55), channel_id=1, replica_groups=mesh['tiles'=32,'reps'=4] {'tiles'}, dimensions={0} | all-to-all | bytes 262144 | tf_op jit(solution)/shard_map/all_to_all | solution.py:340
  208.9 11.2 %all_to_all.77 = f32[32,8,128]{2,1,0:T(8,128)S(1)} all-to-all(f32[32,8,128]{2,1,0:T(8,128)S(1)} %total.1), channel_id=1, replica_groups=mesh['tiles'=32,'reps'=4] {'tiles'}, dimensions={0} | all-to-all | bytes 262144 | tf_op jit(solution)/shard_map/all_to_all | solution.py:340
  220.1 0.3 moment.1
  220.5 4.1 %collective-permute-start.8 = (f32[16,512]{1,0:T(8,128)S(1)}, f32[16,512]{1,0:T(8,128)S(1)}, u32[]{:S(2)}, u32[]{:S(2)}) collective-permute-start(f32[16,512]{1,0:T(8,128)S(1)} %moment.1), channel_id=1, source_target_pairs={{0,3},{1,0},{2,1},{3,2},{4,7},{5,4},{6,5},{7,6},{8,11},{9,8},{10,9... | collective-permute-start | bytes 98312 | tf_op jit(solution)/shard_map/ppermute | solution.py:458
  224.5 0.0 collective-permute-start.7
  224.6 1.9 collective-permute-start.6
  226.4 0.7 emit.1
  227.1 0.0 collective-permute-done.8
  227.1 2.9 %collective-permute-done.7 = f32[16,512]{1,0:T(8,128)S(1)} collective-permute-done((f32[16,512]{1,0:T(8,128)S(1)}, f32[16,512]{1,0:T(8,128)S(1)}, u32[]{:S(2)}, u32[]{:S(2)}) %collective-permute-start.7) | collective-permute-done | bytes 32800 | tf_op jit(solution)/shard_map/ppermute | solution.py:458
  230.0 0.0 collective-permute-done.6
  230.0 0.6 add_multiply_fusion
  (5 shorter events, 0.0 us)
Async XLA Ops:
  0.6 40.1 %copy-start.4 = (s32[128]{0:T(128)S(1)}, s32[128]{0:T(128)}, u32[]{:S(2)}) copy-start(s32[128]{0:T(128)} %refs_1_.9) | copy-start | bytes 1540
  0.6 40.1 %copy-start.3 = (s32[128]{0:T(128)S(1)}, s32[128]{0:T(128)}, u32[]{:S(2)}) copy-start(s32[128]{0:T(128)} %refs_0_.9) | copy-start | bytes 1540
  0.7 22.9 %copy-start.2 = (s32[64,256]{1,0:T(8,128)S(1)}, s32[64,256]{1,0:T(8,128)}, u32[]{:S(2)}) copy-start(s32[64,256]{1,0:T(8,128)} %signs_ref.1) | copy-start | bytes 196612
  0.7 22.9 %copy-start.7 = (s32[256]{0:T(256)S(1)}, s32[256]{0:T(256)}, u32[]{:S(2)}) copy-start(s32[256]{0:T(256)} %param.22) | copy-start | bytes 3076
  0.7 22.9 %copy-start.6 = (f32[256]{0:T(256)S(1)}, f32[256]{0:T(256)}, u32[]{:S(2)}) copy-start(f32[256]{0:T(256)} %param.21) | copy-start | bytes 3076
  0.7 22.9 %copy-start.5 = (f32[256]{0:T(256)S(1)}, f32[256]{0:T(256)}, u32[]{:S(2)}) copy-start(f32[256]{0:T(256)} %param.20) | copy-start | bytes 3076
  24.0 1.6 collective-permute-start
  58.4 1.4 collective-permute-start.1
  92.6 1.4 collective-permute-start.2
  126.8 1.4 collective-permute-start.3
  161.0 1.4 collective-permute-start.4
  177.6 19.1 %copy-start = (f32[512,512]{1,0:T(8,128)S(1)}, f32[512,512]{1,0:T(8,128)}, u32[]{:S(2)}) copy-start(f32[512,512]{1,0:T(8,128)} %refs_7_.1) | copy-start | bytes 3145732
  177.6 19.1 %copy-start.1 = (f32[256,512]{1,0:T(8,128)S(1)}, f32[256,512]{1,0:T(8,128)}, u32[]{:S(2)}) copy-start(f32[256,512]{1,0:T(8,128)} %refs_6_.1) | copy-start | bytes 1572868
  195.2 1.4 collective-permute-start.5
  220.5 6.6 %collective-permute-start.8 = (f32[16,512]{1,0:T(8,128)S(1)}, f32[16,512]{1,0:T(8,128)S(1)}, u32[]{:S(2)}, u32[]{:S(2)}) collective-permute-start(f32[16,512]{1,0:T(8,128)S(1)} %moment.1), channel_id=1, source_target_pairs={{0,3},{1,0},{2,1},{3,2},{4,7},{5,4},{6,5},{7,6},{8,11},{9,8},{10,9... | collective-permute-start | bytes 98312 | tf_op jit(solution)/shard_map/ppermute | solution.py:458
  224.5 5.5 %collective-permute-start.7 = (f32[16,512]{1,0:T(8,128)S(1)}, f32[16,512]{1,0:T(8,128)S(1)}, u32[]{:S(2)}, u32[]{:S(2)}) collective-permute-start(f32[16,512]{1,0:T(8,128)S(1)} %moment.1), channel_id=1, source_target_pairs={{0,1},{1,2},{2,3},{3,0},{4,5},{5,6},{6,7},{7,4},{8,9},{9,10},{10,1... | collective-permute-start | bytes 98312 | tf_op jit(solution)/shard_map/ppermute | solution.py:458
  224.6 5.5 %collective-permute-start.6 = (f32[16,512]{1,0:T(8,128)S(1)}, f32[16,512]{1,0:T(8,128)S(1)}, u32[]{:S(2)}, u32[]{:S(2)}) collective-permute-start(f32[16,512]{1,0:T(8,128)S(1)} %moment.1), channel_id=1, source_target_pairs={{0,2},{1,3},{2,0},{3,1},{4,6},{5,7},{6,4},{7,5},{8,10},{9,11},{10,... | collective-permute-start | bytes 98312 | tf_op jit(solution)/shard_map/ppermute | solution.py:458

commit v8 on v6

--- a/solution.py
+++ b/solution.py
@@ -53,19 +53,18 @@
 def add_pairs(count, row, plan, w_ref, x_ref, acc_ref):
     def step(p):
         i = 2 * p
-        pair = jnp.concatenate([w_ref[plan[row, i]], w_ref[plan[row, i + 1]]], axis=1)
-        both = jnp.dot(x_ref[plan[row + 2, i]], pair, preferred_element_type=F32)
-        acc_ref[plan[row + 1, i]] += both[:, :CELLS]
-        acc_ref[plan[row + 1, i + 1]] += both[:, CELLS:]
+        values = jnp.concatenate([x_ref[plan[row + 2, i]], x_ref[plan[row + 2, i + 1]]], axis=1)
+        pair = jnp.concatenate([w_ref[plan[row, i]], w_ref[plan[row, i + 1]]], axis=0)
+        acc_ref[plan[row + 1, i]] += jnp.dot(values, pair, preferred_element_type=F32)
 
     each_tile(count, step, count)
 
 
-def pair_plan(source, target, spare, slots):
-    tiles = source.shape[1]
-    along = jnp.broadcast_to(source, (tiles, tiles))
+def pair_plan(target, source, slots):
+    tiles = target.shape[1]
+    along = jnp.broadcast_to(target, (tiles, tiles))
     down = along.T
-    targets = jnp.broadcast_to(target, (tiles, tiles)).T
+    sources = jnp.broadcast_to(source, (tiles, tiles)).T
     row = lax.broadcasted_iota(jnp.int32, (tiles, tiles), 0)
     column = lax.broadcasted_iota(jnp.int32, (tiles, tiles), 1)
     same = along == down
@@ -77,13 +76,13 @@
     odd = size - 2.0 * jnp.floor(0.5 * size)
     width = 1.0 + jnp.where(count(same & (row < column), 0) == 0.0, odd, 0.0)
     place = jnp.sum(jnp.where(along < down, width, 0.0), axis=1, keepdims=True) + count(same & (column < row), 1)
-    numbers = row.astype(F32)
+    numbers = row.astype(F32) - tiles
     plans = ([], [], [])
     for base in range(0, slots, tiles):
         here = place == column.astype(F32) + base
-        plans[0].append(jnp.sum(jnp.where(here, numbers, 0.0), axis=0, keepdims=True))
-        plans[1].append(jnp.sum(jnp.where(here, targets - spare, 0.0), axis=0, keepdims=True) + spare)
-        plans[2].append(jnp.sum(jnp.where(here, down, 0.0), axis=0, keepdims=True))
+        plans[0].append(jnp.sum(jnp.where(here, numbers, 0.0), axis=0, keepdims=True) + tiles)
+        plans[1].append(jnp.sum(jnp.where(here, down, 0.0), axis=0, keepdims=True))
+        plans[2].append(jnp.sum(jnp.where(here, sources, 0.0), axis=0, keepdims=True))
     return [jnp.concatenate(plan, axis=1).astype(jnp.int32) for plan in plans]
 
 
@@ -104,7 +103,8 @@
         (to_hbm, to_row),
     ]
     copies = [pltpu.make_async_copy(source, target, sems.at[i]) for i, (source, target) in enumerate(small)]
-    chunk = w_ref.shape[0] // CHUNKS
+    tiles = w_hbm.shape[0]
+    chunk = tiles // CHUNKS
     loads = []
     for c in range(CHUNKS):
         part = pl.ds(c * chunk, chunk)
@@ -113,6 +113,8 @@
         copy.start()
     acc_ref[...] = jnp.zeros_like(acc_ref)
     mass_ref[...] = jnp.zeros_like(mass_ref)
+    w_ref[tiles] = jnp.zeros((CELLS, CELLS), BF16)
+    turned_ref[tiles] = jnp.zeros((CELLS, CELLS), BF16)
     for copy in copies:
         copy.wait()
     reps = signs_ref.shape[0]
@@ -136,8 +138,8 @@
         each_tile(chunk, lambda i, c=c: step(c * chunk + i))
         if c == 0:
             worker, owner = tw_row[...].astype(F32), to_row[...].astype(F32)
-            pull = pair_plan(owner, worker, WORK_BLOCKS, plan_ref.shape[1])
-            push = pair_plan(worker, owner, z_ref.shape[0], plan_ref.shape[1])
+            pull = pair_plan(worker, owner, plan_ref.shape[1])
+            push = pair_plan(owner, worker, plan_ref.shape[1])
             for r, values in enumerate(pull + push):
                 plan_ref[r : r + 1] = values
     for b in range(WORK_BLOCKS):
@@ -165,11 +167,11 @@
     accw_ref, x_ref, accz_ref, plan, sems, *refs = refs
     tables = pltpu.make_async_copy(plan_any, plan, sems.at[0])
     tables.start()
-    tiles, owners = w_ref.shape[0], z_ref.shape[0]
+    tiles, owners = w_ref.shape[0] - 1, z_ref.shape[0]
     accw_ref[...] = jnp.zeros_like(accw_ref)
     accz_ref[...] = jnp.zeros_like(accz_ref)
     tables.wait()
-    add_pairs((tiles + owners) // 2, 0, plan, turned_ref, f_ref, accw_ref)
+    add_pairs((tiles + WORK_BLOCKS) // 2, 0, plan, turned_ref, f_ref, accw_ref)
     if last:
         (out_ref,) = refs
     for b in range(WORK_BLOCKS):
@@ -180,8 +182,8 @@
     if last:
         copy = pltpu.make_async_copy(out_ref, out_hbm, sems.at[1])
         copy.start()
-    add_pairs((tiles + WORK_BLOCKS) // 2, 3, plan, w_ref, x_ref, accz_ref)
-    z_ref[...] = accz_ref[:owners].astype(BF16)
+    add_pairs((tiles + owners) // 2, 3, plan, w_ref, x_ref, accz_ref)
+    z_ref[...] = accz_ref[...].astype(BF16)
     if last:
         copy.wait()
 
@@ -358,7 +360,7 @@
     firm_shape = ((FIRM_BLOCKS, reps, CELLS), F32)
     tiles = tiles_w.shape[0]
     plan_shape = ((8, 2 * tiles), jnp.int32)
-    held_shape = (tiles_w.shape, BF16, "keep")
+    held_shape = ((tiles + 1, CELLS, CELLS), BF16, "keep")
     inverse_shape = ((WORK_BLOCKS, 8, CELLS), F32)
     inputs = (rows(tile_worker), rows(tile_owner), owner_block, tiles_w, signs)
     inputs += (rows(worker_base), rows(worker_noise), rows(worker_cluster))
@@ -394,8 +396,8 @@
         name="first_firm",
     )
     older = None
-    scratch = (((WORK_BLOCKS + 1, reps, CELLS), F32), ((WORK_BLOCKS, reps, CELLS), BF16))
-    scratch += (((owners + 1, reps, CELLS), F32), pltpu.SMEM(*plan_shape), pltpu.SemaphoreType.DMA((2,)))
+    scratch = (work_shape, ((WORK_BLOCKS, reps, CELLS), BF16))
+    scratch += (((owners, reps, CELLS), F32), pltpu.SMEM(*plan_shape), pltpu.SemaphoreType.DMA((2,)))
     for k in range(1, SWEEPS):
         last = k == SWEEPS - 1
         f = exchange(send)

time: 228 us -> 227 us (level)
  no operation moved by 1% of the time
where the time goes in v8:
time: 227 us; the launch traced here: 226 us
  blocking collectives  192 us (85%)
  Pallas kernels  23.8 us (10%)
  starting transfers between devices  5.97 us (3%)
  waiting for transfers between devices  2.93 us (1%)
    all_to_all x13, blocking collectives, exchange(): return lax.all_to_all(values, axes, 0, 0, tiled=True)  192 us
    pallas_call x15, Pallas kernels, call(): pl.pallas_call(kernel, in_specs=specs or [SMEM] * scalars + [VMEM] * (len...  23.8 us
    ppermute x3, starting transfers between devices, body(): lax.ppermute(moment, 'reps', [(g, (g + d) % groups) for g in range(groups)])  5.97 us
  transfers between devices with their start and end apart: 3, of which 1 were waited for; matrix products, arithmetic and copies ran while one was open for 0% of the time, Pallas kernels for 0%

profile of v8, /device:TPU:0, one launch (start us, length us, event | category | flops | bytes accessed | tf_op | source)
XLA Modules:
  0.0 226.3 jit_solution(14184866261281283560)
XLA Ops:
  0.6 0.0 copy-start.2
  0.6 0.0 copy-start.5
  0.7 0.0 copy-start.4
  0.7 0.0 copy-start.3
  0.7 3.9 %first_push.1 = (bf16[32,72,128]{2,1,0:T(8,128)(2,1)S(1)}, f32[16,64,128]{2,1,0:T(8,128)S(1)}, bf16[129,128,128]{2,1,0:T(8,128)(2,1)S(1)}, bf16[129,128,128]{2,1...) custom-call(s32[1,128]{1,0:T(1,128)} %bitcast.20, s32[1,128]{1,0:T(1,128)} %bitcast.21, ...), custom_call_target="tpu_custom_call" | custom-call | tf_op jit(solution)/shard_map/first_push/pallas_call | solution.py:320
  4.6 19.0 %all_to_all.65.z_ref = bf16[32,72,128]{2,1,0:T(8,128)(2,1)S(1)} all-to-all(bf16[32,72,128]{2,1,0:T(8,128)(2,1)S(1)} %get-tuple-element.33), channel_id=1, replica_groups=mesh['tiles'=32,'reps'=4] {'tiles'}, dimensions={0} | all-to-all | bytes 1179648 | tf_op jit(solution)/shard_map/all_to_all | solution.py:353
  23.5 0.0 copy-done.2
  23.5 0.0 copy-done.5
  23.5 0.0 copy-done.4
  23.6 0.0 copy-done.3
  23.6 0.5 first_firm.1
  24.1 15.0 %all_to_all.66.refs_3_ = bf16[32,64,128]{2,1,0:T(8,128)(2,1)S(1)} all-to-all(bf16[32,64,128]{2,1,0:T(8,128)(2,1)S(1)} %get-tuple-element.34), channel_id=1, replica_groups=mesh['tiles'=32,'reps'=4] {'tiles'}, dimensions={0} | all-to-all | bytes 1048576 | tf_op jit(solution)/shard_map/all_to_all | solution.py:353
  39.1 3.1 %sweep.4 = bf16[32,64,128]{2,1,0:T(8,128)(2,1)S(1)} custom-call(s32[8,256]{1,0:T(8,128)S(1)} %get-tuple-element.29.refs_0_, bf16[129,128,128]{2,1,0:T(8,128)(2,1)S(1)} %get-tuple-element.30.refs_1_, bf16[129,128,128]{2,1,0:T(8,128)(2,1)S(1)} %get-tuple-element.31.refs_2_, bf16[32,64,128]{2,1,0:T(8,128)(2,1)S(1)} %all_to_all.66.refs_3_, ...), custom_call_target="tpu_custom_call" | custom-call | tf_op jit(solution)/shard_map/sweep/pallas_call | solution.py:320
  42.2 15.0 %all_to_all.67.refs_0_ = bf16[32,64,128]{2,1,0:T(8,128)(2,1)S(1)} all-to-all(bf16[32,64,128]{2,1,0:T(8,128)(2,1)S(1)} %sweep.4), channel_id=1, replica_groups=mesh['tiles'=32,'reps'=4] {'tiles'}, dimensions={0} | all-to-all | bytes 1048576 | tf_op jit(solution)/shard_map/all_to_all | solution.py:353
  57.3 0.3 firm.4
  57.6 15.0 %all_to_all.68.refs_3_ = bf16[32,64,128]{2,1,0:T(8,128)(2,1)S(1)} all-to-all(bf16[32,64,128]{2,1,0:T(8,128)(2,1)S(1)} %get-tuple-element.40), channel_id=1, replica_groups=mesh['tiles'=32,'reps'=4] {'tiles'}, dimensions={0} | all-to-all | bytes 1048576 | tf_op jit(solution)/shard_map/all_to_all | solution.py:353
  72.6 3.1 %sweep.5 = bf16[32,64,128]{2,1,0:T(8,128)(2,1)S(1)} custom-call(s32[8,256]{1,0:T(8,128)S(1)} %get-tuple-element.29.refs_0_, bf16[129,128,128]{2,1,0:T(8,128)(2,1)S(1)} %get-tuple-element.30.refs_1_, bf16[129,128,128]{2,1,0:T(8,128)(2,1)S(1)} %get-tuple-element.31.refs_2_, bf16[32,64,128]{2,1,0:T(8,128)(2,1)S(1)} %all_to_all.68.refs_3_, ...), custom_call_target="tpu_custom_call" | custom-call | tf_op jit(solution)/shard_map/sweep/pallas_call | solution.py:320
  75.7 15.0 %all_to_all.69.refs_0_ = bf16[32,64,128]{2,1,0:T(8,128)(2,1)S(1)} all-to-all(bf16[32,64,128]{2,1,0:T(8,128)(2,1)S(1)} %sweep.5), channel_id=1, replica_groups=mesh['tiles'=32,'reps'=4] {'tiles'}, dimensions={0} | all-to-all | bytes 1048576 | tf_op jit(solution)/shard_map/all_to_all | solution.py:353
  90.7 0.3 firm.5
  91.0 15.0 %all_to_all.70.refs_3_ = bf16[32,64,128]{2,1,0:T(8,128)(2,1)S(1)} all-to-all(bf16[32,64,128]{2,1,0:T(8,128)(2,1)S(1)} %get-tuple-element.42), channel_id=1, replica_groups=mesh['tiles'=32,'reps'=4] {'tiles'}, dimensions={0} | all-to-all | bytes 1048576 | tf_op jit(solution)/shard_map/all_to_all | solution.py:353
  106.0 3.1 %sweep.6 = bf16[32,64,128]{2,1,0:T(8,128)(2,1)S(1)} custom-call(s32[8,256]{1,0:T(8,128)S(1)} %get-tuple-element.29.refs_0_, bf16[129,128,128]{2,1,0:T(8,128)(2,1)S(1)} %get-tuple-element.30.refs_1_, bf16[129,128,128]{2,1,0:T(8,128)(2,1)S(1)} %get-tuple-element.31.refs_2_, bf16[32,64,128]{2,1,0:T(8,128)(2,1)S(1)} %all_to_all.70.refs_3_, ...), custom_call_target="tpu_custom_call" | custom-call | tf_op jit(solution)/shard_map/sweep/pallas_call | solution.py:320
  109.1 15.0 %all_to_all.71.refs_0_ = bf16[32,64,128]{2,1,0:T(8,128)(2,1)S(1)} all-to-all(bf16[32,64,128]{2,1,0:T(8,128)(2,1)S(1)} %sweep.6), channel_id=1, replica_groups=mesh['tiles'=32,'reps'=4] {'tiles'}, dimensions={0} | all-to-all | bytes 1048576 | tf_op jit(solution)/shard_map/all_to_all | solution.py:353
  124.2 0.3 firm.6
  124.5 15.0 %all_to_all.72.refs_3_ = bf16[32,64,128]{2,1,0:T(8,128)(2,1)S(1)} all-to-all(bf16[32,64,128]{2,1,0:T(8,128)(2,1)S(1)} %get-tuple-element.44), channel_id=1, replica_groups=mesh['tiles'=32,'reps'=4] {'tiles'}, dimensions={0} | all-to-all | bytes 1048576 | tf_op jit(solution)/shard_map/all_to_all | solution.py:353
  139.5 3.1 %sweep.7 = bf16[32,64,128]{2,1,0:T(8,128)(2,1)S(1)} custom-call(s32[8,256]{1,0:T(8,128)S(1)} %get-tuple-element.29.refs_0_, bf16[129,128,128]{2,1,0:T(8,128)(2,1)S(1)} %get-tuple-element.30.refs_1_, bf16[129,128,128]{2,1,0:T(8,128)(2,1)S(1)} %get-tuple-element.31.refs_2_, bf16[32,64,128]{2,1,0:T(8,128)(2,1)S(1)} %all_to_all.72.refs_3_, ...), custom_call_target="tpu_custom_call" | custom-call | tf_op jit(solution)/shard_map/sweep/pallas_call | solution.py:320
  142.6 15.0 %all_to_all.73.refs_0_ = bf16[32,64,128]{2,1,0:T(8,128)(2,1)S(1)} all-to-all(bf16[32,64,128]{2,1,0:T(8,128)(2,1)S(1)} %sweep.7), channel_id=1, replica_groups=mesh['tiles'=32,'reps'=4] {'tiles'}, dimensions={0} | all-to-all | bytes 1048576 | tf_op jit(solution)/shard_map/all_to_all | solution.py:353
  157.6 0.3 firm.7
  157.9 15.0 %all_to_all.74.refs_3_ = bf16[32,64,128]{2,1,0:T(8,128)(2,1)S(1)} all-to-all(bf16[32,64,128]{2,1,0:T(8,128)(2,1)S(1)} %firm.7), channel_id=1, replica_groups=mesh['tiles'=32,'reps'=4] {'tiles'}, dimensions={0} | all-to-all | bytes 1048576 | tf_op jit(solution)/shard_map/all_to_all | solution.py:353
  172.9 0.0 copy-start
  172.9 0.0 copy-start.1
  172.9 3.7 %sweep_close.1 = (bf16[32,64,128]{2,1,0:T(8,128)(2,1)S(1)}, f32[64,2048]{1,0:T(8,128)}) custom-call(s32[8,256]{1,0:T(8,128)S(1)} %get-tuple-element.29.refs_0_, bf16[129,128,128]{2,1,0:T(8,128)(2,1)S(1)} %get-tuple-element.30.refs_1_, bf16[129,128,128]{2,1,0:T(8,128)(2,1)S(1)} %get-tuple-element.31.refs_2_, bf16[32,64,128]{2,1,0:T(8,128)(2,1)S(1)} %all_to_all.74.refs_3_, ...), custom_call_target="tpu_custom_call" | custom-call | tf_op jit(solution)/shard_map/sweep_close/pallas_call | solution.py:320
  176.7 15.0 %all_to_all.75.refs_0_ = bf16[32,64,128]{2,1,0:T(8,128)(2,1)S(1)} all-to-all(bf16[32,64,128]{2,1,0:T(8,128)(2,1)S(1)} %get-tuple-element.47), channel_id=1, replica_groups=mesh['tiles'=32,'reps'=4] {'tiles'}, dimensions={0} | all-to-all | bytes 1048576 | tf_op jit(solution)/shard_map/all_to_all | solution.py:353
  191.7 0.0 copy-done
  191.7 0.0 copy-done.1
  191.7 1.0 close_firm.1
  192.7 11.8 %all_to_all.76.part_ref = f32[32,8,128]{2,1,0:T(8,128)S(1)} all-to-all(f32[32,8,128]{2,1,0:T(8,128)S(1)} %bitcast.13), channel_id=1, replica_groups=mesh['tiles'=32,'reps'=4] {'tiles'}, dimensions={0} | all-to-all | bytes 262144 | tf_op jit(solution)/shard_map/all_to_all | solution.py:353
  204.6 11.2 %all_to_all.77 = f32[32,8,128]{2,1,0:T(8,128)S(1)} all-to-all(f32[32,8,128]{2,1,0:T(8,128)S(1)} %total.1), channel_id=1, replica_groups=mesh['tiles'=32,'reps'=4] {'tiles'}, dimensions={0} | all-to-all | bytes 262144 | tf_op jit(solution)/shard_map/all_to_all | solution.py:353
  215.8 0.3 moment.1
  216.1 4.1 %collective-permute-start.2 = (f32[16,512]{1,0:T(8,128)S(1)}, f32[16,512]{1,0:T(8,128)S(1)}, u32[]{:S(2)}, u32[]{:S(2)}) collective-permute-start(f32[16,512]{1,0:T(8,128)S(1)} %moment.1), channel_id=1, source_target_pairs={{0,3},{1,0},{2,1},{3,2},{4,7},{5,4},{6,5},{7,6},{8,11},{9,8},{10,9... | collective-permute-start | bytes 98312 | tf_op jit(solution)/shard_map/ppermute | solution.py:453
  220.2 0.0 collective-permute-start.1
  220.2 1.9 collective-permute-start
  222.1 0.7 emit.1
  222.8 0.0 collective-permute-done.2
  222.8 2.9 %collective-permute-done.1 = f32[16,512]{1,0:T(8,128)S(1)} collective-permute-done((f32[16,512]{1,0:T(8,128)S(1)}, f32[16,512]{1,0:T(8,128)S(1)}, u32[]{:S(2)}, u32[]{:S(2)}) %collective-permute-start.1) | collective-permute-done | bytes 32800 | tf_op jit(solution)/shard_map/ppermute | solution.py:453
  225.7 0.0 collective-permute-done
  225.7 0.6 add_multiply_fusion
  (1 shorter events, 0.0 us)
Async XLA Ops:
  0.6 22.9 %copy-start.2 = (s32[64,256]{1,0:T(8,128)S(1)}, s32[64,256]{1,0:T(8,128)}, u32[]{:S(2)}) copy-start(s32[64,256]{1,0:T(8,128)} %signs_ref.1) | copy-start | bytes 196612
  0.6 22.9 %copy-start.5 = (s32[256]{0:T(256)S(1)}, s32[256]{0:T(256)}, u32[]{:S(2)}) copy-start(s32[256]{0:T(256)} %param.22) | copy-start | bytes 3076
  0.7 22.9 %copy-start.4 = (f32[256]{0:T(256)S(1)}, f32[256]{0:T(256)}, u32[]{:S(2)}) copy-start(f32[256]{0:T(256)} %param.21) | copy-start | bytes 3076
  0.7 22.9 %copy-start.3 = (f32[256]{0:T(256)S(1)}, f32[256]{0:T(256)}, u32[]{:S(2)}) copy-start(f32[256]{0:T(256)} %param.20) | copy-start | bytes 3076
  172.9 18.8 %copy-start = (f32[512,512]{1,0:T(8,128)S(1)}, f32[512,512]{1,0:T(8,128)}, u32[]{:S(2)}) copy-start(f32[512,512]{1,0:T(8,128)} %refs_6_.1) | copy-start | bytes 3145732
  172.9 18.8 %copy-start.1 = (f32[256,512]{1,0:T(8,128)S(1)}, f32[256,512]{1,0:T(8,128)}, u32[]{:S(2)}) copy-start(f32[256,512]{1,0:T(8,128)} %refs_5_.1) | copy-start | bytes 1572868
  216.1 6.7 %collective-permute-start.2 = (f32[16,512]{1,0:T(8,128)S(1)}, f32[16,512]{1,0:T(8,128)S(1)}, u32[]{:S(2)}, u32[]{:S(2)}) collective-permute-start(f32[16,512]{1,0:T(8,128)S(1)} %moment.1), channel_id=1, source_target_pairs={{0,3},{1,0},{2,1},{3,2},{4,7},{5,4},{6,5},{7,6},{8,11},{9,8},{10,9... | collective-permute-start | bytes 98312 | tf_op jit(solution)/shard_map/ppermute | solution.py:453
  220.2 5.5 %collective-permute-start.1 = (f32[16,512]{1,0:T(8,128)S(1)}, f32[16,512]{1,0:T(8,128)S(1)}, u32[]{:S(2)}, u32[]{:S(2)}) collective-permute-start(f32[16,512]{1,0:T(8,128)S(1)} %moment.1), channel_id=1, source_target_pairs={{0,1},{1,2},{2,3},{3,0},{4,5},{5,6},{6,7},{7,4},{8,9},{9,10},{10,1... | collective-permute-start | bytes 98312 | tf_op jit(solution)/shard_map/ppermute | solution.py:453
  220.2 5.5 %collective-permute-start = (f32[16,512]{1,0:T(8,128)S(1)}, f32[16,512]{1,0:T(8,128)S(1)}, u32[]{:S(2)}, u32[]{:S(2)}) collective-permute-start(f32[16,512]{1,0:T(8,128)S(1)} %moment.1), channel_id=1, source_target_pairs={{0,2},{1,3},{2,0},{3,1},{4,6},{5,7},{6,4},{7,5},{8,10},{9,11},{10,... | collective-permute-start | bytes 98312 | tf_op jit(solution)/shard_map/ppermute | solution.py:453

commit v9 on v8

--- a/solution.py
+++ b/solution.py
@@ -161,31 +161,24 @@
 
 
 def sweep_kernel(last, *refs):
-    (plan_any, w_ref, turned_ref, f_ref, wo_ref, inv_ref), (z_ref, *refs) = refs[:6], refs[6:]
+    plan_any, w_ref, turned_ref, f_ref, wo_ref, inv_ref, z_ref, *refs = refs
     if last:
-        out_hbm, *refs = refs
-    accw_ref, x_ref, accz_ref, plan, sems, *refs = refs
-    tables = pltpu.make_async_copy(plan_any, plan, sems.at[0])
+        out_ref, *refs = refs
+    accw_ref, x_ref, accz_ref, plan, sem = refs
+    tables = pltpu.make_async_copy(plan_any, plan, sem)
     tables.start()
     tiles, owners = w_ref.shape[0] - 1, z_ref.shape[0]
     accw_ref[...] = jnp.zeros_like(accw_ref)
     accz_ref[...] = jnp.zeros_like(accz_ref)
     tables.wait()
     add_pairs((tiles + WORK_BLOCKS) // 2, 0, plan, turned_ref, f_ref, accw_ref)
-    if last:
-        (out_ref,) = refs
     for b in range(WORK_BLOCKS):
         worker = wo_ref[b] - accw_ref[b] * inv_ref[b, :1]
         if last:
             out_ref[:, b * CELLS : (b + 1) * CELLS] = worker
         x_ref[b] = worker.astype(BF16)
-    if last:
-        copy = pltpu.make_async_copy(out_ref, out_hbm, sems.at[1])
-        copy.start()
     add_pairs((tiles + owners) // 2, 3, plan, w_ref, x_ref, accz_ref)
     z_ref[...] = accz_ref[...].astype(BF16)
-    if last:
-        copy.wait()
 
 
 def halves(value):
@@ -303,13 +296,16 @@
     moment_ref[...] = rows_ref[pl.ds(start, share_rows)]
 
 
-def emit_kernel(all_ref, now_ref, coef_ref, firm_ref):
+def emit_kernel(all_ref, now_ref, worker_ref, coef_ref, firm_ref, out_hbm, sem):
+    copy = pltpu.make_async_copy(worker_ref, out_hbm, sem)
+    copy.start()
     reps, covars = coef_ref.shape
     columns = covars // CELLS
     for c in range(columns):
         coef_ref[:, c * CELLS : (c + 1) * CELLS] = all_ref[pl.ds(c, reps, stride=columns)]
     for j in range(FIRM_BLOCKS):
         firm_ref[:, j * CELLS : (j + 1) * CELLS] = now_ref[j]
+    copy.wait()
 
 
 def keep(value):
@@ -397,23 +393,19 @@
     )
     older = None
     scratch = (work_shape, ((WORK_BLOCKS, reps, CELLS), BF16))
-    scratch += (((owners, reps, CELLS), F32), pltpu.SMEM(*plan_shape), pltpu.SemaphoreType.DMA((2,)))
+    scratch += (((owners, reps, CELLS), F32), pltpu.SMEM(*plan_shape), pltpu.SemaphoreType.DMA)
     for k in range(1, SWEEPS):
         last = k == SWEEPS - 1
         f = exchange(send)
-        outputs, more, out_specs = (push_shape,), (), [VMEM]
+        outputs = (push_shape,)
         if last:
-            whole = ((reps, WORK_BLOCKS * CELLS), F32)
-            outputs += (whole,)
-            more = (whole,)
-            out_specs.append(HBM)
+            outputs += (((reps, WORK_BLOCKS * CELLS), F32, "keep"),)
         z, *rest = call(
             lambda *refs, e=last: sweep_kernel(e, *refs),
             (plan, keep(held), keep(turned), f, worker_outcome, worker_inverse),
             outputs,
-            scratch + more,
+            scratch,
             specs=[ANY] + [VMEM] * 5,
-            out_specs=out_specs,
             name="sweep_close" if last else "sweep",
         )
         z = exchange(z)
@@ -444,15 +436,18 @@
         scalars=1,
         name="moment",
     )
-    coefficients, firm_effect = call(
+    workers = keep(rest[0])
+    coefficients, firm_effect, worker_effect = call(
         emit_kernel,
-        (everything, firms),
-        (((reps, covars), F32), ((reps, FIRM_BLOCKS * CELLS), F32)),
+        (everything, firms, workers),
+        (((reps, covars), F32), ((reps, FIRM_BLOCKS * CELLS), F32), (workers.shape, F32)),
+        (pltpu.SemaphoreType.DMA,),
+        out_specs=[VMEM, VMEM, HBM],
         name="emit",
     )
     shifted = [lax.ppermute(moment, "reps", [(g, (g + d) % groups) for g in range(groups)]) for d in range(1, groups)]
     covariance = ((moment + shifted[1]) + (shifted[0] + shifted[2])) / (reps * groups)
-    return (rest[0], firm_effect, coefficients, covariance)
+    return (worker_effect, firm_effect, coefficients, covariance)
 
 
 def solution(mesh):

time: 227 us -> 226 us (level)
  transfers between devices with their start and end apart: 3 -> 3, of which waited for: 1 -> 1; matrix products, arithmetic and copies ran while one was open for 0% -> 0% of each run, Pallas kernels for 0% -> 1%
where the time goes in v9:
time: 226 us
  blocking collectives  192 us (85%)
  Pallas kernels  23.9 us (11%)
  starting transfers between devices  5.97 us (3%)
    all_to_all x13, blocking collectives, exchange(): return lax.all_to_all(values, axes, 0, 0, tiled=True)  192 us
    pallas_call x15, Pallas kernels, call(): pl.pallas_call(kernel, in_specs=specs or [SMEM] * scalars + [VMEM] * (len...  23.9 us
    ppermute x3, starting transfers between devices, body(): lax.ppermute(moment, 'reps', [(g, (g + d) % groups) for g in range(groups)])  5.97 us
  transfers between devices with their start and end apart: 3, of which 1 were waited for; matrix products, arithmetic and copies ran while one was open for 0% of the time, Pallas kernels for 1%

profile of v9, /device:TPU:0, one launch (start us, length us, event | category | flops | bytes accessed | tf_op | source)
XLA Modules:
  0.0 225.7 jit_solution(1998982255837139398)
XLA Ops:
  0.6 0.0 copy-start.2
  0.6 0.0 copy-start.5
  0.7 0.0 copy-start.4
  0.7 0.0 copy-start.3
  0.7 3.9 %first_push.1 = (bf16[32,72,128]{2,1,0:T(8,128)(2,1)S(1)}, f32[16,64,128]{2,1,0:T(8,128)S(1)}, bf16[129,128,128]{2,1,0:T(8,128)(2,1)S(1)}, bf16[129,128,128]{2,1...) custom-call(s32[1,128]{1,0:T(1,128)} %bitcast.20, s32[1,128]{1,0:T(1,128)} %bitcast.21, ...), custom_call_target="tpu_custom_call" | custom-call | tf_op jit(solution)/shard_map/first_push/pallas_call | solution.py:316
  4.6 19.0 %all_to_all.65.z_ref = bf16[32,72,128]{2,1,0:T(8,128)(2,1)S(1)} all-to-all(bf16[32,72,128]{2,1,0:T(8,128)(2,1)S(1)} %get-tuple-element.34), channel_id=1, replica_groups=mesh['tiles'=32,'reps'=4] {'tiles'}, dimensions={0} | all-to-all | bytes 1179648 | tf_op jit(solution)/shard_map/all_to_all | solution.py:349
  23.6 0.0 copy-done.2
  23.6 0.0 copy-done.5
  23.6 0.0 copy-done.4
  23.6 0.0 copy-done.3
  23.6 0.5 first_firm.1
  24.1 15.0 %all_to_all.66.refs_3_ = bf16[32,64,128]{2,1,0:T(8,128)(2,1)S(1)} all-to-all(bf16[32,64,128]{2,1,0:T(8,128)(2,1)S(1)} %get-tuple-element.35), channel_id=1, replica_groups=mesh['tiles'=32,'reps'=4] {'tiles'}, dimensions={0} | all-to-all | bytes 1048576 | tf_op jit(solution)/shard_map/all_to_all | solution.py:349
  39.1 3.1 %sweep.4 = bf16[32,64,128]{2,1,0:T(8,128)(2,1)S(1)} custom-call(s32[8,256]{1,0:T(8,128)S(1)} %get-tuple-element.30.refs_0_, bf16[129,128,128]{2,1,0:T(8,128)(2,1)S(1)} %get-tuple-element.31.refs_1_, bf16[129,128,128]{2,1,0:T(8,128)(2,1)S(1)} %get-tuple-element.32.refs_2_, bf16[32,64,128]{2,1,0:T(8,128)(2,1)S(1)} %all_to_all.66.refs_3_, ...), custom_call_target="tpu_custom_call" | custom-call | tf_op jit(solution)/shard_map/sweep/pallas_call | solution.py:316
  42.2 15.0 %all_to_all.67.refs_0_ = bf16[32,64,128]{2,1,0:T(8,128)(2,1)S(1)} all-to-all(bf16[32,64,128]{2,1,0:T(8,128)(2,1)S(1)} %sweep.4), channel_id=1, replica_groups=mesh['tiles'=32,'reps'=4] {'tiles'}, dimensions={0} | all-to-all | bytes 1048576 | tf_op jit(solution)/shard_map/all_to_all | solution.py:349
  57.3 0.3 firm.4
  57.6 15.0 %all_to_all.68.refs_3_ = bf16[32,64,128]{2,1,0:T(8,128)(2,1)S(1)} all-to-all(bf16[32,64,128]{2,1,0:T(8,128)(2,1)S(1)} %get-tuple-element.41), channel_id=1, replica_groups=mesh['tiles'=32,'reps'=4] {'tiles'}, dimensions={0} | all-to-all | bytes 1048576 | tf_op jit(solution)/shard_map/all_to_all | solution.py:349
  72.6 3.1 %sweep.5 = bf16[32,64,128]{2,1,0:T(8,128)(2,1)S(1)} custom-call(s32[8,256]{1,0:T(8,128)S(1)} %get-tuple-element.30.refs_0_, bf16[129,128,128]{2,1,0:T(8,128)(2,1)S(1)} %get-tuple-element.31.refs_1_, bf16[129,128,128]{2,1,0:T(8,128)(2,1)S(1)} %get-tuple-element.32.refs_2_, bf16[32,64,128]{2,1,0:T(8,128)(2,1)S(1)} %all_to_all.68.refs_3_, ...), custom_call_target="tpu_custom_call" | custom-call | tf_op jit(solution)/shard_map/sweep/pallas_call | solution.py:316
  75.7 15.0 %all_to_all.69.refs_0_ = bf16[32,64,128]{2,1,0:T(8,128)(2,1)S(1)} all-to-all(bf16[32,64,128]{2,1,0:T(8,128)(2,1)S(1)} %sweep.5), channel_id=1, replica_groups=mesh['tiles'=32,'reps'=4] {'tiles'}, dimensions={0} | all-to-all | bytes 1048576 | tf_op jit(solution)/shard_map/all_to_all | solution.py:349
  90.7 0.3 firm.5
  91.0 15.0 %all_to_all.70.refs_3_ = bf16[32,64,128]{2,1,0:T(8,128)(2,1)S(1)} all-to-all(bf16[32,64,128]{2,1,0:T(8,128)(2,1)S(1)} %get-tuple-element.43), channel_id=1, replica_groups=mesh['tiles'=32,'reps'=4] {'tiles'}, dimensions={0} | all-to-all | bytes 1048576 | tf_op jit(solution)/shard_map/all_to_all | solution.py:349
  106.0 3.1 %sweep.6 = bf16[32,64,128]{2,1,0:T(8,128)(2,1)S(1)} custom-call(s32[8,256]{1,0:T(8,128)S(1)} %get-tuple-element.30.refs_0_, bf16[129,128,128]{2,1,0:T(8,128)(2,1)S(1)} %get-tuple-element.31.refs_1_, bf16[129,128,128]{2,1,0:T(8,128)(2,1)S(1)} %get-tuple-element.32.refs_2_, bf16[32,64,128]{2,1,0:T(8,128)(2,1)S(1)} %all_to_all.70.refs_3_, ...), custom_call_target="tpu_custom_call" | custom-call | tf_op jit(solution)/shard_map/sweep/pallas_call | solution.py:316
  109.1 15.0 %all_to_all.71.refs_0_ = bf16[32,64,128]{2,1,0:T(8,128)(2,1)S(1)} all-to-all(bf16[32,64,128]{2,1,0:T(8,128)(2,1)S(1)} %sweep.6), channel_id=1, replica_groups=mesh['tiles'=32,'reps'=4] {'tiles'}, dimensions={0} | all-to-all | bytes 1048576 | tf_op jit(solution)/shard_map/all_to_all | solution.py:349
  124.1 0.3 firm.6
  124.4 15.0 %all_to_all.72.refs_3_ = bf16[32,64,128]{2,1,0:T(8,128)(2,1)S(1)} all-to-all(bf16[32,64,128]{2,1,0:T(8,128)(2,1)S(1)} %get-tuple-element.45), channel_id=1, replica_groups=mesh['tiles'=32,'reps'=4] {'tiles'}, dimensions={0} | all-to-all | bytes 1048576 | tf_op jit(solution)/shard_map/all_to_all | solution.py:349
  139.5 3.1 %sweep.7 = bf16[32,64,128]{2,1,0:T(8,128)(2,1)S(1)} custom-call(s32[8,256]{1,0:T(8,128)S(1)} %get-tuple-element.30.refs_0_, bf16[129,128,128]{2,1,0:T(8,128)(2,1)S(1)} %get-tuple-element.31.refs_1_, bf16[129,128,128]{2,1,0:T(8,128)(2,1)S(1)} %get-tuple-element.32.refs_2_, bf16[32,64,128]{2,1,0:T(8,128)(2,1)S(1)} %all_to_all.72.refs_3_, ...), custom_call_target="tpu_custom_call" | custom-call | tf_op jit(solution)/shard_map/sweep/pallas_call | solution.py:316
  142.6 15.0 %all_to_all.73.refs_0_ = bf16[32,64,128]{2,1,0:T(8,128)(2,1)S(1)} all-to-all(bf16[32,64,128]{2,1,0:T(8,128)(2,1)S(1)} %sweep.7), channel_id=1, replica_groups=mesh['tiles'=32,'reps'=4] {'tiles'}, dimensions={0} | all-to-all | bytes 1048576 | tf_op jit(solution)/shard_map/all_to_all | solution.py:349
  157.6 0.3 firm.7
  157.9 15.0 %all_to_all.74.refs_3_ = bf16[32,64,128]{2,1,0:T(8,128)(2,1)S(1)} all-to-all(bf16[32,64,128]{2,1,0:T(8,128)(2,1)S(1)} %firm.7), channel_id=1, replica_groups=mesh['tiles'=32,'reps'=4] {'tiles'}, dimensions={0} | all-to-all | bytes 1048576 | tf_op jit(solution)/shard_map/all_to_all | solution.py:349
  172.9 0.0 copy-start
  172.9 0.0 copy-start.1
  172.9 3.1 %sweep_close.1 = (bf16[32,64,128]{2,1,0:T(8,128)(2,1)S(1)}, f32[64,2048]{1,0:T(8,128)S(1)}) custom-call(s32[8,256]{1,0:T(8,128)S(1)} %get-tuple-element.30.refs_0_, bf16[129,128,128]{2,1,0:T(8,128)(2,1)S(1)} %get-tuple-element.31.refs_1_, bf16[129,128,128]{2,1,0:T(8,128)(2,1)S(1)} %get-tuple-element.32.refs_2_, bf16[32,64,128]{2,1,0:T(8,128)(2,1)S(1)} %all_to_all.74.refs_3_, ...), custom_call_target="tpu_custom_call" | custom-call | tf_op jit(solution)/shard_map/sweep_close/pallas_call | solution.py:316
  176.0 15.0 %all_to_all.75.refs_0_ = bf16[32,64,128]{2,1,0:T(8,128)(2,1)S(1)} all-to-all(bf16[32,64,128]{2,1,0:T(8,128)(2,1)S(1)} %get-tuple-element.47), channel_id=1, replica_groups=mesh['tiles'=32,'reps'=4] {'tiles'}, dimensions={0} | all-to-all | bytes 1048576 | tf_op jit(solution)/shard_map/all_to_all | solution.py:349
  191.1 0.0 copy-done
  191.1 0.0 copy-done.1
  191.1 1.0 close_firm.1
  192.1 11.8 %all_to_all.76.part_ref = f32[32,8,128]{2,1,0:T(8,128)S(1)} all-to-all(f32[32,8,128]{2,1,0:T(8,128)S(1)} %bitcast.13), channel_id=1, replica_groups=mesh['tiles'=32,'reps'=4] {'tiles'}, dimensions={0} | all-to-all | bytes 262144 | tf_op jit(solution)/shard_map/all_to_all | solution.py:349
  203.9 11.2 %all_to_all.77 = f32[32,8,128]{2,1,0:T(8,128)S(1)} all-to-all(f32[32,8,128]{2,1,0:T(8,128)S(1)} %total.1), channel_id=1, replica_groups=mesh['tiles'=32,'reps'=4] {'tiles'}, dimensions={0} | all-to-all | bytes 262144 | tf_op jit(solution)/shard_map/all_to_all | solution.py:349
  215.2 0.3 moment.1
  215.5 4.1 %collective-permute-start.2 = (f32[16,512]{1,0:T(8,128)S(1)}, f32[16,512]{1,0:T(8,128)S(1)}, u32[]{:S(2)}, u32[]{:S(2)}) collective-permute-start(f32[16,512]{1,0:T(8,128)S(1)} %moment.1), channel_id=1, source_target_pairs={{0,3},{1,0},{2,1},{3,2},{4,7},{5,4},{6,5},{7,6},{8,11},{9,8},{10,9... | collective-permute-start | bytes 98312 | tf_op jit(solution)/shard_map/ppermute | solution.py:448
  219.6 0.0 collective-permute-start.1
  219.6 1.8 collective-permute-start
  221.4 1.5 emit.1
  222.9 0.0 collective-permute-done.2
  222.9 2.1 collective-permute-done.1
  225.1 0.0 collective-permute-done
  225.1 0.6 add_multiply_fusion
  (1 shorter events, 0.0 us)
Async XLA Ops:
  0.6 22.9 %copy-start.2 = (s32[64,256]{1,0:T(8,128)S(1)}, s32[64,256]{1,0:T(8,128)}, u32[]{:S(2)}) copy-start(s32[64,256]{1,0:T(8,128)} %signs_ref.1) | copy-start | bytes 196612
  0.6 22.9 %copy-start.5 = (s32[256]{0:T(256)S(1)}, s32[256]{0:T(256)}, u32[]{:S(2)}) copy-start(s32[256]{0:T(256)} %param.22) | copy-start | bytes 3076
  0.7 22.9 %copy-start.4 = (f32[256]{0:T(256)S(1)}, f32[256]{0:T(256)}, u32[]{:S(2)}) copy-start(f32[256]{0:T(256)} %param.21) | copy-start | bytes 3076
  0.7 22.9 %copy-start.3 = (f32[256]{0:T(256)S(1)}, f32[256]{0:T(256)}, u32[]{:S(2)}) copy-start(f32[256]{0:T(256)} %param.20) | copy-start | bytes 3076
  172.9 18.2 %copy-start = (f32[512,512]{1,0:T(8,128)S(1)}, f32[512,512]{1,0:T(8,128)}, u32[]{:S(2)}) copy-start(f32[512,512]{1,0:T(8,128)} %refs_6_.1) | copy-start | bytes 3145732
  172.9 18.2 %copy-start.1 = (f32[256,512]{1,0:T(8,128)S(1)}, f32[256,512]{1,0:T(8,128)}, u32[]{:S(2)}) copy-start(f32[256,512]{1,0:T(8,128)} %refs_5_.1) | copy-start | bytes 1572868
  215.5 7.5 %collective-permute-start.2 = (f32[16,512]{1,0:T(8,128)S(1)}, f32[16,512]{1,0:T(8,128)S(1)}, u32[]{:S(2)}, u32[]{:S(2)}) collective-permute-start(f32[16,512]{1,0:T(8,128)S(1)} %moment.1), channel_id=1, source_target_pairs={{0,3},{1,0},{2,1},{3,2},{4,7},{5,4},{6,5},{7,6},{8,11},{9,8},{10,9... | collective-permute-start | bytes 98312 | tf_op jit(solution)/shard_map/ppermute | solution.py:448
  219.6 5.5 %collective-permute-start.1 = (f32[16,512]{1,0:T(8,128)S(1)}, f32[16,512]{1,0:T(8,128)S(1)}, u32[]{:S(2)}, u32[]{:S(2)}) collective-permute-start(f32[16,512]{1,0:T(8,128)S(1)} %moment.1), channel_id=1, source_target_pairs={{0,1},{1,2},{2,3},{3,0},{4,5},{5,6},{6,7},{7,4},{8,9},{9,10},{10,1... | collective-permute-start | bytes 98312 | tf_op jit(solution)/shard_map/ppermute | solution.py:448
  219.6 5.5 %collective-permute-start = (f32[16,512]{1,0:T(8,128)S(1)}, f32[16,512]{1,0:T(8,128)S(1)}, u32[]{:S(2)}, u32[]{:S(2)}) collective-permute-start(f32[16,512]{1,0:T(8,128)S(1)} %moment.1), channel_id=1, source_target_pairs={{0,2},{1,3},{2,0},{3,1},{4,6},{5,7},{6,4},{7,5},{8,10},{9,11},{10,... | collective-permute-start | bytes 98312 | tf_op jit(solution)/shard_map/ppermute | solution.py:448

commit v10 on v9

--- a/solution.py
+++ b/solution.py
@@ -192,7 +192,9 @@
     def dot(p, q):
         return lax.dot_general(p, q, (dims, ((), ())), preferred_element_type=F32)
 
-    return (dot(a, d) + dot(b, c)) + dot(a, c)
+    rows = a.shape[1 - dims[0][0]]
+    both = dot(jnp.concatenate([a, b], axis=1 - dims[0][0]), c)
+    return (dot(a, d) + both[rows:]) + both[:rows]
 
 
 def gather_sums(z_ref, flags_ref, reps):
@@ -204,7 +206,7 @@
         upper = jnp.broadcast_to(flags_ref[s, :1], part.shape) > 0.5
         return first + jnp.where(upper, 0.0, part), second + jnp.where(upper, part, 0.0)
 
-    return lax.fori_loop(0, z_ref.shape[0], body, (zero, zero), unroll=4)
+    return lax.fori_loop(0, z_ref.shape[0], body, (zero, zero), unroll=16)
 
 
 def scatter_firms(firms, flags_ref, send_ref):
@@ -214,7 +216,7 @@
         upper = jnp.broadcast_to(flags_ref[s, :1], first.shape) > 0.5
         send_ref[s] = jnp.where(upper, second, first).astype(BF16)
 
-    each_tile(send_ref.shape[0], step, 8)
+    each_tile(send_ref.shape[0], step, 16)
 
 
 def open_firm_kernel(z_ref, signs_ref, base_ref, noise_ref, cluster_ref, send_ref, fo_ref, inv_ref, flags_ref, now_ref):

time: 226 us -> 226 us (level)
  no operation moved by 1% of the time
where the time goes in v10:
time: 226 us; the launch traced here: 225 us
  blocking collectives  192 us (85%)
  Pallas kernels  23.5 us (10%)
  starting transfers between devices  5.98 us (3%)
    all_to_all x13, blocking collectives, exchange(): return lax.all_to_all(values, axes, 0, 0, tiled=True)  192 us
    pallas_call x15, Pallas kernels, call(): pl.pallas_call(kernel, in_specs=specs or [SMEM] * scalars + [VMEM] * (len...  23.5 us
    ppermute x3, starting transfers between devices, body(): lax.ppermute(moment, 'reps', [(g, (g + d) % groups) for g in range(groups)])  5.98 us
  transfers between devices with their start and end apart: 3, of which 1 were waited for; matrix products, arithmetic and copies ran while one was open for 0% of the time, Pallas kernels for 1%

profile of v10, /device:TPU:0, one launch (start us, length us, event | category | flops | bytes accessed | tf_op | source)
XLA Modules:
  0.0 225.2 jit_solution(322087659226465601)
XLA Ops:
  0.6 0.0 copy-start.2
  0.6 0.0 copy-start.5
  0.7 0.0 copy-start.4
  0.7 0.0 copy-start.3
  0.7 3.9 %first_push.1 = (bf16[32,72,128]{2,1,0:T(8,128)(2,1)S(1)}, f32[16,64,128]{2,1,0:T(8,128)S(1)}, bf16[129,128,128]{2,1,0:T(8,128)(2,1)S(1)}, bf16[129,128,128]{2,1...) custom-call(s32[1,128]{1,0:T(1,128)} %bitcast.20, s32[1,128]{1,0:T(1,128)} %bitcast.21, ...), custom_call_target="tpu_custom_call" | custom-call | tf_op jit(solution)/shard_map/first_push/pallas_call | solution.py:318
  4.6 19.0 %all_to_all.65.z_ref = bf16[32,72,128]{2,1,0:T(8,128)(2,1)S(1)} all-to-all(bf16[32,72,128]{2,1,0:T(8,128)(2,1)S(1)} %get-tuple-element.34), channel_id=1, replica_groups=mesh['tiles'=32,'reps'=4] {'tiles'}, dimensions={0} | all-to-all | bytes 1179648 | tf_op jit(solution)/shard_map/all_to_all | solution.py:351
  23.5 0.0 copy-done.2
  23.5 0.0 copy-done.5
  23.5 0.0 copy-done.4
  23.6 0.0 copy-done.3
  23.6 0.5 first_firm.1
  24.0 15.0 %all_to_all.66.refs_3_ = bf16[32,64,128]{2,1,0:T(8,128)(2,1)S(1)} all-to-all(bf16[32,64,128]{2,1,0:T(8,128)(2,1)S(1)} %get-tuple-element.35), channel_id=1, replica_groups=mesh['tiles'=32,'reps'=4] {'tiles'}, dimensions={0} | all-to-all | bytes 1048576 | tf_op jit(solution)/shard_map/all_to_all | solution.py:351
  39.1 3.1 %sweep.4 = bf16[32,64,128]{2,1,0:T(8,128)(2,1)S(1)} custom-call(s32[8,256]{1,0:T(8,128)S(1)} %get-tuple-element.30.refs_0_, bf16[129,128,128]{2,1,0:T(8,128)(2,1)S(1)} %get-tuple-element.31.refs_1_, bf16[129,128,128]{2,1,0:T(8,128)(2,1)S(1)} %get-tuple-element.32.refs_2_, bf16[32,64,128]{2,1,0:T(8,128)(2,1)S(1)} %all_to_all.66.refs_3_, ...), custom_call_target="tpu_custom_call" | custom-call | tf_op jit(solution)/shard_map/sweep/pallas_call | solution.py:318
  42.2 15.0 %all_to_all.67.refs_0_ = bf16[32,64,128]{2,1,0:T(8,128)(2,1)S(1)} all-to-all(bf16[32,64,128]{2,1,0:T(8,128)(2,1)S(1)} %sweep.4), channel_id=1, replica_groups=mesh['tiles'=32,'reps'=4] {'tiles'}, dimensions={0} | all-to-all | bytes 1048576 | tf_op jit(solution)/shard_map/all_to_all | solution.py:351
  57.2 0.3 firm.4
  57.5 15.0 %all_to_all.68.refs_3_ = bf16[32,64,128]{2,1,0:T(8,128)(2,1)S(1)} all-to-all(bf16[32,64,128]{2,1,0:T(8,128)(2,1)S(1)} %get-tuple-element.41), channel_id=1, replica_groups=mesh['tiles'=32,'reps'=4] {'tiles'}, dimensions={0} | all-to-all | bytes 1048576 | tf_op jit(solution)/shard_map/all_to_all | solution.py:351
  72.5 3.1 %sweep.5 = bf16[32,64,128]{2,1,0:T(8,128)(2,1)S(1)} custom-call(s32[8,256]{1,0:T(8,128)S(1)} %get-tuple-element.30.refs_0_, bf16[129,128,128]{2,1,0:T(8,128)(2,1)S(1)} %get-tuple-element.31.refs_1_, bf16[129,128,128]{2,1,0:T(8,128)(2,1)S(1)} %get-tuple-element.32.refs_2_, bf16[32,64,128]{2,1,0:T(8,128)(2,1)S(1)} %all_to_all.68.refs_3_, ...), custom_call_target="tpu_custom_call" | custom-call | tf_op jit(solution)/shard_map/sweep/pallas_call | solution.py:318
  75.6 15.0 %all_to_all.69.refs_0_ = bf16[32,64,128]{2,1,0:T(8,128)(2,1)S(1)} all-to-all(bf16[32,64,128]{2,1,0:T(8,128)(2,1)S(1)} %sweep.5), channel_id=1, replica_groups=mesh['tiles'=32,'reps'=4] {'tiles'}, dimensions={0} | all-to-all | bytes 1048576 | tf_op jit(solution)/shard_map/all_to_all | solution.py:351
  90.6 0.3 firm.5
  90.9 15.0 %all_to_all.70.refs_3_ = bf16[32,64,128]{2,1,0:T(8,128)(2,1)S(1)} all-to-all(bf16[32,64,128]{2,1,0:T(8,128)(2,1)S(1)} %get-tuple-element.43), channel_id=1, replica_groups=mesh['tiles'=32,'reps'=4] {'tiles'}, dimensions={0} | all-to-all | bytes 1048576 | tf_op jit(solution)/shard_map/all_to_all | solution.py:351
  105.9 3.1 %sweep.6 = bf16[32,64,128]{2,1,0:T(8,128)(2,1)S(1)} custom-call(s32[8,256]{1,0:T(8,128)S(1)} %get-tuple-element.30.refs_0_, bf16[129,128,128]{2,1,0:T(8,128)(2,1)S(1)} %get-tuple-element.31.refs_1_, bf16[129,128,128]{2,1,0:T(8,128)(2,1)S(1)} %get-tuple-element.32.refs_2_, bf16[32,64,128]{2,1,0:T(8,128)(2,1)S(1)} %all_to_all.70.refs_3_, ...), custom_call_target="tpu_custom_call" | custom-call | tf_op jit(solution)/shard_map/sweep/pallas_call | solution.py:318
  109.0 15.0 %all_to_all.71.refs_0_ = bf16[32,64,128]{2,1,0:T(8,128)(2,1)S(1)} all-to-all(bf16[32,64,128]{2,1,0:T(8,128)(2,1)S(1)} %sweep.6), channel_id=1, replica_groups=mesh['tiles'=32,'reps'=4] {'tiles'}, dimensions={0} | all-to-all | bytes 1048576 | tf_op jit(solution)/shard_map/all_to_all | solution.py:351
  124.0 0.3 firm.6
  124.3 15.0 %all_to_all.72.refs_3_ = bf16[32,64,128]{2,1,0:T(8,128)(2,1)S(1)} all-to-all(bf16[32,64,128]{2,1,0:T(8,128)(2,1)S(1)} %get-tuple-element.45), channel_id=1, replica_groups=mesh['tiles'=32,'reps'=4] {'tiles'}, dimensions={0} | all-to-all | bytes 1048576 | tf_op jit(solution)/shard_map/all_to_all | solution.py:351
  139.3 3.1 %sweep.7 = bf16[32,64,128]{2,1,0:T(8,128)(2,1)S(1)} custom-call(s32[8,256]{1,0:T(8,128)S(1)} %get-tuple-element.30.refs_0_, bf16[129,128,128]{2,1,0:T(8,128)(2,1)S(1)} %get-tuple-element.31.refs_1_, bf16[129,128,128]{2,1,0:T(8,128)(2,1)S(1)} %get-tuple-element.32.refs_2_, bf16[32,64,128]{2,1,0:T(8,128)(2,1)S(1)} %all_to_all.72.refs_3_, ...), custom_call_target="tpu_custom_call" | custom-call | tf_op jit(solution)/shard_map/sweep/pallas_call | solution.py:318
  142.4 15.0 %all_to_all.73.refs_0_ = bf16[32,64,128]{2,1,0:T(8,128)(2,1)S(1)} all-to-all(bf16[32,64,128]{2,1,0:T(8,128)(2,1)S(1)} %sweep.7), channel_id=1, replica_groups=mesh['tiles'=32,'reps'=4] {'tiles'}, dimensions={0} | all-to-all | bytes 1048576 | tf_op jit(solution)/shard_map/all_to_all | solution.py:351
  157.4 0.3 firm.7
  157.7 15.0 %all_to_all.74.refs_3_ = bf16[32,64,128]{2,1,0:T(8,128)(2,1)S(1)} all-to-all(bf16[32,64,128]{2,1,0:T(8,128)(2,1)S(1)} %firm.7), channel_id=1, replica_groups=mesh['tiles'=32,'reps'=4] {'tiles'}, dimensions={0} | all-to-all | bytes 1048576 | tf_op jit(solution)/shard_map/all_to_all | solution.py:351
  172.7 0.0 copy-start
  172.7 0.0 copy-start.1
  172.7 3.1 %sweep_close.1 = (bf16[32,64,128]{2,1,0:T(8,128)(2,1)S(1)}, f32[64,2048]{1,0:T(8,128)S(1)}) custom-call(s32[8,256]{1,0:T(8,128)S(1)} %get-tuple-element.30.refs_0_, bf16[129,128,128]{2,1,0:T(8,128)(2,1)S(1)} %get-tuple-element.31.refs_1_, bf16[129,128,128]{2,1,0:T(8,128)(2,1)S(1)} %get-tuple-element.32.refs_2_, bf16[32,64,128]{2,1,0:T(8,128)(2,1)S(1)} %all_to_all.74.refs_3_, ...), custom_call_target="tpu_custom_call" | custom-call | tf_op jit(solution)/shard_map/sweep_close/pallas_call | solution.py:318
  175.8 15.0 %all_to_all.75.refs_0_ = bf16[32,64,128]{2,1,0:T(8,128)(2,1)S(1)} all-to-all(bf16[32,64,128]{2,1,0:T(8,128)(2,1)S(1)} %get-tuple-element.47), channel_id=1, replica_groups=mesh['tiles'=32,'reps'=4] {'tiles'}, dimensions={0} | all-to-all | bytes 1048576 | tf_op jit(solution)/shard_map/all_to_all | solution.py:351
  190.8 0.0 copy-done
  190.8 0.0 copy-done.1
  190.8 0.8 close_firm.1
  191.6 11.8 %all_to_all.76.part_ref = f32[32,8,128]{2,1,0:T(8,128)S(1)} all-to-all(f32[32,8,128]{2,1,0:T(8,128)S(1)} %bitcast.13), channel_id=1, replica_groups=mesh['tiles'=32,'reps'=4] {'tiles'}, dimensions={0} | all-to-all | bytes 262144 | tf_op jit(solution)/shard_map/all_to_all | solution.py:351
  203.4 11.2 %all_to_all.77 = f32[32,8,128]{2,1,0:T(8,128)S(1)} all-to-all(f32[32,8,128]{2,1,0:T(8,128)S(1)} %total.1), channel_id=1, replica_groups=mesh['tiles'=32,'reps'=4] {'tiles'}, dimensions={0} | all-to-all | bytes 262144 | tf_op jit(solution)/shard_map/all_to_all | solution.py:351
  214.7 0.3 moment.1
  215.0 4.1 %collective-permute-start.2 = (f32[16,512]{1,0:T(8,128)S(1)}, f32[16,512]{1,0:T(8,128)S(1)}, u32[]{:S(2)}, u32[]{:S(2)}) collective-permute-start(f32[16,512]{1,0:T(8,128)S(1)} %moment.1), channel_id=1, source_target_pairs={{0,3},{1,0},{2,1},{3,2},{4,7},{5,4},{6,5},{7,6},{8,11},{9,8},{10,9... | collective-permute-start | bytes 98312 | tf_op jit(solution)/shard_map/ppermute | solution.py:450
  219.1 0.0 collective-permute-start.1
  219.1 1.9 collective-permute-start
  221.0 1.5 emit.1
  222.4 0.0 collective-permute-done.2
  222.5 2.1 collective-permute-done.1
  224.6 0.0 collective-permute-done
  224.6 0.6 add_multiply_fusion
  (1 shorter events, 0.0 us)
Async XLA Ops:
  0.6 22.9 %copy-start.2 = (s32[64,256]{1,0:T(8,128)S(1)}, s32[64,256]{1,0:T(8,128)}, u32[]{:S(2)}) copy-start(s32[64,256]{1,0:T(8,128)} %signs_ref.1) | copy-start | bytes 196612
  0.6 22.9 %copy-start.5 = (s32[256]{0:T(256)S(1)}, s32[256]{0:T(256)}, u32[]{:S(2)}) copy-start(s32[256]{0:T(256)} %param.22) | copy-start | bytes 3076
  0.7 22.9 %copy-start.4 = (f32[256]{0:T(256)S(1)}, f32[256]{0:T(256)}, u32[]{:S(2)}) copy-start(f32[256]{0:T(256)} %param.21) | copy-start | bytes 3076
  0.7 22.9 %copy-start.3 = (f32[256]{0:T(256)S(1)}, f32[256]{0:T(256)}, u32[]{:S(2)}) copy-start(f32[256]{0:T(256)} %param.20) | copy-start | bytes 3076
  172.7 18.1 %copy-start = (f32[512,512]{1,0:T(8,128)S(1)}, f32[512,512]{1,0:T(8,128)}, u32[]{:S(2)}) copy-start(f32[512,512]{1,0:T(8,128)} %refs_6_.1) | copy-start | bytes 3145732
  172.7 18.1 %copy-start.1 = (f32[256,512]{1,0:T(8,128)S(1)}, f32[256,512]{1,0:T(8,128)}, u32[]{:S(2)}) copy-start(f32[256,512]{1,0:T(8,128)} %refs_5_.1) | copy-start | bytes 1572868
  215.0 7.5 %collective-permute-start.2 = (f32[16,512]{1,0:T(8,128)S(1)}, f32[16,512]{1,0:T(8,128)S(1)}, u32[]{:S(2)}, u32[]{:S(2)}) collective-permute-start(f32[16,512]{1,0:T(8,128)S(1)} %moment.1), channel_id=1, source_target_pairs={{0,3},{1,0},{2,1},{3,2},{4,7},{5,4},{6,5},{7,6},{8,11},{9,8},{10,9... | collective-permute-start | bytes 98312 | tf_op jit(solution)/shard_map/ppermute | solution.py:450
  219.1 5.5 %collective-permute-start.1 = (f32[16,512]{1,0:T(8,128)S(1)}, f32[16,512]{1,0:T(8,128)S(1)}, u32[]{:S(2)}, u32[]{:S(2)}) collective-permute-start(f32[16,512]{1,0:T(8,128)S(1)} %moment.1), channel_id=1, source_target_pairs={{0,1},{1,2},{2,3},{3,0},{4,5},{5,6},{6,7},{7,4},{8,9},{9,10},{10,1... | collective-permute-start | bytes 98312 | tf_op jit(solution)/shard_map/ppermute | solution.py:450
  219.1 5.5 %collective-permute-start = (f32[16,512]{1,0:T(8,128)S(1)}, f32[16,512]{1,0:T(8,128)S(1)}, u32[]{:S(2)}, u32[]{:S(2)}) collective-permute-start(f32[16,512]{1,0:T(8,128)S(1)} %moment.1), channel_id=1, source_target_pairs={{0,2},{1,3},{2,0},{3,1},{4,6},{5,7},{6,4},{7,5},{8,10},{9,11},{10,... | collective-permute-start | bytes 98312 | tf_op jit(solution)/shard_map/ppermute | solution.py:450

commit v11 on v10

--- a/solution.py
+++ b/solution.py
@@ -12,7 +12,7 @@
 EXTRA = 8
 SPECTRAL = 0.8
 UNROLL = 64
-CHUNKS = 4
+CHUNKS = 2
 
 F32 = jnp.float32
 BF16 = jnp.bfloat16

time: 226 us -> 226 us (level)
  no operation moved by 1% of the time
where the time goes in v11:
time: 226 us; the launch traced here: 225 us
  blocking collectives  192 us (85%)
  Pallas kernels  23.6 us (10%)
  starting transfers between devices  5.97 us (3%)
    all_to_all x13, blocking collectives, exchange(): return lax.all_to_all(values, axes, 0, 0, tiled=True)  192 us
    pallas_call x15, Pallas kernels, call(): pl.pallas_call(kernel, in_specs=specs or [SMEM] * scalars + [VMEM] * (len...  23.6 us
    ppermute x3, starting transfers between devices, body(): lax.ppermute(moment, 'reps', [(g, (g + d) % groups) for g in range(groups)])  5.97 us
  transfers between devices with their start and end apart: 3, of which 1 were waited for; matrix products, arithmetic and copies ran while one was open for 0% of the time, Pallas kernels for 1%

profile of v11, /device:TPU:0, one launch (start us, length us, event | category | flops | bytes accessed | tf_op | source)
XLA Modules:
  0.0 225.3 jit_solution(3523694119888107506)
XLA Ops:
  0.6 0.0 copy-start.2
  0.6 0.0 copy-start.5
  0.7 0.0 copy-start.4
  0.7 0.0 copy-start.3
  0.7 3.9 %first_push.1 = (bf16[32,72,128]{2,1,0:T(8,128)(2,1)S(1)}, f32[16,64,128]{2,1,0:T(8,128)S(1)}, bf16[129,128,128]{2,1,0:T(8,128)(2,1)S(1)}, bf16[129,128,128]{2,1...) custom-call(s32[1,128]{1,0:T(1,128)} %bitcast.20, s32[1,128]{1,0:T(1,128)} %bitcast.21, ...), custom_call_target="tpu_custom_call" | custom-call | tf_op jit(solution)/shard_map/first_push/pallas_call | solution.py:318
  4.6 19.0 %all_to_all.65.z_ref = bf16[32,72,128]{2,1,0:T(8,128)(2,1)S(1)} all-to-all(bf16[32,72,128]{2,1,0:T(8,128)(2,1)S(1)} %get-tuple-element.34), channel_id=1, replica_groups=mesh['tiles'=32,'reps'=4] {'tiles'}, dimensions={0} | all-to-all | bytes 1179648 | tf_op jit(solution)/shard_map/all_to_all | solution.py:351
  23.6 0.0 copy-done.2
  23.6 0.0 copy-done.5
  23.6 0.0 copy-done.4
  23.6 0.0 copy-done.3
  23.6 0.5 first_firm.1
  24.1 15.0 %all_to_all.66.refs_3_ = bf16[32,64,128]{2,1,0:T(8,128)(2,1)S(1)} all-to-all(bf16[32,64,128]{2,1,0:T(8,128)(2,1)S(1)} %get-tuple-element.35), channel_id=1, replica_groups=mesh['tiles'=32,'reps'=4] {'tiles'}, dimensions={0} | all-to-all | bytes 1048576 | tf_op jit(solution)/shard_map/all_to_all | solution.py:351
  39.2 3.1 %sweep.4 = bf16[32,64,128]{2,1,0:T(8,128)(2,1)S(1)} custom-call(s32[8,256]{1,0:T(8,128)S(1)} %get-tuple-element.30.refs_0_, bf16[129,128,128]{2,1,0:T(8,128)(2,1)S(1)} %get-tuple-element.31.refs_1_, bf16[129,128,128]{2,1,0:T(8,128)(2,1)S(1)} %get-tuple-element.32.refs_2_, bf16[32,64,128]{2,1,0:T(8,128)(2,1)S(1)} %all_to_all.66.refs_3_, ...), custom_call_target="tpu_custom_call" | custom-call | tf_op jit(solution)/shard_map/sweep/pallas_call | solution.py:318
  42.3 15.0 %all_to_all.67.refs_0_ = bf16[32,64,128]{2,1,0:T(8,128)(2,1)S(1)} all-to-all(bf16[32,64,128]{2,1,0:T(8,128)(2,1)S(1)} %sweep.4), channel_id=1, replica_groups=mesh['tiles'=32,'reps'=4] {'tiles'}, dimensions={0} | all-to-all | bytes 1048576 | tf_op jit(solution)/shard_map/all_to_all | solution.py:351
  57.3 0.3 firm.4
  57.5 15.0 %all_to_all.68.refs_3_ = bf16[32,64,128]{2,1,0:T(8,128)(2,1)S(1)} all-to-all(bf16[32,64,128]{2,1,0:T(8,128)(2,1)S(1)} %get-tuple-element.41), channel_id=1, replica_groups=mesh['tiles'=32,'reps'=4] {'tiles'}, dimensions={0} | all-to-all | bytes 1048576 | tf_op jit(solution)/shard_map/all_to_all | solution.py:351
  72.6 3.1 %sweep.5 = bf16[32,64,128]{2,1,0:T(8,128)(2,1)S(1)} custom-call(s32[8,256]{1,0:T(8,128)S(1)} %get-tuple-element.30.refs_0_, bf16[129,128,128]{2,1,0:T(8,128)(2,1)S(1)} %get-tuple-element.31.refs_1_, bf16[129,128,128]{2,1,0:T(8,128)(2,1)S(1)} %get-tuple-element.32.refs_2_, bf16[32,64,128]{2,1,0:T(8,128)(2,1)S(1)} %all_to_all.68.refs_3_, ...), custom_call_target="tpu_custom_call" | custom-call | tf_op jit(solution)/shard_map/sweep/pallas_call | solution.py:318
  75.7 15.0 %all_to_all.69.refs_0_ = bf16[32,64,128]{2,1,0:T(8,128)(2,1)S(1)} all-to-all(bf16[32,64,128]{2,1,0:T(8,128)(2,1)S(1)} %sweep.5), channel_id=1, replica_groups=mesh['tiles'=32,'reps'=4] {'tiles'}, dimensions={0} | all-to-all | bytes 1048576 | tf_op jit(solution)/shard_map/all_to_all | solution.py:351
  90.7 0.3 firm.5
  91.0 15.0 %all_to_all.70.refs_3_ = bf16[32,64,128]{2,1,0:T(8,128)(2,1)S(1)} all-to-all(bf16[32,64,128]{2,1,0:T(8,128)(2,1)S(1)} %get-tuple-element.43), channel_id=1, replica_groups=mesh['tiles'=32,'reps'=4] {'tiles'}, dimensions={0} | all-to-all | bytes 1048576 | tf_op jit(solution)/shard_map/all_to_all | solution.py:351
  106.0 3.1 %sweep.6 = bf16[32,64,128]{2,1,0:T(8,128)(2,1)S(1)} custom-call(s32[8,256]{1,0:T(8,128)S(1)} %get-tuple-element.30.refs_0_, bf16[129,128,128]{2,1,0:T(8,128)(2,1)S(1)} %get-tuple-element.31.refs_1_, bf16[129,128,128]{2,1,0:T(8,128)(2,1)S(1)} %get-tuple-element.32.refs_2_, bf16[32,64,128]{2,1,0:T(8,128)(2,1)S(1)} %all_to_all.70.refs_3_, ...), custom_call_target="tpu_custom_call" | custom-call | tf_op jit(solution)/shard_map/sweep/pallas_call | solution.py:318
  109.1 15.0 %all_to_all.71.refs_0_ = bf16[32,64,128]{2,1,0:T(8,128)(2,1)S(1)} all-to-all(bf16[32,64,128]{2,1,0:T(8,128)(2,1)S(1)} %sweep.6), channel_id=1, replica_groups=mesh['tiles'=32,'reps'=4] {'tiles'}, dimensions={0} | all-to-all | bytes 1048576 | tf_op jit(solution)/shard_map/all_to_all | solution.py:351
  124.1 0.3 firm.6
  124.4 15.0 %all_to_all.72.refs_3_ = bf16[32,64,128]{2,1,0:T(8,128)(2,1)S(1)} all-to-all(bf16[32,64,128]{2,1,0:T(8,128)(2,1)S(1)} %get-tuple-element.45), channel_id=1, replica_groups=mesh['tiles'=32,'reps'=4] {'tiles'}, dimensions={0} | all-to-all | bytes 1048576 | tf_op jit(solution)/shard_map/all_to_all | solution.py:351
  139.4 3.1 %sweep.7 = bf16[32,64,128]{2,1,0:T(8,128)(2,1)S(1)} custom-call(s32[8,256]{1,0:T(8,128)S(1)} %get-tuple-element.30.refs_0_, bf16[129,128,128]{2,1,0:T(8,128)(2,1)S(1)} %get-tuple-element.31.refs_1_, bf16[129,128,128]{2,1,0:T(8,128)(2,1)S(1)} %get-tuple-element.32.refs_2_, bf16[32,64,128]{2,1,0:T(8,128)(2,1)S(1)} %all_to_all.72.refs_3_, ...), custom_call_target="tpu_custom_call" | custom-call | tf_op jit(solution)/shard_map/sweep/pallas_call | solution.py:318
  142.5 15.0 %all_to_all.73.refs_0_ = bf16[32,64,128]{2,1,0:T(8,128)(2,1)S(1)} all-to-all(bf16[32,64,128]{2,1,0:T(8,128)(2,1)S(1)} %sweep.7), channel_id=1, replica_groups=mesh['tiles'=32,'reps'=4] {'tiles'}, dimensions={0} | all-to-all | bytes 1048576 | tf_op jit(solution)/shard_map/all_to_all | solution.py:351
  157.5 0.3 firm.7
  157.7 15.0 %all_to_all.74.refs_3_ = bf16[32,64,128]{2,1,0:T(8,128)(2,1)S(1)} all-to-all(bf16[32,64,128]{2,1,0:T(8,128)(2,1)S(1)} %firm.7), channel_id=1, replica_groups=mesh['tiles'=32,'reps'=4] {'tiles'}, dimensions={0} | all-to-all | bytes 1048576 | tf_op jit(solution)/shard_map/all_to_all | solution.py:351
  172.8 0.0 copy-start
  172.8 0.0 copy-start.1
  172.8 3.1 %sweep_close.1 = (bf16[32,64,128]{2,1,0:T(8,128)(2,1)S(1)}, f32[64,2048]{1,0:T(8,128)S(1)}) custom-call(s32[8,256]{1,0:T(8,128)S(1)} %get-tuple-element.30.refs_0_, bf16[129,128,128]{2,1,0:T(8,128)(2,1)S(1)} %get-tuple-element.31.refs_1_, bf16[129,128,128]{2,1,0:T(8,128)(2,1)S(1)} %get-tuple-element.32.refs_2_, bf16[32,64,128]{2,1,0:T(8,128)(2,1)S(1)} %all_to_all.74.refs_3_, ...), custom_call_target="tpu_custom_call" | custom-call | tf_op jit(solution)/shard_map/sweep_close/pallas_call | solution.py:318
  175.9 15.0 %all_to_all.75.refs_0_ = bf16[32,64,128]{2,1,0:T(8,128)(2,1)S(1)} all-to-all(bf16[32,64,128]{2,1,0:T(8,128)(2,1)S(1)} %get-tuple-element.47), channel_id=1, replica_groups=mesh['tiles'=32,'reps'=4] {'tiles'}, dimensions={0} | all-to-all | bytes 1048576 | tf_op jit(solution)/shard_map/all_to_all | solution.py:351
  190.9 0.0 copy-done
  190.9 0.0 copy-done.1
  190.9 0.8 close_firm.1
  191.7 11.8 %all_to_all.76.part_ref = f32[32,8,128]{2,1,0:T(8,128)S(1)} all-to-all(f32[32,8,128]{2,1,0:T(8,128)S(1)} %bitcast.13), channel_id=1, replica_groups=mesh['tiles'=32,'reps'=4] {'tiles'}, dimensions={0} | all-to-all | bytes 262144 | tf_op jit(solution)/shard_map/all_to_all | solution.py:351
  203.5 11.2 %all_to_all.77 = f32[32,8,128]{2,1,0:T(8,128)S(1)} all-to-all(f32[32,8,128]{2,1,0:T(8,128)S(1)} %total.1), channel_id=1, replica_groups=mesh['tiles'=32,'reps'=4] {'tiles'}, dimensions={0} | all-to-all | bytes 262144 | tf_op jit(solution)/shard_map/all_to_all | solution.py:351
  214.8 0.3 moment.1
  215.1 4.1 %collective-permute-start.2 = (f32[16,512]{1,0:T(8,128)S(1)}, f32[16,512]{1,0:T(8,128)S(1)}, u32[]{:S(2)}, u32[]{:S(2)}) collective-permute-start(f32[16,512]{1,0:T(8,128)S(1)} %moment.1), channel_id=1, source_target_pairs={{0,3},{1,0},{2,1},{3,2},{4,7},{5,4},{6,5},{7,6},{8,11},{9,8},{10,9... | collective-permute-start | bytes 98312 | tf_op jit(solution)/shard_map/ppermute | solution.py:450
  219.2 0.0 collective-permute-start.1
  219.2 1.9 collective-permute-start
  221.1 1.5 emit.1
  222.5 0.0 collective-permute-done.2
  222.6 2.1 collective-permute-done.1
  224.7 0.0 collective-permute-done
  224.7 0.6 add_multiply_fusion
  (1 shorter events, 0.0 us)
Async XLA Ops:
  0.6 23.0 %copy-start.2 = (s32[64,256]{1,0:T(8,128)S(1)}, s32[64,256]{1,0:T(8,128)}, u32[]{:S(2)}) copy-start(s32[64,256]{1,0:T(8,128)} %signs_ref.1) | copy-start | bytes 196612
  0.6 23.0 %copy-start.5 = (s32[256]{0:T(256)S(1)}, s32[256]{0:T(256)}, u32[]{:S(2)}) copy-start(s32[256]{0:T(256)} %param.22) | copy-start | bytes 3076
  0.7 23.0 %copy-start.4 = (f32[256]{0:T(256)S(1)}, f32[256]{0:T(256)}, u32[]{:S(2)}) copy-start(f32[256]{0:T(256)} %param.21) | copy-start | bytes 3076
  0.7 23.0 %copy-start.3 = (f32[256]{0:T(256)S(1)}, f32[256]{0:T(256)}, u32[]{:S(2)}) copy-start(f32[256]{0:T(256)} %param.20) | copy-start | bytes 3076
  172.8 18.2 %copy-start = (f32[512,512]{1,0:T(8,128)S(1)}, f32[512,512]{1,0:T(8,128)}, u32[]{:S(2)}) copy-start(f32[512,512]{1,0:T(8,128)} %refs_6_.1) | copy-start | bytes 3145732
  172.8 18.2 %copy-start.1 = (f32[256,512]{1,0:T(8,128)S(1)}, f32[256,512]{1,0:T(8,128)}, u32[]{:S(2)}) copy-start(f32[256,512]{1,0:T(8,128)} %refs_5_.1) | copy-start | bytes 1572868
  215.1 7.5 %collective-permute-start.2 = (f32[16,512]{1,0:T(8,128)S(1)}, f32[16,512]{1,0:T(8,128)S(1)}, u32[]{:S(2)}, u32[]{:S(2)}) collective-permute-start(f32[16,512]{1,0:T(8,128)S(1)} %moment.1), channel_id=1, source_target_pairs={{0,3},{1,0},{2,1},{3,2},{4,7},{5,4},{6,5},{7,6},{8,11},{9,8},{10,9... | collective-permute-start | bytes 98312 | tf_op jit(solution)/shard_map/ppermute | solution.py:450
  219.2 5.5 %collective-permute-start.1 = (f32[16,512]{1,0:T(8,128)S(1)}, f32[16,512]{1,0:T(8,128)S(1)}, u32[]{:S(2)}, u32[]{:S(2)}) collective-permute-start(f32[16,512]{1,0:T(8,128)S(1)} %moment.1), channel_id=1, source_target_pairs={{0,1},{1,2},{2,3},{3,0},{4,5},{5,6},{6,7},{7,4},{8,9},{9,10},{10,1... | collective-permute-start | bytes 98312 | tf_op jit(solution)/shard_map/ppermute | solution.py:450
  219.2 5.5 %collective-permute-start = (f32[16,512]{1,0:T(8,128)S(1)}, f32[16,512]{1,0:T(8,128)S(1)}, u32[]{:S(2)}, u32[]{:S(2)}) collective-permute-start(f32[16,512]{1,0:T(8,128)S(1)} %moment.1), channel_id=1, source_target_pairs={{0,2},{1,3},{2,0},{3,1},{4,6},{5,7},{6,4},{7,5},{8,10},{9,11},{10,... | collective-permute-start | bytes 98312 | tf_op jit(solution)/shard_map/ppermute | solution.py:450

commit v12 on v10

--- a/solution.py
+++ b/solution.py
@@ -133,15 +133,14 @@
         turned_ref[t] = turned
         mass_ref[tw[0, t]] += jnp.sum(turned.astype(F32).reshape(CELLS // 8, 8, CELLS), axis=0)
 
+    worker, owner = tw_row[...].astype(F32), to_row[...].astype(F32)
+    pull = pair_plan(worker, owner, plan_ref.shape[1])
+    push = pair_plan(owner, worker, plan_ref.shape[1])
+    for r, values in enumerate(pull + push):
+        plan_ref[r : r + 1] = values
     for c in range(CHUNKS):
         loads[c].wait()
         each_tile(chunk, lambda i, c=c: step(c * chunk + i))
-        if c == 0:
-            worker, owner = tw_row[...].astype(F32), to_row[...].astype(F32)
-            pull = pair_plan(worker, owner, plan_ref.shape[1])
-            push = pair_plan(owner, worker, plan_ref.shape[1])
-            for r, values in enumerate(pull + push):
-                plan_ref[r : r + 1] = values
     for b in range(WORK_BLOCKS):
         inverse = 1.0 / (1.0 + jnp.sum(mass_ref[b], axis=0, keepdims=True))
         inv_ref[b] = jnp.broadcast_to(inverse, (8, CELLS))

time: 226 us -> 226 us (level)
  no operation moved by 1% of the time
where the time goes in v12:
time: 226 us; the launch traced here: 225 us
  blocking collectives  192 us (85%)
  Pallas kernels  23.4 us (10%)
  starting transfers between devices  5.98 us (3%)
    all_to_all x13, blocking collectives, exchange(): return lax.all_to_all(values, axes, 0, 0, tiled=True)  192 us
    pallas_call x15, Pallas kernels, call(): pl.pallas_call(kernel, in_specs=specs or [SMEM] * scalars + [VMEM] * (len...  23.4 us
    ppermute x3, starting transfers between devices, body(): lax.ppermute(moment, 'reps', [(g, (g + d) % groups) for g in range(groups)])  5.98 us
  transfers between devices with their start and end apart: 3, of which 1 were waited for; matrix products, arithmetic and copies ran while one was open for 0% of the time, Pallas kernels for 1%

profile of v12, /device:TPU:0, one launch (start us, length us, event | category | flops | bytes accessed | tf_op | source)
XLA Modules:
  0.0 225.2 jit_solution(9248635073610615761)
XLA Ops:
  0.6 0.0 copy-start.2
  0.6 0.0 copy-start.5
  0.7 0.0 copy-start.4
  0.7 0.0 copy-start.3
  0.7 3.8 %first_push.1 = (bf16[32,72,128]{2,1,0:T(8,128)(2,1)S(1)}, f32[16,64,128]{2,1,0:T(8,128)S(1)}, bf16[129,128,128]{2,1,0:T(8,128)(2,1)S(1)}, bf16[129,128,128]{2,1...) custom-call(s32[1,128]{1,0:T(1,128)} %bitcast.20, s32[1,128]{1,0:T(1,128)} %bitcast.21, ...), custom_call_target="tpu_custom_call" | custom-call | tf_op jit(solution)/shard_map/first_push/pallas_call | solution.py:317
  4.5 19.0 %all_to_all.65.z_ref = bf16[32,72,128]{2,1,0:T(8,128)(2,1)S(1)} all-to-all(bf16[32,72,128]{2,1,0:T(8,128)(2,1)S(1)} %get-tuple-element.34), channel_id=1, replica_groups=mesh['tiles'=32,'reps'=4] {'tiles'}, dimensions={0} | all-to-all | bytes 1179648 | tf_op jit(solution)/shard_map/all_to_all | solution.py:350
  23.5 0.0 copy-done.2
  23.5 0.0 copy-done.5
  23.5 0.0 copy-done.4
  23.5 0.0 copy-done.3
  23.5 0.5 first_firm.1
  23.9 15.0 %all_to_all.66.refs_3_ = bf16[32,64,128]{2,1,0:T(8,128)(2,1)S(1)} all-to-all(bf16[32,64,128]{2,1,0:T(8,128)(2,1)S(1)} %get-tuple-element.35), channel_id=1, replica_groups=mesh['tiles'=32,'reps'=4] {'tiles'}, dimensions={0} | all-to-all | bytes 1048576 | tf_op jit(solution)/shard_map/all_to_all | solution.py:350
  39.0 3.1 %sweep.4 = bf16[32,64,128]{2,1,0:T(8,128)(2,1)S(1)} custom-call(s32[8,256]{1,0:T(8,128)S(1)} %get-tuple-element.30.refs_0_, bf16[129,128,128]{2,1,0:T(8,128)(2,1)S(1)} %get-tuple-element.31.refs_1_, bf16[129,128,128]{2,1,0:T(8,128)(2,1)S(1)} %get-tuple-element.32.refs_2_, bf16[32,64,128]{2,1,0:T(8,128)(2,1)S(1)} %all_to_all.66.refs_3_, ...), custom_call_target="tpu_custom_call" | custom-call | tf_op jit(solution)/shard_map/sweep/pallas_call | solution.py:317
  42.1 15.0 %all_to_all.67.refs_0_ = bf16[32,64,128]{2,1,0:T(8,128)(2,1)S(1)} all-to-all(bf16[32,64,128]{2,1,0:T(8,128)(2,1)S(1)} %sweep.4), channel_id=1, replica_groups=mesh['tiles'=32,'reps'=4] {'tiles'}, dimensions={0} | all-to-all | bytes 1048576 | tf_op jit(solution)/shard_map/all_to_all | solution.py:350
  57.1 0.3 firm.4
  57.4 15.0 %all_to_all.68.refs_3_ = bf16[32,64,128]{2,1,0:T(8,128)(2,1)S(1)} all-to-all(bf16[32,64,128]{2,1,0:T(8,128)(2,1)S(1)} %get-tuple-element.41), channel_id=1, replica_groups=mesh['tiles'=32,'reps'=4] {'tiles'}, dimensions={0} | all-to-all | bytes 1048576 | tf_op jit(solution)/shard_map/all_to_all | solution.py:350
  72.4 3.1 %sweep.5 = bf16[32,64,128]{2,1,0:T(8,128)(2,1)S(1)} custom-call(s32[8,256]{1,0:T(8,128)S(1)} %get-tuple-element.30.refs_0_, bf16[129,128,128]{2,1,0:T(8,128)(2,1)S(1)} %get-tuple-element.31.refs_1_, bf16[129,128,128]{2,1,0:T(8,128)(2,1)S(1)} %get-tuple-element.32.refs_2_, bf16[32,64,128]{2,1,0:T(8,128)(2,1)S(1)} %all_to_all.68.refs_3_, ...), custom_call_target="tpu_custom_call" | custom-call | tf_op jit(solution)/shard_map/sweep/pallas_call | solution.py:317
  75.5 15.0 %all_to_all.69.refs_0_ = bf16[32,64,128]{2,1,0:T(8,128)(2,1)S(1)} all-to-all(bf16[32,64,128]{2,1,0:T(8,128)(2,1)S(1)} %sweep.5), channel_id=1, replica_groups=mesh['tiles'=32,'reps'=4] {'tiles'}, dimensions={0} | all-to-all | bytes 1048576 | tf_op jit(solution)/shard_map/all_to_all | solution.py:350
  90.5 0.3 firm.5
  90.8 15.0 %all_to_all.70.refs_3_ = bf16[32,64,128]{2,1,0:T(8,128)(2,1)S(1)} all-to-all(bf16[32,64,128]{2,1,0:T(8,128)(2,1)S(1)} %get-tuple-element.43), channel_id=1, replica_groups=mesh['tiles'=32,'reps'=4] {'tiles'}, dimensions={0} | all-to-all | bytes 1048576 | tf_op jit(solution)/shard_map/all_to_all | solution.py:350
  105.8 3.1 %sweep.6 = bf16[32,64,128]{2,1,0:T(8,128)(2,1)S(1)} custom-call(s32[8,256]{1,0:T(8,128)S(1)} %get-tuple-element.30.refs_0_, bf16[129,128,128]{2,1,0:T(8,128)(2,1)S(1)} %get-tuple-element.31.refs_1_, bf16[129,128,128]{2,1,0:T(8,128)(2,1)S(1)} %get-tuple-element.32.refs_2_, bf16[32,64,128]{2,1,0:T(8,128)(2,1)S(1)} %all_to_all.70.refs_3_, ...), custom_call_target="tpu_custom_call" | custom-call | tf_op jit(solution)/shard_map/sweep/pallas_call | solution.py:317
  108.9 15.0 %all_to_all.71.refs_0_ = bf16[32,64,128]{2,1,0:T(8,128)(2,1)S(1)} all-to-all(bf16[32,64,128]{2,1,0:T(8,128)(2,1)S(1)} %sweep.6), channel_id=1, replica_groups=mesh['tiles'=32,'reps'=4] {'tiles'}, dimensions={0} | all-to-all | bytes 1048576 | tf_op jit(solution)/shard_map/all_to_all | solution.py:350
  123.9 0.3 firm.6
  124.2 15.0 %all_to_all.72.refs_3_ = bf16[32,64,128]{2,1,0:T(8,128)(2,1)S(1)} all-to-all(bf16[32,64,128]{2,1,0:T(8,128)(2,1)S(1)} %get-tuple-element.45), channel_id=1, replica_groups=mesh['tiles'=32,'reps'=4] {'tiles'}, dimensions={0} | all-to-all | bytes 1048576 | tf_op jit(solution)/shard_map/all_to_all | solution.py:350
  139.2 3.1 %sweep.7 = bf16[32,64,128]{2,1,0:T(8,128)(2,1)S(1)} custom-call(s32[8,256]{1,0:T(8,128)S(1)} %get-tuple-element.30.refs_0_, bf16[129,128,128]{2,1,0:T(8,128)(2,1)S(1)} %get-tuple-element.31.refs_1_, bf16[129,128,128]{2,1,0:T(8,128)(2,1)S(1)} %get-tuple-element.32.refs_2_, bf16[32,64,128]{2,1,0:T(8,128)(2,1)S(1)} %all_to_all.72.refs_3_, ...), custom_call_target="tpu_custom_call" | custom-call | tf_op jit(solution)/shard_map/sweep/pallas_call | solution.py:317
  142.3 15.0 %all_to_all.73.refs_0_ = bf16[32,64,128]{2,1,0:T(8,128)(2,1)S(1)} all-to-all(bf16[32,64,128]{2,1,0:T(8,128)(2,1)S(1)} %sweep.7), channel_id=1, replica_groups=mesh['tiles'=32,'reps'=4] {'tiles'}, dimensions={0} | all-to-all | bytes 1048576 | tf_op jit(solution)/shard_map/all_to_all | solution.py:350
  157.4 0.3 firm.7
  157.6 15.0 %all_to_all.74.refs_3_ = bf16[32,64,128]{2,1,0:T(8,128)(2,1)S(1)} all-to-all(bf16[32,64,128]{2,1,0:T(8,128)(2,1)S(1)} %firm.7), channel_id=1, replica_groups=mesh['tiles'=32,'reps'=4] {'tiles'}, dimensions={0} | all-to-all | bytes 1048576 | tf_op jit(solution)/shard_map/all_to_all | solution.py:350
  172.6 0.0 copy-start
  172.6 0.0 copy-start.1
  172.6 3.1 %sweep_close.1 = (bf16[32,64,128]{2,1,0:T(8,128)(2,1)S(1)}, f32[64,2048]{1,0:T(8,128)S(1)}) custom-call(s32[8,256]{1,0:T(8,128)S(1)} %get-tuple-element.30.refs_0_, bf16[129,128,128]{2,1,0:T(8,128)(2,1)S(1)} %get-tuple-element.31.refs_1_, bf16[129,128,128]{2,1,0:T(8,128)(2,1)S(1)} %get-tuple-element.32.refs_2_, bf16[32,64,128]{2,1,0:T(8,128)(2,1)S(1)} %all_to_all.74.refs_3_, ...), custom_call_target="tpu_custom_call" | custom-call | tf_op jit(solution)/shard_map/sweep_close/pallas_call | solution.py:317
  175.8 15.0 %all_to_all.75.refs_0_ = bf16[32,64,128]{2,1,0:T(8,128)(2,1)S(1)} all-to-all(bf16[32,64,128]{2,1,0:T(8,128)(2,1)S(1)} %get-tuple-element.47), channel_id=1, replica_groups=mesh['tiles'=32,'reps'=4] {'tiles'}, dimensions={0} | all-to-all | bytes 1048576 | tf_op jit(solution)/shard_map/all_to_all | solution.py:350
  190.8 0.0 copy-done
  190.8 0.0 copy-done.1
  190.8 0.8 close_firm.1
  191.6 11.8 %all_to_all.76.part_ref = f32[32,8,128]{2,1,0:T(8,128)S(1)} all-to-all(f32[32,8,128]{2,1,0:T(8,128)S(1)} %bitcast.13), channel_id=1, replica_groups=mesh['tiles'=32,'reps'=4] {'tiles'}, dimensions={0} | all-to-all | bytes 262144 | tf_op jit(solution)/shard_map/all_to_all | solution.py:350
  203.4 11.2 %all_to_all.77 = f32[32,8,128]{2,1,0:T(8,128)S(1)} all-to-all(f32[32,8,128]{2,1,0:T(8,128)S(1)} %total.1), channel_id=1, replica_groups=mesh['tiles'=32,'reps'=4] {'tiles'}, dimensions={0} | all-to-all | bytes 262144 | tf_op jit(solution)/shard_map/all_to_all | solution.py:350
  214.6 0.3 moment.1
  215.0 4.1 %collective-permute-start.2 = (f32[16,512]{1,0:T(8,128)S(1)}, f32[16,512]{1,0:T(8,128)S(1)}, u32[]{:S(2)}, u32[]{:S(2)}) collective-permute-start(f32[16,512]{1,0:T(8,128)S(1)} %moment.1), channel_id=1, source_target_pairs={{0,3},{1,0},{2,1},{3,2},{4,7},{5,4},{6,5},{7,6},{8,11},{9,8},{10,9... | collective-permute-start | bytes 98312 | tf_op jit(solution)/shard_map/ppermute | solution.py:449
  219.1 0.0 collective-permute-start.1
  219.1 1.9 collective-permute-start
  220.9 1.5 emit.1
  222.4 0.0 collective-permute-done.2
  222.4 2.1 collective-permute-done.1
  224.5 0.0 collective-permute-done
  224.5 0.6 add_multiply_fusion
  (1 shorter events, 0.0 us)
Async XLA Ops:
  0.6 22.8 %copy-start.2 = (s32[64,256]{1,0:T(8,128)S(1)}, s32[64,256]{1,0:T(8,128)}, u32[]{:S(2)}) copy-start(s32[64,256]{1,0:T(8,128)} %signs_ref.1) | copy-start | bytes 196612
  0.6 22.8 %copy-start.5 = (s32[256]{0:T(256)S(1)}, s32[256]{0:T(256)}, u32[]{:S(2)}) copy-start(s32[256]{0:T(256)} %param.22) | copy-start | bytes 3076
  0.7 22.8 %copy-start.4 = (f32[256]{0:T(256)S(1)}, f32[256]{0:T(256)}, u32[]{:S(2)}) copy-start(f32[256]{0:T(256)} %param.21) | copy-start | bytes 3076
  0.7 22.8 %copy-start.3 = (f32[256]{0:T(256)S(1)}, f32[256]{0:T(256)}, u32[]{:S(2)}) copy-start(f32[256]{0:T(256)} %param.20) | copy-start | bytes 3076
  172.6 18.2 %copy-start = (f32[512,512]{1,0:T(8,128)S(1)}, f32[512,512]{1,0:T(8,128)}, u32[]{:S(2)}) copy-start(f32[512,512]{1,0:T(8,128)} %refs_6_.1) | copy-start | bytes 3145732
  172.6 18.2 %copy-start.1 = (f32[256,512]{1,0:T(8,128)S(1)}, f32[256,512]{1,0:T(8,128)}, u32[]{:S(2)}) copy-start(f32[256,512]{1,0:T(8,128)} %refs_5_.1) | copy-start | bytes 1572868
  215.0 7.5 %collective-permute-start.2 = (f32[16,512]{1,0:T(8,128)S(1)}, f32[16,512]{1,0:T(8,128)S(1)}, u32[]{:S(2)}, u32[]{:S(2)}) collective-permute-start(f32[16,512]{1,0:T(8,128)S(1)} %moment.1), channel_id=1, source_target_pairs={{0,3},{1,0},{2,1},{3,2},{4,7},{5,4},{6,5},{7,6},{8,11},{9,8},{10,9... | collective-permute-start | bytes 98312 | tf_op jit(solution)/shard_map/ppermute | solution.py:449
  219.1 5.5 %collective-permute-start.1 = (f32[16,512]{1,0:T(8,128)S(1)}, f32[16,512]{1,0:T(8,128)S(1)}, u32[]{:S(2)}, u32[]{:S(2)}) collective-permute-start(f32[16,512]{1,0:T(8,128)S(1)} %moment.1), channel_id=1, source_target_pairs={{0,1},{1,2},{2,3},{3,0},{4,5},{5,6},{6,7},{7,4},{8,9},{9,10},{10,1... | collective-permute-start | bytes 98312 | tf_op jit(solution)/shard_map/ppermute | solution.py:449
  219.1 5.5 %collective-permute-start = (f32[16,512]{1,0:T(8,128)S(1)}, f32[16,512]{1,0:T(8,128)S(1)}, u32[]{:S(2)}, u32[]{:S(2)}) collective-permute-start(f32[16,512]{1,0:T(8,128)S(1)} %moment.1), channel_id=1, source_target_pairs={{0,2},{1,3},{2,0},{3,1},{4,6},{5,7},{6,4},{7,5},{8,10},{9,11},{10,... | collective-permute-start | bytes 98312 | tf_op jit(solution)/shard_map/ppermute | solution.py:449
